TPU v7x, 16 devices: a 4x2x1 block of a 4x4x8 slice. The times are simulated.
16 devices in a mesh: dp: 2 (over y, z), sp: 8 (over x, core).
Axes of the slice: x: 4, y: 2, z: 1, core: 2. Of those that a mesh axis runs over, the one named last changes fastest.
The devices are a block of a 4x4x8 slice.
Arguments:
- hidden: bfloat16 [16, 1024, 2048], P('dp', 'sp'), parts along dimension 0
- norm_w: bfloat16 [2048], replicated
- w_qkv: bfloat16 [2048, 3072], replicated
- w_out: bfloat16 [32, 64, 2048], replicated
- long_factor: float32 [32], replicated
- grad_out: bfloat16 [16, 1024, 2048], P('dp', 'sp'), parts along dimension 0
Outputs:
- output 1: bfloat16 [16, 1024, 2048], P('dp', 'sp'), parts along dimension 0
- output 2: bfloat16 [16, 1024, 2048], P('dp', 'sp'), parts along dimension 0
- output 3: float32 [4096, 3072], P('dp'), parts along dimension 0
- output 4: float32 [64, 64, 2048], P('dp'), parts along dimension 0
- output 5: float32 [4096], P('dp'), parts along dimension 0
There are 2 independent parts. A program takes and returns all parts, laid end to end along the dimension named above; an argument that names none is the same for every part.
All inputs are finite; a program needn't handle non-finite values.
Results may differ from a plain program's by a relative error of at most 0.0104791.
Values are sent between devices in bfloat16 or wider.
A program may use at most 768 MiB of HBM per device.

v0:
```python
import math
import functools
import jax
import jax.numpy as jnp
from jax import lax
from jax.sharding import PartitionSpec as P, NamedSharding

NORM_EPS = 1e-5
ROPE_BASE = 10000.0
ROPE_GAIN = math.sqrt(1.0 + math.log(32.0) / math.log(4096.0))
MASK_VALUE = -1e30


def rope_tables(positions, long_factor):
    half_rot = long_factor.shape[0]
    exponent = jnp.arange(half_rot, dtype=jnp.float32) / half_rot
    inv_freq = 1.0 / (long_factor * jnp.power(ROPE_BASE, exponent))
    angles = positions.astype(jnp.float32)[:, None] * inv_freq[None, :]
    return jnp.cos(angles) * ROPE_GAIN, jnp.sin(angles) * ROPE_GAIN


def rotate(head_vals, cos_t, sin_t, direction):
    half_rot = cos_t.shape[1]
    cos_b = cos_t[None, :, None, :]
    sin_b = sin_t[None, :, None, :] * direction
    first_half = head_vals[..., :half_rot]
    second_half = head_vals[..., half_rot:2 * half_rot]
    rest_dims = head_vals[..., 2 * half_rot:].astype(jnp.float32)
    return jnp.concatenate([first_half * cos_b - second_half * sin_b, second_half * cos_b + first_half * sin_b, rest_dims], axis=-1)


def norm_forward(hidden, norm_w):
    hidden_f = hidden.astype(jnp.float32)
    inv_rms = lax.rsqrt(jnp.mean(hidden_f * hidden_f, axis=-1, keepdims=True) + NORM_EPS)
    unit_rows = hidden_f * inv_rms
    return (unit_rows * norm_w.astype(jnp.float32)).astype(jnp.bfloat16), unit_rows, inv_rms


def norm_backward(grad_normed, unit_rows, inv_rms, norm_w):
    grad_unit = grad_normed * norm_w.astype(jnp.float32)
    mean_dot = jnp.mean(grad_unit * unit_rows, axis=-1, keepdims=True)
    return inv_rms * (grad_unit - unit_rows * mean_dot)


def split_fused(fused_qkv, n_heads, kv_heads, head_dim, cos_t, sin_t):
    n_batch, tok_len = fused_qkv.shape[0], fused_qkv.shape[1]
    q_width = n_heads * head_dim
    kv_width = kv_heads * head_dim
    queries = fused_qkv[..., :q_width].reshape(n_batch, tok_len, n_heads, head_dim)
    key_vals = fused_qkv[..., q_width:q_width + kv_width].reshape(n_batch, tok_len, kv_heads, head_dim)
    value_vals = fused_qkv[..., q_width + kv_width:].reshape(n_batch, tok_len, kv_heads, head_dim)
    return (rotate(queries, cos_t, sin_t, 1.0).astype(jnp.bfloat16), rotate(key_vals, cos_t, sin_t, 1.0).astype(jnp.bfloat16), value_vals.astype(jnp.bfloat16))


def merge_grads(grad_q, grad_k, grad_v, cos_t, sin_t):
    n_batch, tok_len = grad_q.shape[0], grad_q.shape[1]
    return jnp.concatenate([
        rotate(grad_q, cos_t, sin_t, -1.0).reshape(n_batch, tok_len, -1),
        rotate(grad_k, cos_t, sin_t, -1.0).reshape(n_batch, tok_len, -1),
        grad_v.astype(jnp.float32).reshape(n_batch, tok_len, -1)], axis=-1).astype(jnp.bfloat16)


def causal_probs(queries, key_vals):
    seq_len, head_dim = queries.shape[1], queries.shape[-1]
    scores = jnp.einsum('bqkge,bske->bkgqs', queries, key_vals, preferred_element_type=jnp.float32) * (head_dim ** -0.5)
    causal = jnp.arange(seq_len)[:, None] >= jnp.arange(seq_len)[None, :]
    return jax.nn.softmax(jnp.where(causal, scores, MASK_VALUE), axis=-1)


def attention_forward(queries, key_vals, value_vals):
    prob_mat = causal_probs(queries, key_vals)
    return jnp.einsum('bkgqs,bske->bqkge', prob_mat.astype(jnp.bfloat16), value_vals, preferred_element_type=jnp.float32).astype(jnp.bfloat16)


def attention_backward(queries, key_vals, value_vals, grad_attn):
    head_dim = queries.shape[-1]
    prob_mat = causal_probs(queries, key_vals)
    grad_v = jnp.einsum('bkgqs,bqkge->bske', prob_mat.astype(jnp.bfloat16), grad_attn, preferred_element_type=jnp.float32)
    grad_p = jnp.einsum('bqkge,bske->bkgqs', grad_attn, value_vals, preferred_element_type=jnp.float32)
    row_dot = jnp.sum(grad_p * prob_mat, axis=-1, keepdims=True)
    grad_s = (prob_mat * (grad_p - row_dot) * (head_dim ** -0.5)).astype(jnp.bfloat16)
    grad_q = jnp.einsum('bkgqs,bske->bqkge', grad_s, key_vals, preferred_element_type=jnp.float32)
    grad_k = jnp.einsum('bkgqs,bqkge->bske', grad_s, queries, preferred_element_type=jnp.float32)
    return grad_q.astype(jnp.bfloat16), grad_k.astype(jnp.bfloat16), grad_v.astype(jnp.bfloat16)


def solution(mesh):
    group_devs = mesh.shape['sp']
    to_heads = functools.partial(lax.all_to_all, axis_name='sp', split_axis=2, concat_axis=1, tiled=True)
    to_tokens = functools.partial(lax.all_to_all, axis_name='sp', split_axis=1, concat_axis=2, tiled=True)

    def device_step(hidden, norm_w, w_qkv, w_out, long_factor, grad_out):
        n_batch, tok_len = hidden.shape[0], hidden.shape[1]
        n_heads, head_dim = w_out.shape[0], w_out.shape[1]
        kv_heads = (w_qkv.shape[1] // head_dim - n_heads) // 2
        seq_len = tok_len * group_devs
        heads_local = n_heads // group_devs
        kv_local = kv_heads // group_devs
        head_shape = (n_batch, seq_len, kv_local, n_heads // kv_heads, head_dim)
        positions = lax.axis_index('sp') * tok_len + jnp.arange(tok_len)
        cos_t, sin_t = rope_tables(positions, long_factor)
        normed, unit_rows, inv_rms = norm_forward(hidden, norm_w)
        fused_qkv = jnp.einsum('btd,dw->btw', normed, w_qkv, preferred_element_type=jnp.float32)
        q_local, k_local, v_local = split_fused(fused_qkv, n_heads, kv_heads, head_dim, cos_t, sin_t)
        q_heads = to_heads(q_local).reshape(head_shape)
        k_heads = to_heads(k_local)
        v_heads = to_heads(v_local)
        attn_heads = attention_forward(q_heads, k_heads, v_heads)
        attn_local = to_tokens(attn_heads.reshape(n_batch, seq_len, heads_local, head_dim))
        projected = jnp.einsum('bthe,hed->btd', attn_local, w_out, preferred_element_type=jnp.float32)
        block_out = (hidden.astype(jnp.float32) + projected).astype(jnp.bfloat16)

        grad_w_out = jnp.einsum('bthe,btd->hed', attn_local, grad_out, preferred_element_type=jnp.float32)
        grad_attn = jnp.einsum('btd,hed->bthe', grad_out, w_out, preferred_element_type=jnp.float32).astype(jnp.bfloat16)
        grad_attn_heads = to_heads(grad_attn).reshape(head_shape)
        grad_q, grad_k, grad_v = attention_backward(q_heads, k_heads, v_heads, grad_attn_heads)
        grad_q_local = to_tokens(grad_q.reshape(n_batch, seq_len, heads_local, head_dim))
        grad_fused = merge_grads(grad_q_local, to_tokens(grad_k), to_tokens(grad_v), cos_t, sin_t)
        grad_w_qkv = jnp.einsum('btd,btw->dw', normed, grad_fused, preferred_element_type=jnp.float32)
        grad_normed = jnp.einsum('btw,dw->btd', grad_fused, w_qkv, preferred_element_type=jnp.float32)
        grad_hidden = (grad_out.astype(jnp.float32) + norm_backward(grad_normed, unit_rows, inv_rms, norm_w)).astype(jnp.bfloat16)
        grad_norm_w = jnp.sum(grad_normed * unit_rows, axis=(0, 1))
        return (block_out, grad_hidden, lax.psum(grad_w_qkv, 'sp'), lax.psum(grad_w_out, 'sp'), lax.psum(grad_norm_w, 'sp'))

    tok_spec = P('dp', 'sp', None)
    return jax.shard_map(device_step, mesh=mesh,
                         in_specs=(tok_spec, P(), P(), P(), P(), tok_spec),
                         out_specs=(tok_spec, tok_spec, P('dp', None), P('dp', None, None), P('dp')),
                         check_vma=False)
```

profile of v0, /device:TPU:112, one launch (start us, length us, event | category | flops | bytes accessed | tf_op | source)
XLA Modules:
  0.0 1297.4 jit_solution(17674945855273749610)
XLA Ops:
  11.6 17.2 %fusion.15 = f32[8,128,3072]{2,1,0:T(8,128)S(1)} fusion(bf16[2048,3072]{1,0:T(8,128)(2,1)} %param.8, bf16[8,128,2048]{2,1,0:T(8,128)(2,1)} %param.6, f32[2048]{0:T(1024)S(1)} %convert_element_type.108, f32[8,128]{1,0:T(8,128)S(1)} %add_rsqrt_fusion), kind=kOutput, calls=%fused_computation.20 | convolution fusion | flops 12893290496 | bytes 29372416 | tf_op jit(solution)/shard_map/btd,dw->btw/dot_general | solution.py:103
  48.1 12.5 all-to-all-done.1
  95.7 12.5 fusion.44
  111.1 34.1 %all-to-all-done.2 = bf16[8,128,32,64]{1,3,0,2:T(8,128)(2,1)} async-done(((bf16[8,128,32,64]{1,3,0,2:T(8,128)(2,1)}), bf16[8,128,32,64]{1,3,0,2:T(8,128)(2,1)}, u32[]{:S(2)}, u32[]{:S(2)}) %all-to-all-start.2) | async-done | bytes 4194336 | tf_op jit(solution)/shard_map/all_to_all | solution.py:105
  156.7 12.7 copy.116
  176.9 22.5 %all-to-all-done.4 = bf16[8,128,32,64]{1,3,0,2:T(8,128)(2,1)} async-done(((bf16[8,128,32,64]{1,3,0,2:T(8,128)(2,1)}), bf16[8,128,32,64]{1,3,0,2:T(8,128)(2,1)}, u32[]{:S(2)}, u32[]{:S(2)}) %all-to-all-start.4) | async-done | bytes 4194336 | tf_op jit(solution)/shard_map/all_to_all | solution.py:115
  199.4 12.3 copy.115
  219.0 46.3 %fusion.6 = (f32[8,4,1024]{2,1,0:T(4,128)S(1)}, f32[8,1024,1024,4]{2,1,3,0:T(8,128)}) fusion(pred[1024,1024]{0,1:T(8,128)(4,1)S(1)} %iota_compare_fusion, bf16[8,1024,4,64]{1,3,2,0:T(8,128)(2,1)} %reshape.201, bf16[8,1024,64,1]{1,2,0,3:T(8,128)(2,1)S(1)} %reshape.210), kind=kOutput, calls=%fused_computation.10 | convolution fusion | flops 4395597824 | bytes 140640256 | tf_op jit(solution)/shard_map/bqkge,bske->bkgqs/dot_general | solution.py:65
  265.3 41.6 %fusion.5 = f32[8,4,1024]{2,1,0:T(4,128)S(1)} fusion(f32[8,1024,1024,4]{2,1,3,0:T(8,128)} %get-tuple-element.21, f32[8,4,1024]{2,1,0:T(4,128)S(1)} %get-tuple-element.20, pred[1024,1024]{0,1:T(8,128)(4,1)S(1)} %iota_compare_fusion), kind=kLoop, calls=%fused_computation.9 | loop fusion | flops 134184960 | bytes 135528448 | tf_op jit(solution)/shard_map/reduce_sum | solution.py:67
  306.9 99.7 %fusion = (f32[8,4,1024]{2,1,0:T(4,128)S(1)}, f32[8,1024,1024,4]{2,1,3,0:T(8,128)}) fusion(f32[8,4,1024]{2,1,0:T(4,128)S(1)} %fusion.5, f32[8,4,1024]{2,1,0:T(4,128)S(1)} %get-tuple-element.20, f32[8,1024,1024,4]{2,1,3,0:T(8,128)} %get-tuple-element.21, pred[1024,1024]{0,1:T(8,128)(4,1)S(1)} %iota_compare_fusion, bf16[8,1024,4,64]{1,3,2,0:T(8,128)(2,1)} %reshape.204, ...), kind=kOutput, calls=%fused_computation.3 | convolution fusion | flops 4496261120 | bytes 275120128 | tf_op jit(solution)/shard_map/bqkge,bske->bkgqs/dot_general | solution.py:79
  406.7 104.4 %fusion.7 = bf16[8,4,1024,1024]{2,3,1,0:T(8,128)(2,1)} fusion(f32[8,1024,1024,4]{2,1,3,0:T(8,128)} %get-tuple-element.23, f32[8,4,1024]{2,1,0:T(4,128)S(1)} %get-tuple-element.22, f32[8,4,1024]{2,1,0:T(4,128)S(1)} %fusion.5, f32[8,4,1024]{2,1,0:T(4,128)S(1)} %get-tuple-element.20, f32[8,1024,1024,4]{2,1,3,0:T(8,128)} %get-tuple-element.21, ...), kind=kLoop, calls=%fused_computation.11 | loop fusion | flops 268435456 | bytes 336986112 | tf_op jit(solution)/shard_map/reshape.30
  511.1 30.6 %fusion.53 = bf16[8,1024,1,64]{1,3,0,2:T(8,128)(2,1)} fusion(bf16[8,1024,4,64]{1,3,2,0:T(8,128)(2,1)} %reshape.201, bf16[8,4,1024,1024]{2,3,1,0:T(8,128)(2,1)} %fusion.7), kind=kOutput, calls=%fused_computation.67 | convolution fusion | flops 4295491584 | bytes 72351744 | tf_op jit(solution)/shard_map/bkgqs,bqkge->bske/dot_general | solution.py:83
  551.5 49.2 %fusion.54 = bf16[8,1024,1,64]{1,3,0,2:T(8,128)(2,1)} fusion(bf16[8,1024,4,64]{1,3,2,0:T(8,128)(2,1)} %reshape.204, f32[8,4,1024]{2,1,0:T(4,128)S(1)} %fusion.5, f32[8,4,1024]{2,1,0:T(4,128)S(1)} %get-tuple-element.20, f32[8,1024,1024,4]{2,1,3,0:T(8,128)} %get-tuple-element.21, pred[1024,1024]{0,1:T(8,128)(4,1)S(1)} %iota_compare_fusion), kind=kOutput, calls=%fused_computation.68 | convolution fusion | flops 4463263744 | bytes 140771328 | tf_op jit(solution)/shard_map/bkgqs,bqkge->bske/dot_general | solution.py:78
  610.8 25.8 %convert_bitcast_fusion = bf16[8,1024,4,64]{1,3,2,0:T(8,128)(2,1)} fusion(bf16[8,4,1024,1024]{2,3,1,0:T(8,128)(2,1)} %fusion.7, bf16[8,1024,64,1]{1,2,0,3:T(8,128)(2,1)} %copy-done.4), kind=kOutput, calls=%fused_computation.58 | convolution fusion | flops 4297064448 | bytes 72351744 | tf_op jit(solution)/shard_map/bkgqs,bske->bqkge/dot_general | solution.py:82
  636.6 13.6 %copy.85 = bf16[8,1024,4,64]{3,2,0,1:T(4,128)(2,1)} copy(bf16[8,1024,4,64]{1,3,2,0:T(8,128)(2,1)} %convert_bitcast_fusion) | data formatting | bytes 8388608 | tf_op jit(solution)/shard_map/reshape | solution.py:117
  666.0 49.7 %convert_bitcast_fusion.1 = bf16[8,1024,4,64]{1,3,2,0:T(8,128)(2,1)} fusion(bf16[8,1024,64,1]{1,2,0,3:T(8,128)(2,1)S(1)} %copy-done.10, f32[8,4,1024]{2,1,0:T(4,128)S(1)} %fusion.5, f32[8,4,1024]{2,1,0:T(4,128)S(1)} %get-tuple-element.20, f32[8,1024,1024,4]{2,1,3,0:T(8,128)} %get-tuple-element.21, pred[1024,1024]{0,1:T(8,128)(4,1)S(1)} %iota_compare_fusion), kind=kOutput, calls=%fused_computation.59 | convolution fusion | flops 4464836608 | bytes 140771328 | tf_op jit(solution)/shard_map/bkgqs,bske->bqkge/dot_general | solution.py:72
  715.6 13.6 %copy.80 = bf16[8,1024,4,64]{3,2,0,1:T(4,128)(2,1)} copy(bf16[8,1024,4,64]{1,3,2,0:T(8,128)(2,1)} %convert_bitcast_fusion.1) | data formatting | bytes 8388608 | tf_op jit(solution)/shard_map/reshape | solution.py:109
  817.0 14.1 %convolution_bitcast_fusion.1 = f32[32,64,2048]{2,1,0:T(8,128)} fusion(bf16[8,128,32,64]{1,3,2,0:T(8,128)(2,1)} %bitcast.206, bf16[8,128,2048]{2,1,0:T(8,128)(2,1)} %param.11), kind=kOutput, calls=%fused_computation.42 | convolution fusion | flops 8589934592 | bytes 25165824 | tf_op jit(solution)/shard_map/bthe,btd->hed/dot_general | solution.py:113
  831.1 18.3 %convolution_bitcast_fusion = f32[2048,3072]{1,0:T(8,128)} fusion(bf16[8,128,2048]{2,1,0:T(8,128)(2,1)S(1)} %copy-done.1, f32[2048]{0:T(1024)S(1)} %copy-done.16, f32[8,128]{1,0:T(8,128)S(1)} %copy-done.18, bf16[8,128,512]{2,1,0:T(8,128)(2,1)S(1)} %copy.97, bf16[8,128,512]{2,1,0:T(8,128)(2,1)S(1)} %copy-done.11, bf16[8,128,2048]{2,1,0:T(8,128)(2,1)S(1)} %copy-done.8), kind=kOutput, calls=%fused_computation.17 | convolution fusion | flops 12912164864 | bytes 35663872 | tf_op jit(solution)/shard_map/btd,btw->dw/dot_general | solution.py:119
  849.5 20.6 %fusion.27 = (f32[2048]{0:T(1024)S(1)}, f32[8,128]{1,0:T(8,128)S(1)}, f32[8,128,2048]{2,1,0:T(8,128)}) fusion(bf16[8,128,2048]{2,1,0:T(8,128)(2,1)} %param.6, f32[8,128]{1,0:T(8,128)S(1)} %copy-done.18, f32[2048]{0:T(1024)S(1)} %copy-done.16, bf16[2048,3072]{1,0:T(8,128)(2,1)} %param.8, bf16[8,128,512]{2,1,0:T(8,128)(2,1)S(1)} %copy.97, ...), kind=kOutput, calls=%fused_computation.35 | convolution fusion | flops 12918453248 | bytes 31481856 | tf_op jit(solution)/shard_map/btw,dw->btd/dot_general | solution.py:120
  870.1 16.0 %psum.23 = f32[2048]{0:T(1024)} all-reduce(f32[2048]{0:T(1024)S(1)} %get-tuple-element.5), channel_id=1, replica_groups=mesh['dp'=2,'sp'=8] {'sp'}, use_global_device_ids=true, to_apply=%region_8.9 | all-reduce | flops 2048 | bytes 16384 | tf_op jit(solution)/shard_map/psum | solution.py:123
  896.0 12.8 fusion.29
  908.8 353.6 %all-reduce.3.cloned.1.call-done = (f32[2048,3072]{1,0:T(8,128)}, f32[32,64,2048]{2,1,0:T(8,128)}) async-done(((f32[2048,3072]{1,0:T(8,128)}, f32[32,64,2048]{2,1,0:T(8,128)}), (f32[2048,3072]{1,0:T(8,128)}, f32[32,64,2048]{2,1,0:T(8,128)})) %all-reduce.3.cloned.1.call-update) | async-done | bytes 41943056 | tf_op jit(solution)/shard_map/psum | solution.py:123
  1262.5 18.8 %copy.119 = f32[2048,3072]{1,0:T(8,128)} copy(f32[2048,3072]{1,0:T(8,128)} %get-tuple-element.27) | data formatting | bytes 50331648
  (105 shorter events, 230.2 us)
Async XLA Ops:
  10.3 18.5 %copy-start.17 = (f32[8,128]{1,0:T(8,128)}, f32[8,128]{1,0:T(8,128)S(1)}, u32[]{:S(2)}) copy-start(f32[8,128]{1,0:T(8,128)S(1)} %add_rsqrt_fusion) | copy-start | bytes 12292
  11.0 17.8 %copy-start.15 = (f32[2048]{0:T(1024)}, f32[2048]{0:T(1024)S(1)}, u32[]{:S(2)}) copy-start(f32[2048]{0:T(1024)S(1)} %convert_element_type.108) | copy-start | bytes 24580
  37.8 43.5 %copy-start.12 = (f32[128,32]{0,1:T(8,128)}, f32[128,32]{0,1:T(8,128)S(1)}, u32[]{:S(2)}) copy-start(f32[128,32]{0,1:T(8,128)S(1)} %get-tuple-element.19) | copy-start | bytes 49156
  39.3 21.3 %all-to-all-start.1 = ((bf16[8,128,8,64]{1,3,0,2:T(8,128)(2,1)}), bf16[8,128,8,64]{1,3,0,2:T(8,128)(2,1)S(1)}, u32[]{:S(2)}, u32[]{:S(2)}) async-start(bf16[8,128,8,64]{1,3,0,2:T(8,128)(2,1)} %copy.74), calls=%async_computation.1 | async-start | bytes 2097152 | tf_op jit(solution)/shard_map/all_to_all | solution.py:106
  60.6 30.2 %all-to-all-start = ((bf16[8,128,8,64]{1,3,0,2:T(8,128)(2,1)}), bf16[8,128,8,64]{1,3,0,2:T(8,128)(2,1)S(1)}, u32[]{:S(2)}, u32[]{:S(2)}) async-start(bf16[8,128,8,64]{1,3,0,2:T(8,128)(2,1)} %copy.71), calls=%async_computation | async-start | bytes 2097152 | tf_op jit(solution)/shard_map/all_to_all | solution.py:107
  90.8 54.4 %all-to-all-start.2 = ((bf16[8,128,32,64]{1,3,0,2:T(8,128)(2,1)}), bf16[8,128,32,64]{1,3,0,2:T(8,128)(2,1)}, u32[]{:S(2)}, u32[]{:S(2)}) async-start(bf16[8,128,32,64]{1,3,0,2:T(8,128)(2,1)} %copy.77), calls=%async_computation.2 | async-start | bytes 8388608 | tf_op jit(solution)/shard_map/all_to_all | solution.py:105
  145.2 54.2 %all-to-all-start.4 = ((bf16[8,128,32,64]{1,3,0,2:T(8,128)(2,1)}), bf16[8,128,32,64]{1,3,0,2:T(8,128)(2,1)}, u32[]{:S(2)}, u32[]{:S(2)}) async-start(bf16[8,128,32,64]{1,3,0,2:T(8,128)(2,1)} %copy.82), calls=%async_computation.4 | async-start | bytes 8388608 | tf_op jit(solution)/shard_map/all_to_all | solution.py:115
  153.5 65.5 %copy-start.4 = (bf16[8,1024,64,1]{1,2,0,3:T(8,128)(2,1)}, bf16[8,1024,64,1]{1,2,0,3:T(8,128)(2,1)S(1)}, u32[]{:S(2)}) copy-start(bf16[8,1024,64,1]{1,2,0,3:T(8,128)(2,1)S(1)} %reshape.210) | copy-start | bytes 3145732
  156.7 150.2 %copy-start.9 = (bf16[8,1024,64,1]{1,2,0,3:T(8,128)(2,1)}, bf16[8,1024,64,1]{1,2,0,3:T(8,128)(2,1)S(1)}, u32[]{:S(2)}) copy-start(bf16[8,1024,64,1]{1,2,0,3:T(8,128)(2,1)S(1)} %reshape.211) | copy-start | bytes 3145732
  546.9 59.1 %all-to-all-start.6 = ((bf16[8,2,32768]{2,1,0:T(2,128)(2,1)}), bf16[8,2,32768]{2,1,0:T(2,128)(2,1)}, u32[]{:S(2)}, u32[]{:S(2)}) async-start(bf16[8,2,32768]{2,1,0:T(2,128)(2,1)} %reshape.225), calls=%async_computation.6 | async-start | bytes 2097152 | tf_op jit(solution)/shard_map/all_to_all | solution.py:118
  606.1 54.7 %all-to-all-start.7 = ((bf16[8,2,32768]{2,1,0:T(2,128)(2,1)}), bf16[8,2,32768]{2,1,0:T(2,128)(2,1)S(1)}, u32[]{:S(2)}, u32[]{:S(2)}) async-start(bf16[8,2,32768]{2,1,0:T(2,128)(2,1)} %reshape.223), calls=%async_computation.7 | async-start | bytes 2097152 | tf_op jit(solution)/shard_map/all_to_all | solution.py:118
  650.2 15.8 %copy-start.10 = (bf16[8,1024,64,1]{1,2,0,3:T(8,128)(2,1)S(1)}, bf16[8,1024,64,1]{1,2,0,3:T(8,128)(2,1)}, u32[]{:S(2)}) copy-start(bf16[8,1024,64,1]{1,2,0,3:T(8,128)(2,1)} %copy-done.9) | copy-start | bytes 3145732
  660.8 54.9 %copy-start.6 = (bf16[8,2,32768]{2,1,0:T(2,128)(2,1)}, bf16[8,2,32768]{2,1,0:T(2,128)(2,1)S(1)}, u32[]{:S(2)}) copy-start(bf16[8,2,32768]{2,1,0:T(2,128)(2,1)S(1)} %all-to-all-done.7) | copy-start | bytes 3145732
  660.8 79.0 %all-to-all-start.5 = ((bf16[8,2,131072]{2,1,0:T(2,128)(2,1)}), bf16[8,2,131072]{2,1,0:T(2,128)(2,1)}, u32[]{:S(2)}, u32[]{:S(2)}) async-start(bf16[8,2,131072]{2,1,0:T(2,128)(2,1)} %reshape.227), calls=%async_computation.5 | async-start | bytes 8388608 | tf_op jit(solution)/shard_map/all_to_all | solution.py:117
  739.7 10.7 copy-start.13
  739.8 10.7 copy-start.14
  739.8 54.6 %all-to-all-start.3 = ((bf16[8,2,131072]{2,1,0:T(2,128)(2,1)}), bf16[8,2,131072]{2,1,0:T(2,128)(2,1)}, u32[]{:S(2)}, u32[]{:S(2)}) async-start(bf16[8,2,131072]{2,1,0:T(2,128)(2,1)} %reshape.221), calls=%async_computation.3 | async-start | bytes 8388608 | tf_op jit(solution)/shard_map/all_to_all | solution.py:109
  744.7 517.7 %all-reduce.3.cloned.1.call-start = ((), (), s32[]{:S(2)}) async-start(), calls=%async_computation.8 | async-start | bytes 83886080 | tf_op jit(solution)/shard_map/psum | solution.py:123
  817.0 14.1 %copy-start.1 = (bf16[8,128,2048]{2,1,0:T(8,128)(2,1)S(1)}, bf16[8,128,2048]{2,1,0:T(8,128)(2,1)}, u32[]{:S(2)}) copy-start(bf16[8,128,2048]{2,1,0:T(8,128)(2,1)} %param.6) | copy-start | bytes 12582916
  817.0 14.1 %copy-start.8 = (bf16[8,128,2048]{2,1,0:T(8,128)(2,1)S(1)}, bf16[8,128,2048]{2,1,0:T(8,128)(2,1)}, u32[]{:S(2)}) copy-start(bf16[8,128,2048]{2,1,0:T(8,128)(2,1)} %copy.95) | copy-start | bytes 12582916
  817.0 14.1 %copy-start.11 = (bf16[8,128,512]{2,1,0:T(8,128)(2,1)S(1)}, bf16[8,128,512]{2,1,0:T(8,128)(2,1)}, u32[]{:S(2)}) copy-start(bf16[8,128,512]{2,1,0:T(8,128)(2,1)} %copy.96) | copy-start | bytes 3145732
  817.0 14.1 %copy-start.16 = (f32[2048]{0:T(1024)S(1)}, f32[2048]{0:T(1024)}, u32[]{:S(2)}) copy-start(f32[2048]{0:T(1024)} %copy-done.15) | copy-start | bytes 24580
  817.0 14.1 %copy-start.18 = (f32[8,128]{1,0:T(8,128)S(1)}, f32[8,128]{1,0:T(8,128)}, u32[]{:S(2)}) copy-start(f32[8,128]{1,0:T(8,128)} %copy-done.17) | copy-start | bytes 12292
  1262.5 21.8 %copy-start = (f32[32,64,2048]{2,1,0:T(8,128)S(1)}, f32[32,64,2048]{2,1,0:T(8,128)}, u32[]{:S(2)}) copy-start(f32[32,64,2048]{2,1,0:T(8,128)} %get-tuple-element.28) | copy-start | bytes 50331652
  (4 other events, 32.3 us)
Sparse Core Ops, SparseCore 0:
  849.6 412.8 all-reduce.2
where the time goes:
time: 1310 us; the launch traced here: 1300 us
  waiting for transfers between devices  423 us (32%)
  matrix products  397 us (30%)
  local copies, waits for them, and re-layouts  233 us (18%)
  other arithmetic  176 us (13%)
  starting transfers between devices  38.3 us (3%)
  blocking collectives  16 us (1%)
  between operations  14.6 us (1%)
    psum x1, waiting for transfers between devices, device_step(): lax.psum(grad_w_qkv, 'sp')  354 us
    another operation x5, other arithmetic  115 us
    dot_general x1, matrix products, attention_backward(): jnp.einsum('bqkge,bske->bkgqs', grad_attn, value_vals, preferred_element_...  99.7 us
    unnamed x48, local copies, waits for them, and re-layouts  85.4 us
    dot_general x1, matrix products, attention_forward(): jnp.einsum('bkgqs,bske->bqkge', prob_mat.astype(jnp.bfloat16), value_vals...  49.7 us
    dot_general x1, matrix products, attention_backward(): jnp.einsum('bkgqs,bqkge->bske', prob_mat.astype(jnp.bfloat16), grad_attn,...  49.2 us
    dot_general x1, matrix products, causal_probs(): jnp.einsum('bqkge,bske->bkgqs', queries, key_vals, preferred_element_type...  46.3 us
    reduce_sum x1, other arithmetic, causal_probs(): return jax.nn.softmax(jnp.where(causal, scores, MASK_VALUE), axis=-1)  41.6 us
  transfers between devices with their start and end apart: 9, of which 5 were waited for; matrix products, arithmetic and copies ran while one was open for 26% of the time, Pallas kernels for 0%

commit v1 on v0

v1 whole, which is shorter than its diff:
```python
import functools
import math

import jax
import jax.numpy as jnp
from jax import lax
from jax.experimental import pallas as pl
from jax.experimental.pallas import tpu as pltpu
from jax.sharding import Mesh, PartitionSpec as P

NORM_EPS = 1e-5
ROPE_BASE = 10000.0
ROPE_GAIN = math.sqrt(1.0 + math.log(32.0) / math.log(4096.0))
MASK_VALUE = -1e30
LOG2E = math.log2(math.e)
CORES = 2
BF16 = jnp.bfloat16
F32 = jnp.float32
VMEM_LIMIT = 60 * 1024 * 1024

NN = (((1,), (0,)), ((), ()))
NT = (((1,), (1,)), ((), ()))
TN = (((0,), (0,)), ((), ()))


def dot(a, b, dims=NN):
    return lax.dot_general(a, b, dims, preferred_element_type=F32)


def cost(flops, nbytes, trans=0):
    return pl.CostEstimate(flops=int(flops), bytes_accessed=int(nbytes), transcendentals=int(trans))


def params(n_axes=1):
    return pltpu.CompilerParams(dimension_semantics=("arbitrary",) * n_axes, vmem_limit_bytes=VMEM_LIMIT)


def rope_rows(block, cos, sin, direction):
    half = cos.shape[0]
    a, b = block[:half], block[half:2 * half]
    s = sin * direction
    return jnp.concatenate([a * cos - b * s, b * cos + a * s], axis=0)


def kv_proj_kernel(x_ref, g_ref, wk_ref, wv_ref, cos_ref, sin_ref, h_ref, kv_ref):
    nb, tok, d = x_ref.shape
    kvh, _, e2, _ = kv_ref.shape
    e = e2 // 2
    x = x_ref[...].reshape(nb * tok, d).astype(F32)
    inv = lax.rsqrt(jnp.mean(x * x, axis=-1, keepdims=True) + NORM_EPS)
    h = (x * inv * g_ref[...].astype(F32)).astype(BF16)
    h_ref[...] = h.reshape(nb, tok, d)
    cos, sin = cos_ref[...], sin_ref[...]
    k = dot(wk_ref[...], h, NT)
    for i in range(kvh):
        for b in range(nb):
            kv_ref[i, b, 0:e] = rope_rows(k[i * e:(i + 1) * e, b * tok:(b + 1) * tok], cos, sin, 1.0).astype(BF16)
    v = dot(wv_ref[...], h, NT)
    for i in range(kvh):
        for b in range(nb):
            kv_ref[i, b, e:2 * e] = v[i * e:(i + 1) * e, b * tok:(b + 1) * tok].astype(BF16)


def q_proj_kernel(h_ref, w_ref, cos_ref, sin_ref, q_ref):
    nb, tok, d = h_ref.shape
    e = 2 * cos_ref.shape[0]
    rows = w_ref.shape[0]
    h = h_ref[...].reshape(nb * tok, d)
    cos, sin = cos_ref[...], sin_ref[...]
    scale = e ** -0.5
    step = 4 * e
    for r in range(0, rows, step):
        blk = dot(w_ref[r:r + step], h, NT)
        for i in range(0, step, e):
            for b in range(nb):
                q_ref[b, r + i:r + i + e] = (rope_rows(blk[i:i + e, b * tok:(b + 1) * tok], cos, sin, 1.0).astype(BF16)
                                             * scale).astype(BF16)


def do_proj_kernel(g_ref, w_ref, o_ref):
    nb, tok, d = g_ref.shape
    rows = w_ref.shape[0]
    g = g_ref[...].reshape(nb * tok, d)
    step = 256
    for r in range(0, rows, step):
        blk = dot(w_ref[r:r + step], g, NT)
        for b in range(nb):
            o_ref[b, r:r + step] = blk[:, b * tok:(b + 1) * tok].astype(BF16)


def drop_scalar(kernel):
    def wrapped(_, *refs):
        kernel(*refs)
    return wrapped


def attn_kernel(ids, q0_ref, q1_ref, do0_ref, do1_ref, kv_ref, h0_ref, h1_ref, g0_ref, g1_ref, cos_ref, sin_ref,
                own_ref, par_ref, send_ref, s_ref, acc_ref, kvt_ref, gacc_ref):
    chip, core = ids[0], ids[1]
    b_id = pl.program_id(0)
    chips = kv_ref.shape[0]
    rows, tok = q0_ref.shape[1], q0_ref.shape[2]
    e = kv_ref.shape[3] // 2
    reps = rows // e
    blk = 2 * tok
    width = reps * blk

    def heads_to_lanes(first_ref, second_ref):
        full = jnp.concatenate([first_ref[0], second_ref[0]], axis=1)
        return jnp.concatenate([full[i * e:(i + 1) * e] for i in range(reps)], axis=1)

    qt = heads_to_lanes(q0_ref, q1_ref)
    dot_t = heads_to_lanes(do0_ref, do1_ref)
    zero = jnp.zeros_like(qt)
    q_pad = jnp.concatenate([qt, zero], axis=0)
    do_pad = jnp.concatenate([zero, dot_t], axis=0)

    def kv_block(j):
        return jnp.concatenate([kv_ref[j, 0, 0], kv_ref[j, 1, 0]], axis=1)

    def forward_block(j, masked, m_old, l_old):
        kv = kv_block(j)
        kvt = kv.T
        kvt_ref[j] = kvt
        v_t = kv[e:2 * e]
        ms, ls = [], []
        for i in range(reps):
            cols = slice(i * blk, (i + 1) * blk)
            t = dot(kvt, q_pad[:, cols]) * LOG2E
            if masked:
                r = lax.broadcasted_iota(jnp.int32, (blk, blk), 0)
                c = lax.broadcasted_iota(jnp.int32, (blk, blk), 1)
                shift = (1 - 2 * core) * tok
                k_pos = jnp.where(r < tok, r, r - tok + shift)
                q_pos = jnp.where(c < tok, c, c - tok + shift)
                t = jnp.where(k_pos <= q_pos, t, MASK_VALUE)
            s_ref[j, :, cols] = t
            mx = jnp.max(t, axis=0, keepdims=True)
            if masked:
                m_new = mx
                p = jnp.exp2(t - m_new)
                l_new = jnp.sum(p, axis=0, keepdims=True)
                acc_ref[:, cols] = dot(v_t, p.astype(BF16))
            else:
                mo = m_old[:, cols]
                m_new = jnp.maximum(mo, mx)
                p = jnp.exp2(t - m_new)
                alpha = jnp.exp2(mo - m_new)
                l_new = l_old[:, cols] * alpha + jnp.sum(p, axis=0, keepdims=True)
                acc_ref[:, cols] = acc_ref[:, cols] * alpha + dot(v_t, p.astype(BF16))
            ms.append(m_new)
            ls.append(l_new)
        return jnp.concatenate(ms, axis=1), jnp.concatenate(ls, axis=1)

    m, l = forward_block(chip, True, None, None)
    m, l = lax.fori_loop(0, chip, lambda j, ml: forward_block(j, False, *ml), (m, l))

    o_t = acc_ref[...] * (1.0 / l)
    delta = jnp.sum(o_t * dot_t.astype(F32), axis=0, keepdims=True)
    lse = m + jnp.log2(l)
    o_b = o_t.astype(BF16)

    def backward_block(j, first):
        kv = kv_block(j)
        kvt = kvt_ref[j]
        k_t = kv[0:e]
        dk = jnp.zeros((e, blk), F32)
        dv = jnp.zeros((e, blk), F32)
        for i in range(reps):
            cols = slice(i * blk, (i + 1) * blk)
            p = jnp.exp2(s_ref[j, :, cols] - lse[:, cols])
            dp = dot(kvt, do_pad[:, cols])
            ds = (p * (dp - delta[:, cols])).astype(BF16)
            dv = dv + dot(dot_t[:, cols], p.astype(BF16), NT)
            dk = dk + dot(qt[:, cols], ds, NT)
            dq = dot(k_t, ds)
            if first:
                acc_ref[:, cols] = dq
            else:
                acc_ref[:, cols] = acc_ref[:, cols] + dq
        send_ref[j, 0:2 * e, pl.ds(pl.multiple_of(b_id * blk, blk), blk)] = jnp.concatenate([dk, dv], axis=0).astype(BF16)

    backward_block(chip, True)

    def backward_step(j, carry):
        backward_block(j, False)
        return carry

    lax.fori_loop(0, chip, backward_step, 0)

    def zero_step(j, carry):
        send_ref[j, 0:2 * e, pl.ds(pl.multiple_of(b_id * blk, blk), blk)] = jnp.zeros((2 * e, blk), BF16)
        return carry

    lax.fori_loop(chip + 1, chips, zero_step, 0)

    cos = jnp.concatenate([cos_ref[0], cos_ref[1]], axis=1)
    sin = jnp.concatenate([sin_ref[0], sin_ref[1]], axis=1)
    o_rows, dq_rows = [], []
    for i in range(reps):
        cols = slice(i * blk, (i + 1) * blk)
        o_rows.append(o_b[:, cols])
        dq = (acc_ref[:, cols] * (e ** -0.5)).astype(BF16).astype(F32)
        dq_rows.append(rope_rows(dq, cos, sin, -1.0).astype(BF16))
    o_full = jnp.concatenate(o_rows, axis=0)
    dq_full = jnp.concatenate(dq_rows, axis=0)
    own_ref[0, 0] = o_full[:, :tok]
    par_ref[0, 0] = o_full[:, tok:]
    own_ref[1, 0] = dq_full[:, :tok]
    par_ref[1, 0] = dq_full[:, tok:]

    d = h0_ref.shape[2]
    step = 512

    @pl.when(b_id == 0)
    def _():
        gacc_ref[...] = jnp.zeros_like(gacc_ref)

    for c in range(0, d, step):
        cs = slice(c, c + step)
        hh = jnp.concatenate([h0_ref[0, :, cs], h1_ref[0, :, cs]], axis=0)
        gg = jnp.concatenate([g0_ref[0, :, cs], g1_ref[0, :, cs]], axis=0)
        gacc_ref[0:rows, cs] += dot(dq_full, hh)
        gacc_ref[rows:2 * rows, cs] += dot(o_full, gg)

    @pl.when(b_id == pl.num_programs(0) - 1)
    def _():
        for j in range(chips):
            n = rows // chips
            send_ref[j, 2 * e:2 * e + n] = gacc_ref[j * n:(j + 1) * n].astype(BF16)
            send_ref[j, 2 * e + n:2 * e + 2 * n] = gacc_ref[rows + j * n:rows + (j + 1) * n].astype(BF16)


def kv_grad_kernel(*refs, stages):
    recv = refs[:stages]
    h0_ref, h1_ref, cos_ref, sin_ref, own_ref, par_ref, send_ref, gacc_ref = refs[stages:]
    b_id = pl.program_id(0)
    tok = h0_ref.shape[1]
    e2 = own_ref.shape[1] // stages
    e = e2 // 2
    cos = jnp.concatenate([cos_ref[0], cos_ref[1]], axis=1)
    sin = jnp.concatenate([sin_ref[0], sin_ref[1]], axis=1)
    parts = []
    for r in recv:
        total = r[0].astype(F32)
        for j in range(1, r.shape[0]):
            total = total + r[j].astype(F32)
        total = total.astype(BF16).astype(F32)
        parts.append(jnp.concatenate([rope_rows(total[0:e], cos, sin, -1.0), total[e:2 * e]], axis=0).astype(BF16))
    gf = jnp.concatenate(parts, axis=0)
    own_ref[0] = gf[:, :tok]
    par_ref[0] = gf[:, tok:]

    @pl.when(b_id == 0)
    def _():
        gacc_ref[...] = jnp.zeros_like(gacc_ref)

    d = h0_ref.shape[2]
    step = 512
    for c in range(0, d, step):
        cs = slice(c, c + step)
        hh = jnp.concatenate([h0_ref[0, :, cs], h1_ref[0, :, cs]], axis=0)
        gacc_ref[:, cs] += dot(gf, hh)

    @pl.when(b_id == pl.num_programs(0) - 1)
    def _():
        n = send_ref.shape[1]
        for j in range(send_ref.shape[0]):
            send_ref[j] = gacc_ref[j * n:(j + 1) * n].astype(BF16)


def out_kernel(ids, x_ref, w_ref, *refs, stages):
    core = ids[1]
    o_refs, y_ref = refs[:-1], refs[-1]
    nb, tok, d = x_ref.shape
    rows = o_refs[0].shape[2]
    for b in range(nb):
        total = x_ref[b].astype(F32)
        lhs = jnp.concatenate([o[0, b] for o in o_refs], axis=0)
        half = stages * rows
        w_own = w_ref[pl.ds(pl.multiple_of(core * half, half), half), :]
        w_par = w_ref[pl.ds(pl.multiple_of((1 - core) * half, half), half), :]
        total = total + (dot(lhs[:half], w_own, TN) + dot(lhs[half:], w_par, TN))
        y_ref[b] = total.astype(BF16)


def norm_grad_kernel(ids, x_ref, go_ref, g_ref, wt_ref, kv0_ref, kv1_ref, *refs, stages):
    core = ids[1]
    q_refs = refs[:2 * stages]
    gh_ref, gn_ref = refs[2 * stages:]
    nb, tok, d = x_ref.shape
    rows = q_refs[0].shape[2]
    half = stages * rows
    kv_rows = kv0_ref.shape[1]
    e2 = kv_rows // stages
    e = e2 // 2
    kv_half = kv_rows // 2
    g = g_ref[...].astype(F32)

    @pl.when(pl.program_id(0) == 0)
    def _():
        gn_ref[...] = jnp.zeros_like(gn_ref)

    def pick(ref, b):
        full = ref[b]
        ks = jnp.concatenate([full[i * e2:i * e2 + e] for i in range(stages)], axis=0)
        vs = jnp.concatenate([full[i * e2 + e:(i + 1) * e2] for i in range(stages)], axis=0)
        return ks, vs

    for b in range(nb):
        total = jnp.zeros((tok, d), F32)
        for side in range(2):
            who = core if side == 0 else 1 - core
            qs = jnp.concatenate([q[0, b] for q in q_refs[side * stages:(side + 1) * stages]], axis=0)
            ks, vs = pick(kv0_ref if side == 0 else kv1_ref, b)
            total = total + dot(qs, wt_ref[pl.ds(pl.multiple_of(who * half, half), half), :], TN)
            base = 2 * half
            total = total + dot(ks, wt_ref[pl.ds(pl.multiple_of(base + who * kv_half, kv_half), kv_half), :], TN)
            base = base + 2 * kv_half
            total = total + dot(vs, wt_ref[pl.ds(pl.multiple_of(base + who * kv_half, kv_half), kv_half), :], TN)
        x = x_ref[b].astype(F32)
        inv = lax.rsqrt(jnp.mean(x * x, axis=-1, keepdims=True) + NORM_EPS)
        unit = x * inv
        gu = total * g
        mean_dot = jnp.mean(gu * unit, axis=-1, keepdims=True)
        gh_ref[b] = (go_ref[b].astype(F32) + inv * (gu - unit * mean_dot)).astype(BF16)
        gn_ref[...] += jnp.sum((total * unit).reshape(tok // 8, 8, d), axis=0)


def assemble_kernel(in_ref, out_ref):
    chips, n, d = in_ref.shape[0], in_ref.shape[-2], in_ref.shape[-1]
    blk = in_ref[...].reshape(chips * n, d)
    for c in range(0, d, 512):
        out_ref[c:c + 512, :] = blk[:, c:c + 512].astype(F32).T


def solution(mesh):
    chips = mesh.shape['sp'] // CORES
    mesh2 = Mesh(mesh.devices.reshape(mesh.shape['dp'], chips, CORES), ('dp', 'x', 'core'))
    swap = [(i, CORES - 1 - i) for i in range(CORES)]

    def device_step(hidden, norm_w, w_qkv, w_out, long_factor, grad_out):
        n_batch, tok, d = hidden.shape
        n_heads, e = w_out.shape[0], w_out.shape[1]
        kv_heads = (w_qkv.shape[1] // e - n_heads) // 2
        reps = n_heads // kv_heads
        stages = kv_heads // CORES
        rows = reps * e
        q_half = stages * rows
        kv_half = stages * e
        e2 = 2 * e
        half_rot = long_factor.shape[0]
        chip = lax.axis_index('x')
        core = lax.axis_index('core')
        ids = jnp.stack([chip, core]).astype(jnp.int32)
        tiles = 2
        nb = n_batch // tiles

        x_par = lax.ppermute(hidden, 'core', swap)
        go_par = lax.ppermute(grad_out, 'core', swap)
        wt = w_qkv.T
        w_o = w_out.reshape(n_heads * e, d)
        norm2 = norm_w.reshape(1, d)

        exponent = jnp.arange(half_rot, dtype=F32) / half_rot
        inv_freq = 1.0 / (long_factor * jnp.power(ROPE_BASE, exponent))
        sides = jnp.stack([core, 1 - core])
        positions = ((chip * CORES + sides)[:, None] * tok + jnp.arange(tok)[None, :]).astype(F32)
        angles = inv_freq[None, :, None] * positions[:, None, :]
        cos_t, sin_t = jnp.cos(angles) * ROPE_GAIN, jnp.sin(angles) * ROPE_GAIN

        tok_spec = pl.BlockSpec((nb, tok, d), lambda i, _: (i, 0, 0))
        rot_spec = pl.BlockSpec((half_rot, tok), lambda i, _: (0, 0))

        def kv_proj(x, side):
            kb = 2 * q_half // kv_half
            return pl.pallas_call(
                drop_scalar(kv_proj_kernel),
                out_shape=(jax.ShapeDtypeStruct((n_batch, tok, d), BF16), jax.ShapeDtypeStruct((stages, n_batch, e2, tok), BF16)),
                grid_spec=pltpu.PrefetchScalarGridSpec(
                    num_scalar_prefetch=1, grid=(tiles,),
                    in_specs=[tok_spec, pl.BlockSpec((1, d), lambda i, _: (0, 0)),
                              pl.BlockSpec((kv_half, d), lambda i, c: (kb + c[1], 0)),
                              pl.BlockSpec((kv_half, d), lambda i, c: (kb + CORES + c[1], 0)), rot_spec, rot_spec],
                    out_specs=(tok_spec, pl.BlockSpec((stages, nb, e2, tok), lambda i, _: (0, i, 0, 0)))),
                compiler_params=params(), name='kv_proj',
                cost_estimate=cost(2 * n_batch * tok * d * 2 * kv_half, 3 * n_batch * tok * d * 2),
            )(ids, x, norm2, wt, wt, cos_t[side], sin_t[side])

        def q_proj(h, side):
            return pl.pallas_call(
                drop_scalar(q_proj_kernel),
                out_shape=jax.ShapeDtypeStruct((n_batch, q_half, tok), BF16),
                grid_spec=pltpu.PrefetchScalarGridSpec(
                    num_scalar_prefetch=1, grid=(tiles,),
                    in_specs=[tok_spec, pl.BlockSpec((q_half, d), lambda i, c: (c[1], 0)), rot_spec, rot_spec],
                    out_specs=pl.BlockSpec((nb, q_half, tok), lambda i, _: (i, 0, 0))),
                compiler_params=params(), name='q_proj',
                cost_estimate=cost(2 * n_batch * tok * d * q_half, 3 * n_batch * tok * d * 2),
            )(ids, h, wt, cos_t[side], sin_t[side])

        def do_proj(g):
            return pl.pallas_call(
                drop_scalar(do_proj_kernel),
                out_shape=jax.ShapeDtypeStruct((n_batch, q_half, tok), BF16),
                grid_spec=pltpu.PrefetchScalarGridSpec(
                    num_scalar_prefetch=1, grid=(tiles,),
                    in_specs=[tok_spec, pl.BlockSpec((q_half, d), lambda i, c: (c[1], 0))],
                    out_specs=pl.BlockSpec((nb, q_half, tok), lambda i, _: (i, 0, 0))),
                compiler_params=params(), name='do_proj',
                cost_estimate=cost(2 * n_batch * tok * d * q_half, 3 * n_batch * tok * d * 2),
            )(ids, g, w_o)

        h_own, kv_own = kv_proj(hidden, 0)
        h_par, kv_par = kv_proj(x_par, 1)
        gathered = [lax.all_gather(jnp.stack([kv_own[s], kv_par[s]]), 'x') for s in range(stages)]
        q_own, q_par = q_proj(h_own, 0), q_proj(h_par, 1)
        do_own, do_par = do_proj(grad_out), do_proj(go_par)

        def attention(s):
            blk = 2 * tok
            q_spec = pl.BlockSpec((1, rows, tok), lambda b, _: (b, s, 0))
            t_spec = pl.BlockSpec((1, tok, d), lambda b, _: (b, 0, 0))
            r_spec = pl.BlockSpec((2, half_rot, tok), lambda b, _: (0, 0, 0))
            o_spec = pl.BlockSpec((2, 1, rows, tok), lambda b, _: (0, b, 0, 0))
            return pl.pallas_call(
                attn_kernel,
                out_shape=(jax.ShapeDtypeStruct((2, n_batch, rows, tok), BF16), jax.ShapeDtypeStruct((2, n_batch, rows, tok), BF16),
                           jax.ShapeDtypeStruct((chips, e2 + 2 * rows // chips, d), BF16)),
                grid_spec=pltpu.PrefetchScalarGridSpec(
                    num_scalar_prefetch=1, grid=(n_batch,),
                    in_specs=[q_spec, q_spec, q_spec, q_spec,
                              pl.BlockSpec((chips, 2, 1, e2, tok), lambda b, _: (0, 0, b, 0, 0)),
                              t_spec, t_spec, t_spec, t_spec, r_spec, r_spec],
                    out_specs=(o_spec, o_spec, pl.BlockSpec((chips, e2 + 2 * rows // chips, d), lambda b, _: (0, 0, 0))),
                    scratch_shapes=[pltpu.VMEM((chips, blk, reps * blk), F32), pltpu.VMEM((e, reps * blk), F32),
                                    pltpu.VMEM((chips, blk, e2), BF16), pltpu.VMEM((2 * rows, d), F32)]),
                compiler_params=params(), name=f'attn_{s}',
                cost_estimate=cost(4e10, 3e7, 3e7),
            )(ids, q_own, q_par, do_own, do_par, gathered[s], h_own, h_par, grad_out, go_par, cos_t, sin_t)

        own, par, recv = [], [], []
        for s in range(stages):
            own_s, par_s, send_s = attention(s)
            own.append(own_s)
            par.append(lax.ppermute(par_s, 'core', swap))
            recv.append(lax.all_to_all(send_s, 'x', 0, 0, tiled=True))

        n_w = 2 * rows // chips
        shards = [jnp.sum(r[:, e2:].astype(F32), axis=0).astype(BF16) for r in recv]

        blk = 2 * tok
        kv_own_g, kv_par_g, send_kv = pl.pallas_call(
            functools.partial(kv_grad_kernel, stages=stages),
            out_shape=(jax.ShapeDtypeStruct((n_batch, stages * e2, tok), BF16), jax.ShapeDtypeStruct((n_batch, stages * e2, tok), BF16),
                       jax.ShapeDtypeStruct((chips, stages * e2 // chips, d), BF16)),
            grid=(n_batch,),
            in_specs=[pl.BlockSpec((chips, e2, blk), lambda b: (0, 0, b))] * stages
            + [pl.BlockSpec((1, tok, d), lambda b: (b, 0, 0))] * 2 + [pl.BlockSpec((2, half_rot, tok), lambda b: (0, 0, 0))] * 2,
            out_specs=(pl.BlockSpec((1, stages * e2, tok), lambda b: (b, 0, 0)), pl.BlockSpec((1, stages * e2, tok), lambda b: (b, 0, 0)),
                       pl.BlockSpec((chips, stages * e2 // chips, d), lambda b: (0, 0, 0))),
            scratch_shapes=[pltpu.VMEM((stages * e2, d), F32)],
            compiler_params=params(), name='kv_grad',
            cost_estimate=cost(2 * 2 * n_batch * tok * d * stages * e2, 3e7),
        )(*recv, h_own, h_par, cos_t, sin_t)
        kv_other_g = lax.ppermute(kv_par_g, 'core', swap)
        recv_kv = lax.all_to_all(send_kv, 'x', 0, 0, tiled=True)
        shard_kv = jnp.sum(recv_kv.astype(F32), axis=0).astype(BF16)

        nb2 = 2
        t2_spec = pl.BlockSpec((nb2, tok, d), lambda b, _: (b, 0, 0))
        block_out = pl.pallas_call(
            functools.partial(out_kernel, stages=stages),
            out_shape=jax.ShapeDtypeStruct((n_batch, tok, d), BF16),
            grid_spec=pltpu.PrefetchScalarGridSpec(
                num_scalar_prefetch=1, grid=(n_batch // nb2,),
                in_specs=[t2_spec, pl.BlockSpec((n_heads * e, d), lambda b, _: (0, 0))]
                + [pl.BlockSpec((1, nb2, rows, tok), lambda b, _: (0, b, 0, 0))] * (2 * stages),
                out_specs=t2_spec),
            compiler_params=params(), name='out_proj',
            cost_estimate=cost(2 * n_batch * tok * d * n_heads * e, 3e7),
        )(ids, hidden, w_o, *own, *par)

        grad_hidden, gn = pl.pallas_call(
            functools.partial(norm_grad_kernel, stages=stages),
            out_shape=(jax.ShapeDtypeStruct((n_batch, tok, d), BF16), jax.ShapeDtypeStruct((8, d), F32)),
            grid_spec=pltpu.PrefetchScalarGridSpec(
                num_scalar_prefetch=1, grid=(n_batch // nb2,),
                in_specs=[t2_spec, t2_spec, pl.BlockSpec((1, d), lambda b, _: (0, 0)),
                          pl.BlockSpec(wt.shape, lambda b, _: (0, 0))]
                + [pl.BlockSpec((nb2, stages * e2, tok), lambda b, _: (b, 0, 0))] * 2
                + [pl.BlockSpec((1, nb2, rows, tok), lambda b, _: (1, b, 0, 0))] * (2 * stages),
                out_specs=(t2_spec, pl.BlockSpec((8, d), lambda b, _: (0, 0)))),
            compiler_params=params(), name='norm_grad',
            cost_estimate=cost(2 * n_batch * tok * d * wt.shape[0], 4e7),
        )(ids, hidden, grad_out, norm2, wt, kv_own_g, kv_other_g, *own, *par)

        gn_row = jnp.sum(gn, axis=0, keepdims=True)
        gn_hi = gn_row.astype(BF16)
        gn_lo = (gn_row - gn_hi.astype(F32)).astype(BF16)
        pad = jnp.zeros((14, d), BF16)
        tail = lax.all_gather(jnp.concatenate([shard_kv, gn_hi, gn_lo, pad], axis=0), ('x', 'core'))
        main = [lax.all_gather(s, ('x', 'core')) for s in shards]
        main = [m.reshape(chips, CORES, n_w, d) for m in main]
        tail = tail.reshape(chips, CORES, -1, d)
        n_kv = shard_kv.shape[0]

        n_q = rows // chips
        q_part = jnp.stack([m[:, :, :n_q] for m in main])
        o_part = jnp.stack([m[:, :, n_q:] for m in main])
        grad_w_out = jnp.transpose(o_part, (2, 0, 1, 3, 4)).reshape(n_heads, e, d).astype(F32)
        q_cols = jnp.transpose(q_part, (2, 0, 1, 3, 4)).reshape(n_heads * e, d)
        k_cols = jnp.transpose(tail[:, :, :e], (1, 0, 2, 3)).reshape(kv_heads * e, d)
        v_cols = jnp.transpose(tail[:, :, e:2 * e], (1, 0, 2, 3)).reshape(kv_heads * e, d)
        grad_w_qkv = jnp.concatenate([q_cols, k_cols, v_cols], axis=0).astype(F32).T
        gn_all = tail[:, :, n_kv:n_kv + 2].astype(F32)
        grad_norm_w = jnp.sum(gn_all, axis=(0, 1, 2))
        return block_out, grad_hidden, grad_w_qkv, grad_w_out, grad_norm_w

    tok_spec = P('dp', ('x', 'core'), None)
    return jax.shard_map(device_step, mesh=mesh2,
                         in_specs=(tok_spec, P(), P(), P(), P(), tok_spec),
                         out_specs=(tok_spec, tok_spec, P('dp', None), P('dp', None, None), P('dp')),
                         check_vma=False)
```

time: 1310 us -> 818 us (0.62)
  matrix products: 397 us -> 0 us
  waiting for transfers between devices: 423 us -> 68.8 us
  blocking collectives: 16 us -> 306 us
  Pallas kernels: 0 us -> 226 us
  local copies, waits for them, and re-layouts: 233 us -> 88.7 us
  other arithmetic: 176 us -> 42.9 us
  starting transfers between devices: 38.3 us -> 65.3 us
    dot_general x12 -> x0, matrix products: 397 us -> none  [the longest x1 99.7 us: attention_backward(): jnp.einsum('bqkge,bske->bkgqs', grad_attn, value_vals, preferred_element_...]
    psum x1 -> x0, waiting for transfers between devices: 354 us -> none  [device_step(): lax.psum(grad_w_qkv, 'sp')]
    all_to_all x0 -> x3, blocking collectives: none -> 306 us  [device_step(): recv.append(lax.all_to_all(send_s, 'x', 0, 0, tiled=True))]
    pallas_call x0 -> x13, Pallas kernels: none -> 226 us  [the longest x4 119 us: attention(): pl.pallas_call(attn_kernel, out_shape=(jax.ShapeDtypeStruct((2, n_batch,...]
    another operation x5, other arithmetic: 115 us -> 4.04 us  [the longest x4 3.39 us: device_step(): jnp.stack([kv_own[s], kv_par[s]])]
    all_to_all x7 -> x0, local copies, waits for them, and re-layouts: 55.3 us -> none  [the longest x1 12.7 us: device_step(): q_heads = to_heads(q_local).reshape(head_shape)]
    unnamed x48 -> x26, local copies, waits for them, and re-layouts: 85.4 us -> 47.8 us
    reduce_sum x2 -> x7, other arithmetic: 44.7 us -> 9.78 us  [the longest x4 6.73 us: device_step(): shards = [jnp.sum(r[:, e2:].astype(F32), axis=0).astype(BF16) for r in recv]]
  transfers between devices with their start and end apart: 9 -> 18, of which waited for: 5 -> 2; matrix products, arithmetic and copies ran while one was open for 26% -> 9% of each run, Pallas kernels for 0% -> 27%
where the time goes in v1:
time: 818 us; the launch traced here: 812 us
  blocking collectives  306 us (37%)
  Pallas kernels  226 us (28%)
  local copies, waits for them, and re-layouts  88.7 us (11%)
  waiting for transfers between devices  68.8 us (8%)
  starting transfers between devices  65.3 us (8%)
  other arithmetic  42.9 us (5%)
  between operations  14.6 us (2%)
    all_to_all x3, blocking collectives, device_step(): recv.append(lax.all_to_all(send_s, 'x', 0, 0, tiled=True))  306 us
    pallas_call x4, Pallas kernels, attention(): pl.pallas_call(attn_kernel, out_shape=(jax.ShapeDtypeStruct((2, n_batch,...  119 us
    all_to_all x1, waiting for transfers between devices, device_step(): recv.append(lax.all_to_all(send_s, 'x', 0, 0, tiled=True))  64.7 us
    all_to_all x1, starting transfers between devices, device_step(): recv.append(lax.all_to_all(send_s, 'x', 0, 0, tiled=True))  58.3 us
    unnamed x26, local copies, waits for them, and re-layouts  47.8 us
    pallas_call x1, Pallas kernels, device_step(): pl.pallas_call(functools.partial(norm_grad_kernel, stages=stages), out_sh...  26.3 us
    transpose x1, other arithmetic, device_step(): grad_w_qkv = jnp.concatenate([q_cols, k_cols, v_cols], axis=0).astype(F32).T  20.3 us
    pallas_call x2, Pallas kernels, q_proj(): pl.pallas_call(drop_scalar(q_proj_kernel), out_shape=jax.ShapeDtypeStruct...  19.1 us
  transfers between devices with their start and end apart: 18, of which 2 were waited for; matrix products, arithmetic and copies ran while one was open for 9% of the time, Pallas kernels for 27%

profile of v1, /device:TPU:112, one launch (start us, length us, event | category | flops | bytes accessed | tf_op | source)
XLA Modules:
  0.0 812.2 jit_solution(7831808659815949635)
XLA Ops:
  8.6 16.6 %copy.27 = bf16[2048,3072]{0,1:T(8,128)(2,1)} copy(bf16[2048,3072]{1,0:T(8,128)(2,1)} %param.8) | data formatting | bytes 25165824 | tf_op args[2]
  27.0 7.3 kv_proj.2
  35.5 7.3 kv_proj.3
  47.1 9.6 %q_proj.2.q0_ref = bf16[8,1024,128]{2,1,0:T(8,128)(2,1)} custom-call(s32[2]{0:T(128)} %pad_add_fusion._.ids, bf16[8,128,2048]{2,1,0:T(8,128)(2,1)} %get-tuple-element.26.refs_0_.h0_ref.refs_4_, bf16[3072,2048]{1,0:T(8,128)(2,1)} %bitcast.57, f32[32,128]{1,0:T(8,128)} %get-tuple-element.86.refs_4_.refs_2_, f32[32,128]{1,0:T(8,128)} %get-tuple-element.81.refs_5_.refs_3_), custom_call_target="tpu_custom_call" | custom-call | flops 4294967296 | bytes 12582912 | tf_op jit(solution)/shard_map/q_proj/pallas_call | solution.py:391
  56.7 9.2 %do_proj.2.do0_ref = bf16[8,1024,128]{2,1,0:T(8,128)(2,1)} custom-call(s32[2]{0:T(128)} %pad_add_fusion._.ids, bf16[8,128,2048]{2,1,0:T(8,128)(2,1)} %go_ref.1, bf16[2048,2048]{1,0:T(8,128)(2,1)} %bitcast.74), custom_call_target="tpu_custom_call" | custom-call | flops 4294967296 | bytes 12582912 | tf_op jit(solution)/shard_map/do_proj/pallas_call | solution.py:403
  66.8 9.6 %q_proj.3.q1_ref = bf16[8,1024,128]{2,1,0:T(8,128)(2,1)} custom-call(s32[2]{0:T(128)} %pad_add_fusion._.ids, bf16[8,128,2048]{2,1,0:T(8,128)(2,1)} %get-tuple-element.27.refs_0_.h1_ref.refs_5_, bf16[3072,2048]{1,0:T(8,128)(2,1)} %bitcast.58, f32[32,128]{1,0:T(8,128)} %get-tuple-element.87.refs_4_.refs_2_, f32[32,128]{1,0:T(8,128)} %get-tuple-element.80.refs_5_.refs_3_), custom_call_target="tpu_custom_call" | custom-call | flops 4294967296 | bytes 12582912 | tf_op jit(solution)/shard_map/q_proj/pallas_call | solution.py:391
  76.4 9.2 %do_proj.3.do1_ref = bf16[8,1024,128]{2,1,0:T(8,128)(2,1)} custom-call(s32[2]{0:T(128)} %pad_add_fusion._.ids, bf16[8,128,2048]{2,1,0:T(8,128)(2,1)} %collective-permute-done.1.refs_0_.g1_ref, bf16[2048,2048]{1,0:T(8,128)(2,1)} %bitcast.75), custom_call_target="tpu_custom_call" | custom-call | flops 4294967296 | bytes 12582912 | tf_op jit(solution)/shard_map/do_proj/pallas_call | solution.py:403
  85.6 29.7 %attn_3.1 = (bf16[2,8,256,128]{3,2,1,0:T(8,128)(2,1)}, bf16[2,8,256,128]{3,2,1,0:T(8,128)(2,1)}, bf16[4,256,2048]{2,1,0:T(8,128)(2,1)}) custom-call(s32[2]{0:T(128)} %pad_add_fusion._.ids, bf16[8,1024,128]{2,1,0:T(8,128)(2,1)} %q_proj.2.q0_ref, bf16[8,1024,128]{2,1,0:T(8,128)(2,1)} %q_proj.3.q1_ref, bf16[8,1024,128]{2,1,0:T(8,128)(2,1)} %do_proj.2.do0_ref, ...), custom_call_target="tpu_custom_call" | custom-call | flops 40000000000 | bytes 30000000 | tf_op jit(solution)/shard_map/attn_3/pallas_call | solution.py:426
  115.3 58.3 %all-to-all-start.3 = ((bf16[4,256,2048]{2,1,0:T(8,128)(2,1)}), bf16[4,256,2048]{2,1,0:T(8,128)(2,1)}, u32[]{:S(2)}, u32[]{:S(2)}) async-start(bf16[4,256,2048]{2,1,0:T(8,128)(2,1)} %get-tuple-element.41), calls=%async_computation.3 | async-start | bytes 8388608 | tf_op jit(solution)/shard_map/all_to_all | solution.py:447
  174.8 64.7 %all-to-all-done.3.refs_3_ = bf16[4,256,2048]{2,1,0:T(8,128)(2,1)} async-done(((bf16[4,256,2048]{2,1,0:T(8,128)(2,1)}), bf16[4,256,2048]{2,1,0:T(8,128)(2,1)}, u32[]{:S(2)}, u32[]{:S(2)}) %all-to-all-start.3) | async-done | bytes 4194336 | tf_op jit(solution)/shard_map/all_to_all | solution.py:447
  242.6 29.7 %attn_2.1 = (bf16[2,8,256,128]{3,2,1,0:T(8,128)(2,1)}, bf16[2,8,256,128]{3,2,1,0:T(8,128)(2,1)}, bf16[4,256,2048]{2,1,0:T(8,128)(2,1)}) custom-call(s32[2]{0:T(128)} %pad_add_fusion._.ids, bf16[8,1024,128]{2,1,0:T(8,128)(2,1)} %q_proj.2.q0_ref, bf16[8,1024,128]{2,1,0:T(8,128)(2,1)} %q_proj.3.q1_ref, bf16[8,1024,128]{2,1,0:T(8,128)(2,1)} %do_proj.2.do0_ref, ...), custom_call_target="tpu_custom_call" | custom-call | flops 40000000000 | bytes 30000000 | tf_op jit(solution)/shard_map/attn_2/pallas_call | solution.py:426
  272.4 103.1 %all_to_all.25.refs_2_ = bf16[4,256,2048]{2,1,0:T(8,128)(2,1)S(1)} all-to-all(bf16[4,256,2048]{2,1,0:T(8,128)(2,1)} %get-tuple-element.40), channel_id=1, replica_groups=mesh['dp'=2,'x'=4,'core'=2] {'x'}, dimensions={0} | all-to-all | bytes 8388608 | tf_op jit(solution)/shard_map/all_to_all | solution.py:447
  378.9 29.7 %attn_1.1 = (bf16[2,8,256,128]{3,2,1,0:T(8,128)(2,1)}, bf16[2,8,256,128]{3,2,1,0:T(8,128)(2,1)}, bf16[4,256,2048]{2,1,0:T(8,128)(2,1)}) custom-call(s32[2]{0:T(128)} %pad_add_fusion._.ids, bf16[8,1024,128]{2,1,0:T(8,128)(2,1)} %q_proj.2.q0_ref, bf16[8,1024,128]{2,1,0:T(8,128)(2,1)} %q_proj.3.q1_ref, bf16[8,1024,128]{2,1,0:T(8,128)(2,1)} %do_proj.2.do0_ref, ...), custom_call_target="tpu_custom_call" | custom-call | flops 40000000000 | bytes 30000000 | tf_op jit(solution)/shard_map/attn_1/pallas_call | solution.py:426
  408.6 102.1 %all_to_all.26.refs_1_ = bf16[4,256,2048]{2,1,0:T(8,128)(2,1)S(1)} all-to-all(bf16[4,256,2048]{2,1,0:T(8,128)(2,1)} %get-tuple-element.39), channel_id=1, replica_groups=mesh['dp'=2,'x'=4,'core'=2] {'x'}, dimensions={0} | all-to-all | bytes 8388608 | tf_op jit(solution)/shard_map/all_to_all | solution.py:447
  514.1 29.7 %attn_0.1 = (bf16[2,8,256,128]{3,2,1,0:T(8,128)(2,1)}, bf16[2,8,256,128]{3,2,1,0:T(8,128)(2,1)}, bf16[4,256,2048]{2,1,0:T(8,128)(2,1)}) custom-call(s32[2]{0:T(128)} %pad_add_fusion._.ids, bf16[8,1024,128]{2,1,0:T(8,128)(2,1)} %q_proj.2.q0_ref, bf16[8,1024,128]{2,1,0:T(8,128)(2,1)} %q_proj.3.q1_ref, bf16[8,1024,128]{2,1,0:T(8,128)(2,1)} %do_proj.2.do0_ref, ...), custom_call_target="tpu_custom_call" | custom-call | flops 40000000000 | bytes 30000000 | tf_op jit(solution)/shard_map/attn_0/pallas_call | solution.py:426
  543.8 100.8 %all_to_all.27.refs_0_ = bf16[4,256,2048]{2,1,0:T(8,128)(2,1)S(1)} all-to-all(bf16[4,256,2048]{2,1,0:T(8,128)(2,1)} %get-tuple-element.38), channel_id=1, replica_groups=mesh['dp'=2,'x'=4,'core'=2] {'x'}, dimensions={0} | all-to-all | bytes 8388608 | tf_op jit(solution)/shard_map/all_to_all | solution.py:447
  649.1 13.2 %kv_grad.1 = (bf16[8,512,128]{2,1,0:T(8,128)(2,1)}, bf16[8,512,128]{2,1,0:T(8,128)(2,1)}, bf16[4,128,2048]{2,1,0:T(8,128)(2,1)}) custom-call(bf16[4,256,2048]{2,1,0:T(8,128)(2,1)} %copy-done.2, bf16[4,256,2048]{2,1,0:T(8,128)(2,1)} %copy-done.1, bf16[4,256,2048]{2,1,0:T(8,128)(2,1)} %copy-done, bf16[4,256,2048]{2,1,0:T(8,128)(2,1)} %all-to-all-done.3.refs_3_, ...), custom_call_target="tpu_custom_call" | custom-call | flops 4294967296 | bytes 30000000 | tf_op jit(solution)/shard_map/kv_grad/pallas_call | solution.py:453
  666.6 26.3 %norm_grad.1 = (bf16[8,128,2048]{2,1,0:T(8,128)(2,1)}, f32[8,2048]{1,0:T(8,128)}) custom-call(s32[2]{0:T(128)} %pad_add_fusion._.ids, bf16[8,128,2048]{2,1,0:T(8,128)(2,1)} %x_ref.3, bf16[8,128,2048]{2,1,0:T(8,128)(2,1)} %go_ref.1, bf16[1,2048]{1,0:T(2,128)(2,1)} %reshape.106.refs_1_.g_ref, bf16[3072,2048]{1,0:T(8,128)(2,1)} %bitcast.59, ...), custom_call_target="tpu_custom_call" | custom-call | flops 12884901888 | bytes 40000000 | tf_op jit(solution)/shard_map/norm_grad/pallas_call | solution.py:484
  698.8 15.6 %out_proj.1 = bf16[8,128,2048]{2,1,0:T(8,128)(2,1)} custom-call(s32[2]{0:T(128)} %pad_add_fusion._.ids, bf16[8,128,2048]{2,1,0:T(8,128)(2,1)} %x_ref.3, bf16[2048,2048]{1,0:T(8,128)(2,1)} %bitcast.76, bf16[2,8,256,128]{3,2,1,0:T(8,128)(2,1)} %get-tuple-element.30.refs_0_, bf16[2,8,256,128]{3,2,1,0:T(8,128)(2,1)} %get-tuple-element.31.refs_1_, ...), custom_call_target="tpu_custom_call" | custom-call | flops 8589934592 | bytes 30000000 | tf_op jit(solution)/shard_map/out_proj/pallas_call | solution.py:472
  723.2 4.9 slice_bitcast_fusion.2
  736.5 8.6 %copy.28 = bf16[2,4,4,64,2048]{4,3,2,1,0:T(8,128)(2,1)} copy(bf16[2,4,4,64,2048]{4,3,0,2,1:T(8,128)(2,1)} %maximum_bitcast_fusion) | data formatting | bytes 16777216 | tf_op jit(solution)/shard_map/transpose | solution.py:512
  748.7 6.2 copy.31
  760.3 20.3 %convert_bitcast_fusion = f32[2048,3072]{0,1:T(8,128)} fusion(bf16[512,2048]{1,0:T(8,128)(2,1)S(1)} %bitcast.64, bf16[512,2048]{1,0:T(8,128)(2,1)S(1)} %bitcast.65, bf16[2048,2048]{1,0:T(8,128)(2,1)S(1)} %bitcast.62), kind=kLoop, calls=%fused_computation | loop fusion | flops 37748736 | bytes 37748736 | tf_op jit(solution)/shard_map/transpose | solution.py:515
  780.6 24.7 %copy.32 = f32[2048,3072]{1,0:T(8,128)} copy(f32[2048,3072]{0,1:T(8,128)} %convert_bitcast_fusion) | data formatting | bytes 50331648
  (101 shorter events, 61.4 us)
Async XLA Ops:
  7.2 78.5 %all-gather.25.cloned.1.call-start = ((), (), s32[]{:S(2)}) async-start(), calls=%async_computation.8 | async-start | bytes 2621440 | tf_op jit(solution)/shard_map/all_gather | solution.py:416
  7.2 28.3 %collective-permute-start = (bf16[8,128,2048]{2,1,0:T(8,128)(2,1)}, bf16[8,128,2048]{2,1,0:T(8,128)(2,1)}, u32[]{:S(2)}, u32[]{:S(2)}) collective-permute-start(bf16[8,128,2048]{2,1,0:T(8,128)(2,1)} %x_ref.3), channel_id=1, source_target_pairs={{0,1},{1,0},{2,3},{3,2},{4,5},{5,4},{6,7},{7,6},{8,9},{9,8},{10,11... | collective-permute-start | bytes 12582920 | tf_op jit(solution)/shard_map/ppermute | solution.py:359
  8.6 17.3 %copy-start.9 = (f32[32]{0:T(128)S(1)}, f32[32]{0:T(128)}, u32[]{:S(2)}) copy-start(f32[32]{0:T(128)} %param.10) | copy-start | bytes 388
  26.3 7.9 copy-start.7
  26.3 7.9 copy-start.8
  45.0 197.7 %all-gather.23.cloned.1.call-start = ((), (), s32[]{:S(2)}) async-start(), calls=%async_computation.7 | async-start | bytes 2621440 | tf_op jit(solution)/shard_map/all_gather | solution.py:416
  45.1 31.3 %collective-permute-start.1 = (bf16[8,128,2048]{2,1,0:T(8,128)(2,1)}, bf16[8,128,2048]{2,1,0:T(8,128)(2,1)}, u32[]{:S(2)}, u32[]{:S(2)}) collective-permute-start(bf16[8,128,2048]{2,1,0:T(8,128)(2,1)} %go_ref.1), channel_id=1, source_target_pairs={{0,1},{1,0},{2,3},{3,2},{4,5},{5,4},{6,7},{7,6},{8,9},{9,8},{10,11... | collective-permute-start | bytes 12582920 | tf_op jit(solution)/shard_map/ppermute | solution.py:360
  46.5 332.3 %all-gather.21.cloned.1.call-start = ((), (), s32[]{:S(2)}) async-start(), calls=%async_computation.6 | async-start | bytes 2621440 | tf_op jit(solution)/shard_map/all_gather | solution.py:416
  115.3 124.2 %all-to-all-start.3 = ((bf16[4,256,2048]{2,1,0:T(8,128)(2,1)}), bf16[4,256,2048]{2,1,0:T(8,128)(2,1)}, u32[]{:S(2)}, u32[]{:S(2)}) async-start(bf16[4,256,2048]{2,1,0:T(8,128)(2,1)} %get-tuple-element.41), calls=%async_computation.3 | async-start | bytes 8388608 | tf_op jit(solution)/shard_map/all_to_all | solution.py:447
  173.6 340.5 %all-gather.19.cloned.1.call-start = ((), (), s32[]{:S(2)}) async-start(), calls=%async_computation.5 | async-start | bytes 2621440 | tf_op jit(solution)/shard_map/all_gather | solution.py:416
  174.7 539.7 %all-gather.33.cloned.1.call-start = ((), (), s32[]{:S(2)}) async-start(), calls=%async_computation.12 | async-start | bytes 4718592 | tf_op jit(solution)/shard_map/all_gather | solution.py:503
  242.6 475.8 %all-gather.31.cloned.1.call-start = ((), (), s32[]{:S(2)}) async-start(), calls=%async_computation.11 | async-start | bytes 4718592 | tf_op jit(solution)/shard_map/all_gather | solution.py:503
  378.8 344.5 %all-gather.29.cloned.1.call-start = ((), (), s32[]{:S(2)}) async-start(), calls=%async_computation.10 | async-start | bytes 4718592 | tf_op jit(solution)/shard_map/all_gather | solution.py:503
  514.0 214.1 %all-gather.27.cloned.1.call-start = ((), (), s32[]{:S(2)}) async-start(), calls=%async_computation.9 | async-start | bytes 4718592 | tf_op jit(solution)/shard_map/all_gather | solution.py:503
  648.0 18.6 %collective-permute-start.2 = (bf16[2,8,256,128]{3,2,1,0:T(8,128)(2,1)}, bf16[2,8,256,128]{3,2,1,0:T(8,128)(2,1)}, u32[]{:S(2)}, u32[]{:S(2)}) collective-permute-start(bf16[2,8,256,128]{3,2,1,0:T(8,128)(2,1)} %get-tuple-element.34), channel_id=1, source_target_pairs={{0,1},{1,0},{2,3},{3,2},{4,5},{5,4},{6,7},{7,6},{8,9},{9,8},{10,11... | collective-permute-start | bytes 3145736 | tf_op jit(solution)/shard_map/ppermute | solution.py:446
  648.1 18.5 %collective-permute-start.3 = (bf16[2,8,256,128]{3,2,1,0:T(8,128)(2,1)}, bf16[2,8,256,128]{3,2,1,0:T(8,128)(2,1)}, u32[]{:S(2)}, u32[]{:S(2)}) collective-permute-start(bf16[2,8,256,128]{3,2,1,0:T(8,128)(2,1)} %get-tuple-element.35), channel_id=1, source_target_pairs={{0,1},{1,0},{2,3},{3,2},{4,5},{5,4},{6,7},{7,6},{8,9},{9,8},{10,11... | collective-permute-start | bytes 3145736 | tf_op jit(solution)/shard_map/ppermute | solution.py:446
  648.6 18.0 %collective-permute-start.4 = (bf16[2,8,256,128]{3,2,1,0:T(8,128)(2,1)}, bf16[2,8,256,128]{3,2,1,0:T(8,128)(2,1)}, u32[]{:S(2)}, u32[]{:S(2)}) collective-permute-start(bf16[2,8,256,128]{3,2,1,0:T(8,128)(2,1)} %get-tuple-element.36), channel_id=1, source_target_pairs={{0,1},{1,0},{2,3},{3,2},{4,5},{5,4},{6,7},{7,6},{8,9},{9,8},{10,11... | collective-permute-start | bytes 3145736 | tf_op jit(solution)/shard_map/ppermute | solution.py:446
  648.6 17.9 %collective-permute-start.5 = (bf16[2,8,256,128]{3,2,1,0:T(8,128)(2,1)}, bf16[2,8,256,128]{3,2,1,0:T(8,128)(2,1)}, u32[]{:S(2)}, u32[]{:S(2)}) collective-permute-start(bf16[2,8,256,128]{3,2,1,0:T(8,128)(2,1)} %get-tuple-element.37), channel_id=1, source_target_pairs={{0,1},{1,0},{2,3},{3,2},{4,5},{5,4},{6,7},{7,6},{8,9},{9,8},{10,11... | collective-permute-start | bytes 3145736 | tf_op jit(solution)/shard_map/ppermute | solution.py:446
  662.3 4.3 collective-permute-start.6
  662.6 34.7 %all-to-all-start.4 = ((bf16[4,128,2048]{2,1,0:T(8,128)(2,1)}), bf16[4,128,2048]{2,1,0:T(8,128)(2,1)S(1)}, u32[]{:S(2)}, u32[]{:S(2)}) async-start(bf16[4,128,2048]{2,1,0:T(8,128)(2,1)} %get-tuple-element.45), calls=%async_computation.4 | async-start | bytes 4194304 | tf_op jit(solution)/shard_map/all_to_all | solution.py:467
  666.3 88.7 %all-gather.35.cloned.1.call-start = ((), (), s32[]{:S(2)}) async-start(), calls=%async_computation.13 | async-start | bytes 5308416 | tf_op jit(solution)/shard_map/all_gather | solution.py:502
  728.1 4.6 copy-start.6
  736.5 8.6 %copy-start.3 = (bf16[1,4,2,64,2048]{4,3,2,1,0:T(8,128)(2,1)S(1)}, bf16[1,4,2,64,2048]{4,3,2,1,0:T(8,128)(2,1)}, u32[]{:S(2)}) copy-start(bf16[1,4,2,64,2048]{4,3,2,1,0:T(8,128)(2,1)} %get-tuple-element.68) | copy-start | bytes 6291460
  754.9 5.2 slice-start
  (6 other events, 17.3 us)
Sparse Core Ops, SparseCore 0:
  45.1 29.4 all-gather.24
  76.1 26.4 all-gather.22
  104.2 26.5 all-gather.20
  175.6 64.5 all-gather.18
  242.7 28.0 all-gather.32
  378.9 27.7 all-gather.30
  514.2 27.7 all-gather.28
  648.1 32.0 all-gather.26
  698.9 29.5 all-gather.34

commit v2 on v1

v2 whole, which is shorter than its diff:
```python
import functools
import math

import jax
import jax.numpy as jnp
from jax import lax
from jax.experimental import pallas as pl
from jax.experimental.pallas import tpu as pltpu
from jax.sharding import Mesh, PartitionSpec as P


NORM_EPS = 1e-5
ROPE_BASE = 10000.0
ROPE_GAIN = math.sqrt(1.0 + math.log(32.0) / math.log(4096.0))
MASK_VALUE = -1e30
LOG2E = math.log2(math.e)
CORES = 2
BF16 = jnp.bfloat16
F32 = jnp.float32
VMEM_LIMIT = 60 * 1024 * 1024

NN = (((1,), (0,)), ((), ()))
NT = (((1,), (1,)), ((), ()))


def dot(a, b, dims=NN):
    return lax.dot_general(a, b, dims, preferred_element_type=F32)


def cost(flops, nbytes, trans=0):
    return pl.CostEstimate(flops=int(flops), bytes_accessed=int(nbytes), transcendentals=int(trans))


def params(n_axes=1):
    return pltpu.CompilerParams(dimension_semantics=("arbitrary",) * n_axes, vmem_limit_bytes=VMEM_LIMIT)


def rope_rows(block, cos, sin, direction):
    half = cos.shape[0]
    a, b = block[:half], block[half:2 * half]
    s = sin * direction
    return jnp.concatenate([a * cos - b * s, b * cos + a * s], axis=0)


def kv_proj_kernel(x_ref, g_ref, wk_ref, wv_ref, cos_ref, sin_ref, h_ref, kv_ref):
    nb, tok, d = x_ref.shape
    kvh, _, e2, _ = kv_ref.shape
    e = e2 // 2
    x = x_ref[...].reshape(nb * tok, d).astype(F32)
    inv = lax.rsqrt(jnp.mean(x * x, axis=-1, keepdims=True) + NORM_EPS)
    h = (x * inv * g_ref[...].astype(F32)).astype(BF16)
    h_ref[...] = h.reshape(nb, tok, d)
    cos, sin = cos_ref[...], sin_ref[...]
    k = dot(h, wk_ref[...]).T
    for i in range(kvh):
        for b in range(nb):
            kv_ref[i, b, 0:e] = rope_rows(k[i * e:(i + 1) * e, b * tok:(b + 1) * tok], cos, sin, 1.0).astype(BF16)
    v = dot(h, wv_ref[...]).T
    for i in range(kvh):
        for b in range(nb):
            kv_ref[i, b, e:2 * e] = v[i * e:(i + 1) * e, b * tok:(b + 1) * tok].astype(BF16)


def q_proj_kernel(h0_ref, h1_ref, w_ref, cos_ref, sin_ref, q0_ref, q1_ref):
    nb, tok, d = h0_ref.shape
    e = 2 * cos_ref.shape[1]
    rows = w_ref.shape[1]
    scale = e ** -0.5
    step = 4 * e

    def run(h_ref, q_ref, side):
        h = h_ref[...].reshape(nb * tok, d)
        cos, sin = cos_ref[side], sin_ref[side]
        for r in range(0, rows, step):
            blk = dot(h, w_ref[:, r:r + step]).T
            for i in range(0, step, e):
                for b in range(nb):
                    q_ref[b, r + i:r + i + e] = (rope_rows(blk[i:i + e, b * tok:(b + 1) * tok], cos, sin, 1.0).astype(BF16)
                                                 * scale).astype(BF16)

    half = pl.num_programs(0) // 2
    pl.when(pl.program_id(0) < half)(lambda: run(h0_ref, q0_ref, 0))
    pl.when(pl.program_id(0) >= half)(lambda: run(h1_ref, q1_ref, 1))


def do_proj_kernel(g0_ref, g1_ref, w_ref, o0_ref, o1_ref):
    nb, tok, d = g0_ref.shape
    rows = w_ref.shape[0]
    step = 256

    def run(g_ref, o_ref):
        g = g_ref[...].reshape(nb * tok, d)
        for r in range(0, rows, step):
            blk = dot(w_ref[r:r + step], g, NT)
            for b in range(nb):
                o_ref[b, r:r + step] = blk[:, b * tok:(b + 1) * tok].astype(BF16)

    half = pl.num_programs(0) // 2
    pl.when(pl.program_id(0) < half)(lambda: run(g0_ref, o0_ref))
    pl.when(pl.program_id(0) >= half)(lambda: run(g1_ref, o1_ref))


def drop_scalar(kernel):
    def wrapped(_, *refs):
        kernel(*refs)

    return wrapped


def attn_kernel(ids, q0_ref, q1_ref, do0_ref, do1_ref, kv_ref, h0_ref, h1_ref, g0_ref, g1_ref, cos_ref, sin_ref,
                own_ref, par_ref, send_ref, s_ref, acc_ref, kvt_ref, lhs_ref, gacc_ref):
    chip, core = ids[0], ids[1]
    b_id = pl.program_id(0)
    chips = kv_ref.shape[0]
    rows, tok = q0_ref.shape[1], q0_ref.shape[2]
    e = kv_ref.shape[3] // 2
    reps = rows // e
    blk = 2 * tok

    def heads_to_lanes(first_ref, second_ref):
        full = jnp.concatenate([first_ref[0], second_ref[0]], axis=1)
        return jnp.concatenate([full[i * e:(i + 1) * e] for i in range(reps)], axis=1)

    qt = heads_to_lanes(q0_ref, q1_ref)
    dot_t = heads_to_lanes(do0_ref, do1_ref)
    zero = jnp.zeros_like(qt)
    q_pad = jnp.concatenate([qt, zero], axis=0)
    do_pad = jnp.concatenate([zero, dot_t], axis=0)
    head_cols = [slice(i * blk, (i + 1) * blk) for i in range(reps)]

    def kv_block(j):
        return jnp.concatenate([kv_ref[j, 0, 0], kv_ref[j, 1, 0]], axis=1)

    def scores(j, masked):
        kvt = kv_block(j).T
        kvt_ref[j] = kvt
        tops = []
        for cols in head_cols:
            t = dot(kvt, q_pad[:, cols])
            if masked:
                r = lax.broadcasted_iota(jnp.int32, (blk, blk), 0)
                c = lax.broadcasted_iota(jnp.int32, (blk, blk), 1)
                shift = (1 - 2 * core) * tok
                k_pos = jnp.where(r < tok, r, r - tok + shift)
                q_pos = jnp.where(c < tok, c, c - tok + shift)
                t = jnp.where(k_pos <= q_pos, t, MASK_VALUE)
            s_ref[j, :, cols] = t
            tops.append(jnp.max(t, axis=0, keepdims=True))
        return jnp.concatenate(tops, axis=1) * LOG2E

    def accumulate(j, m):
        v_t = kv_block(j)[e:2 * e]
        sums, outs = [], []
        for cols in head_cols:
            p = jnp.exp2(s_ref[j, :, cols] * LOG2E - m[:, cols])
            sums.append(jnp.sum(p, axis=0, keepdims=True))
            outs.append(dot(v_t, p.astype(BF16)))
        return jnp.concatenate(sums, axis=1), jnp.concatenate(outs, axis=1)

    acc_ref[...] = jnp.zeros_like(acc_ref)
    m = scores(chip, True)

    def forward_step(j, carry):
        m, l = carry
        prev = jnp.where(j == 0, chip, j - 1)
        add_l, add_o = accumulate(prev, m)
        m_new = jnp.maximum(m, scores(j, False))
        alpha = jnp.exp2(m - m_new)
        acc_ref[...] = (acc_ref[...] + add_o) * alpha
        return m_new, (l + add_l) * alpha

    m, l = lax.fori_loop(0, chip, forward_step, (m, jnp.zeros_like(m)))
    add_l, add_o = accumulate(jnp.where(chip == 0, chip, chip - 1), m)
    l = l + add_l

    o_t = (acc_ref[...] + add_o) * (1.0 / l)
    delta = jnp.sum(o_t * dot_t.astype(F32), axis=0, keepdims=True)
    lse = m + jnp.log2(l)
    o_b = o_t.astype(BF16)

    def backward_block(j, first):
        kvt = kvt_ref[j]
        k_t = kv_block(j)[0:e]
        dk = jnp.zeros((e, blk), F32)
        dv = jnp.zeros((e, blk), F32)
        for cols in head_cols:
            p = jnp.exp2(s_ref[j, :, cols] * LOG2E - lse[:, cols])
            dp = dot(kvt, do_pad[:, cols])
            ds = (p * (dp - delta[:, cols])).astype(BF16)
            dv = dv + dot(dot_t[:, cols], p.astype(BF16), NT)
            dk = dk + dot(qt[:, cols], ds, NT)
            dq = dot(k_t, ds)
            if first:
                acc_ref[:, cols] = dq
            else:
                acc_ref[:, cols] = acc_ref[:, cols] + dq
        send_ref[j, 0:2 * e, pl.ds(pl.multiple_of(b_id * blk, blk), blk)] = jnp.concatenate([dk, dv], axis=0).astype(BF16)

    backward_block(chip, True)

    def backward_step(j, carry):
        backward_block(j, False)
        return carry

    lax.fori_loop(0, chip, backward_step, 0)

    def zero_step(j, carry):
        send_ref[j, 0:2 * e, pl.ds(pl.multiple_of(b_id * blk, blk), blk)] = jnp.zeros((2 * e, blk), BF16)
        return carry

    lax.fori_loop(chip + 1, chips, zero_step, 0)

    cos = jnp.concatenate([cos_ref[0], cos_ref[1]], axis=1)
    sin = jnp.concatenate([sin_ref[0], sin_ref[1]], axis=1)
    dq_rows = []
    for cols in head_cols:
        dq = (acc_ref[:, cols] * (e ** -0.5)).astype(BF16).astype(F32)
        dq_rows.append(rope_rows(dq, cos, sin, -1.0).astype(BF16))
    o_full = jnp.concatenate([o_b[:, cols] for cols in head_cols], axis=0)
    dq_full = jnp.concatenate(dq_rows, axis=0)
    own_ref[0, 0] = o_full[:, :tok]
    par_ref[0, 0] = o_full[:, tok:]
    own_ref[1, 0] = dq_full[:, :tok]
    par_ref[1, 0] = dq_full[:, tok:]

    d = h0_ref.shape[2]
    step = 512
    odd = lax.rem(b_id, 2)
    lhs_ref[odd, 0:rows] = dq_full
    lhs_ref[odd, rows:2 * rows] = o_full

    def weight_grads(first):
        for c in range(0, d, step):
            cs = slice(c, c + step)
            for r, (a_ref, b_ref) in enumerate(((h0_ref, h1_ref), (g0_ref, g1_ref))):
                rs = slice(r * rows, (r + 1) * rows)
                lhs = jnp.concatenate([lhs_ref[0, rs], lhs_ref[1, rs]], axis=1)
                rhs = jnp.concatenate([a_ref[0, :, cs], b_ref[0, :, cs], a_ref[1, :, cs], b_ref[1, :, cs]], axis=0)
                if first:
                    gacc_ref[rs, cs] = dot(lhs, rhs)
                else:
                    gacc_ref[rs, cs] += dot(lhs, rhs)

    pl.when(b_id == 1)(lambda: weight_grads(True))
    pl.when((odd == 1) & (b_id > 1))(lambda: weight_grads(False))

    @pl.when(b_id == pl.num_programs(0) - 1)
    def _():
        for j in range(chips):
            n = rows // chips
            send_ref[j, 2 * e:2 * e + n] = gacc_ref[j * n:(j + 1) * n].astype(BF16)
            send_ref[j, 2 * e + n:2 * e + 2 * n] = gacc_ref[rows + j * n:rows + (j + 1) * n].astype(BF16)


def kv_grad_kernel(*refs, stages):
    recv = refs[:stages]
    h0_ref, h1_ref, cos_ref, sin_ref, own_ref, par_ref, send_ref, gacc_ref = refs[stages:]
    b_id = pl.program_id(0)
    tok = h0_ref.shape[1]
    e2 = own_ref.shape[1] // stages
    e = e2 // 2
    cos = jnp.concatenate([cos_ref[0], cos_ref[1]], axis=1)
    sin = jnp.concatenate([sin_ref[0], sin_ref[1]], axis=1)
    parts = []
    for r in recv:
        total = r[0].astype(F32)
        for j in range(1, r.shape[0]):
            total = total + r[j].astype(F32)
        total = total.astype(BF16).astype(F32)
        parts.append(jnp.concatenate([rope_rows(total[0:e], cos, sin, -1.0), total[e:2 * e]], axis=0).astype(BF16))
    gf = jnp.concatenate(parts, axis=0)
    own_ref[0] = gf[:, :tok]
    par_ref[0] = gf[:, tok:]

    @pl.when(b_id == 0)
    def _():
        gacc_ref[...] = jnp.zeros_like(gacc_ref)

    d = h0_ref.shape[2]
    step = 512
    for c in range(0, d, step):
        cs = slice(c, c + step)
        hh = jnp.concatenate([h0_ref[0, :, cs], h1_ref[0, :, cs]], axis=0)
        gacc_ref[:, cs] += dot(gf, hh)

    @pl.when(b_id == pl.num_programs(0) - 1)
    def _():
        n = send_ref.shape[1]
        for j in range(send_ref.shape[0]):
            send_ref[j] = gacc_ref[j * n:(j + 1) * n].astype(BF16)


def out_kernel(ids, x_ref, w_ref, *refs, stages):
    core = ids[1]
    o_refs, (y_ref, lhs_ref) = refs[:-2], refs[-2:]
    nb, tok, d = x_ref.shape
    rows = o_refs[0].shape[2]
    half = stages * rows
    for side in range(2):
        base = (core if side == 0 else 1 - core) * half
        for s in range(stages):
            for b in range(nb):
                lhs_ref[b * tok:(b + 1) * tok, pl.ds(pl.multiple_of(base + s * rows, rows), rows)] = o_refs[side * stages + s][0, b].T
    lhs = lhs_ref[...]
    step = 512
    for c in range(0, d, step):
        prod = dot(lhs, w_ref[:, c:c + step])
        y_ref[:, :, c:c + step] = (x_ref[:, :, c:c + step].astype(F32) + prod.reshape(nb, tok, step)).astype(BF16)


def norm_grad_kernel(ids, x_ref, go_ref, g_ref, w_ref, kv0_ref, kv1_ref, *refs, stages):
    core = ids[1]
    q_refs = refs[:2 * stages]
    gh_ref, gn_ref, lhs_ref, tot_ref = refs[2 * stages:]
    nb, tok, d = x_ref.shape
    rows = q_refs[0].shape[2]
    half = stages * rows
    e2 = kv0_ref.shape[1] // stages
    e = e2 // 2
    kv_half = stages * e
    for side in range(2):
        who = core if side == 0 else 1 - core
        kv_ref = kv0_ref if side == 0 else kv1_ref
        for b in range(nb):
            ts = slice(b * tok, (b + 1) * tok)
            for s in range(stages):
                lhs_ref[ts, pl.ds(pl.multiple_of(who * half + s * rows, rows), rows)] = q_refs[side * stages + s][0, b].T
            ks = jnp.concatenate([kv_ref[b, i * e2:i * e2 + e] for i in range(stages)], axis=0)
            vs = jnp.concatenate([kv_ref[b, i * e2 + e:(i + 1) * e2] for i in range(stages)], axis=0)
            base = 2 * half
            lhs_ref[ts, pl.ds(pl.multiple_of(base + who * kv_half, kv_half), kv_half)] = ks.T
            base = base + 2 * kv_half
            lhs_ref[ts, pl.ds(pl.multiple_of(base + who * kv_half, kv_half), kv_half)] = vs.T
    lhs = lhs_ref[...]
    step = 256
    for c in range(0, d, step):
        tot_ref[:, c:c + step] = dot(lhs, w_ref[c:c + step, :], NT)

    @pl.when(pl.program_id(0) == 0)
    def _():
        gn_ref[...] = jnp.zeros_like(gn_ref)

    g = g_ref[...].astype(F32)
    for b in range(nb):
        total = tot_ref[b * tok:(b + 1) * tok]
        x = x_ref[b].astype(F32)
        inv = lax.rsqrt(jnp.mean(x * x, axis=-1, keepdims=True) + NORM_EPS)
        unit = x * inv
        gu = total * g
        mean_dot = jnp.mean(gu * unit, axis=-1, keepdims=True)
        gh_ref[b] = (go_ref[b].astype(F32) + inv * (gu - unit * mean_dot)).astype(BF16)
        gn_ref[...] += jnp.sum((total * unit).reshape(tok // 8, 8, d), axis=0)


def transpose_to(out_ref, blk):
    for c in range(0, blk.shape[1], 256):
        out_ref[c:c + 256, :] = blk[:, c:c + 256].astype(F32).T


def assemble_main_kernel(*refs, stages, n_q):
    ins, (wq_ref, wo_ref) = refs[:stages], refs[stages:]
    for s in range(stages):
        @pl.when(pl.program_id(1) == s)
        def _(ref=ins[s]):
            chips, _, n, d = ref.shape
            transpose_to(wq_ref, ref[:, 0, 0:n_q].reshape(chips * n_q, d))
            wo_ref[...] = ref[:, 0, n_q:n].astype(F32)


def assemble_tail_kernel(in_ref, _, out_ref):
    chips, _, n, d = in_ref.shape
    transpose_to(out_ref, in_ref[:, 0].reshape(chips * n, d))


def solution(mesh):
    chips = mesh.shape['sp'] // CORES
    mesh2 = Mesh(mesh.devices.reshape(mesh.shape['dp'], chips, CORES), ('dp', 'x', 'core'))
    swap = [(i, CORES - 1 - i) for i in range(CORES)]

    def device_step(hidden, norm_w, w_qkv, w_out, long_factor, grad_out):
        n_batch, tok, d = hidden.shape
        n_heads, e = w_out.shape[0], w_out.shape[1]
        kv_heads = (w_qkv.shape[1] // e - n_heads) // 2
        reps = n_heads // kv_heads
        stages = kv_heads // CORES
        rows = reps * e
        q_half = stages * rows
        kv_half = stages * e
        e2 = 2 * e
        half_rot = long_factor.shape[0]
        chip = lax.axis_index('x')
        core = lax.axis_index('core')
        ids = jnp.stack([chip, core]).astype(jnp.int32)
        tiles = 2
        nb = n_batch // tiles

        x_par = lax.ppermute(hidden, 'core', swap)
        go_par = lax.ppermute(grad_out, 'core', swap)
        w_o = w_out.reshape(n_heads * e, d)
        norm2 = norm_w.reshape(1, d)

        exponent = jnp.arange(half_rot, dtype=F32) / half_rot
        inv_freq = 1.0 / (long_factor * jnp.power(ROPE_BASE, exponent))
        sides = jnp.stack([core, 1 - core])
        positions = ((chip * CORES + sides)[:, None] * tok + jnp.arange(tok)[None, :]).astype(F32)
        angles = inv_freq[None, :, None] * positions[:, None, :]
        cos_t, sin_t = jnp.cos(angles) * ROPE_GAIN, jnp.sin(angles) * ROPE_GAIN

        tok_spec = pl.BlockSpec((nb, tok, d), lambda i, _: (i, 0, 0))
        rot_spec = pl.BlockSpec((half_rot, tok), lambda i, _: (0, 0))

        def kv_proj(x, side):
            kb = 2 * q_half // kv_half
            return pl.pallas_call(
                drop_scalar(kv_proj_kernel),
                out_shape=(jax.ShapeDtypeStruct((n_batch, tok, d), BF16), jax.ShapeDtypeStruct((stages, n_batch, e2, tok), BF16)),
                grid_spec=pltpu.PrefetchScalarGridSpec(
                    num_scalar_prefetch=1, grid=(tiles,),
                    in_specs=[tok_spec, pl.BlockSpec((1, d), lambda i, _: (0, 0)),
                              pl.BlockSpec((d, kv_half), lambda i, c: (0, kb + c[1])),
                              pl.BlockSpec((d, kv_half), lambda i, c: (0, kb + CORES + c[1])), rot_spec, rot_spec],
                    out_specs=(tok_spec, pl.BlockSpec((stages, nb, e2, tok), lambda i, _: (0, i, 0, 0)))),
                compiler_params=params(), name='kv_proj',
                cost_estimate=cost(2 * n_batch * tok * d * 2 * kv_half, 3 * n_batch * tok * d * 2),
            )(ids, x, norm2, w_qkv, w_qkv, cos_t[side], sin_t[side])

        first = lambda i: jnp.minimum(i, tiles - 1)
        second = lambda i: jnp.maximum(i - tiles, 0)
        own_spec = pl.BlockSpec((nb, tok, d), lambda i, _: (first(i), 0, 0))
        par_spec = pl.BlockSpec((nb, tok, d), lambda i, _: (second(i), 0, 0))
        own_out = pl.BlockSpec((nb, q_half, tok), lambda i, _: (first(i), 0, 0))
        par_out = pl.BlockSpec((nb, q_half, tok), lambda i, _: (second(i), 0, 0))
        both_rot = pl.BlockSpec((2, half_rot, tok), lambda i, _: (0, 0, 0))
        q_shapes = (jax.ShapeDtypeStruct((n_batch, q_half, tok), BF16), jax.ShapeDtypeStruct((n_batch, q_half, tok), BF16))

        def q_proj(h0, h1):
            return pl.pallas_call(
                drop_scalar(q_proj_kernel), out_shape=q_shapes,
                grid_spec=pltpu.PrefetchScalarGridSpec(
                    num_scalar_prefetch=1, grid=(2 * tiles,),
                    in_specs=[own_spec, par_spec, pl.BlockSpec((d, q_half), lambda i, c: (0, c[1])), both_rot, both_rot],
                    out_specs=(own_out, par_out)),
                compiler_params=params(), name='q_proj',
                cost_estimate=cost(4 * n_batch * tok * d * q_half, 6 * n_batch * tok * d * 2),
            )(ids, h0, h1, w_qkv, cos_t, sin_t)

        def do_proj(g0, g1):
            return pl.pallas_call(
                drop_scalar(do_proj_kernel), out_shape=q_shapes,
                grid_spec=pltpu.PrefetchScalarGridSpec(
                    num_scalar_prefetch=1, grid=(2 * tiles,),
                    in_specs=[own_spec, par_spec, pl.BlockSpec((q_half, d), lambda i, c: (c[1], 0))],
                    out_specs=(own_out, par_out)),
                compiler_params=params(), name='do_proj',
                cost_estimate=cost(4 * n_batch * tok * d * q_half, 6 * n_batch * tok * d * 2),
            )(ids, g0, g1, w_o)

        h_own, kv_own = kv_proj(hidden, 0)
        h_par, kv_par = kv_proj(x_par, 1)
        gathered = []
        for s in range(stages):
            gathered.append(lax.all_gather(jnp.stack([kv_own[s], kv_par[s]]), 'x'))
        q_own, q_par = q_proj(h_own, h_par)
        do_own, do_par = do_proj(grad_out, go_par)

        def attention(s):
            blk = 2 * tok
            q_spec = pl.BlockSpec((1, rows, tok), lambda b, _: (b, s, 0))
            t_spec = pl.BlockSpec((2, tok, d), lambda b, _: (b // 2, 0, 0))
            r_spec = pl.BlockSpec((2, half_rot, tok), lambda b, _: (0, 0, 0))
            o_spec = pl.BlockSpec((2, 1, rows, tok), lambda b, _: (0, b, 0, 0))
            return pl.pallas_call(
                attn_kernel,
                out_shape=(jax.ShapeDtypeStruct((2, n_batch, rows, tok), BF16), jax.ShapeDtypeStruct((2, n_batch, rows, tok), BF16),
                           jax.ShapeDtypeStruct((chips, e2 + 2 * rows // chips, d), BF16)),
                grid_spec=pltpu.PrefetchScalarGridSpec(
                    num_scalar_prefetch=1, grid=(n_batch,),
                    in_specs=[q_spec, q_spec, q_spec, q_spec,
                              pl.BlockSpec((chips, 2, 1, e2, tok), lambda b, _: (0, 0, b, 0, 0)),
                              t_spec, t_spec, t_spec, t_spec, r_spec, r_spec],
                    out_specs=(o_spec, o_spec, pl.BlockSpec((chips, e2 + 2 * rows // chips, d), lambda b, _: (0, 0, 0))),
                    scratch_shapes=[pltpu.VMEM((chips, blk, reps * blk), F32), pltpu.VMEM((e, reps * blk), F32),
                                    pltpu.VMEM((chips, blk, e2), BF16), pltpu.VMEM((2, 2 * rows, blk), BF16),
                                    pltpu.VMEM((2 * rows, d), F32)]),
                compiler_params=params(),
                cost_estimate=cost(4e10, 3e7, 3e7),
            )(ids, q_own, q_par, do_own, do_par, gathered[s], h_own, h_par, grad_out, go_par, cos_t, sin_t)

        own, par, recv = [], [], []
        for s in range(stages):
            own_s, par_s, send_s = attention(s)
            own.append(own_s)
            par.append(lax.ppermute(par_s, 'core', swap))
            recv.append(lax.all_to_all(send_s, 'x', 0, 0, tiled=True))

        n_w = 2 * rows // chips
        shards = [jnp.sum(r[:, e2:].astype(F32), axis=0).astype(BF16) for r in recv]

        blk = 2 * tok
        kv_own_g, kv_par_g, send_kv = pl.pallas_call(
            functools.partial(kv_grad_kernel, stages=stages),
            out_shape=(jax.ShapeDtypeStruct((n_batch, stages * e2, tok), BF16), jax.ShapeDtypeStruct((n_batch, stages * e2, tok), BF16),
                       jax.ShapeDtypeStruct((chips, stages * e2 // chips, d), BF16)),
            grid=(n_batch,),
            in_specs=[pl.BlockSpec((chips, e2, blk), lambda b: (0, 0, b))] * stages
            + [pl.BlockSpec((1, tok, d), lambda b: (b, 0, 0))] * 2 + [pl.BlockSpec((2, half_rot, tok), lambda b: (0, 0, 0))] * 2,
            out_specs=(pl.BlockSpec((1, stages * e2, tok), lambda b: (b, 0, 0)), pl.BlockSpec((1, stages * e2, tok), lambda b: (b, 0, 0)),
                       pl.BlockSpec((chips, stages * e2 // chips, d), lambda b: (0, 0, 0))),
            scratch_shapes=[pltpu.VMEM((stages * e2, d), F32)],
            compiler_params=params(), name='kv_grad',
            cost_estimate=cost(2 * 2 * n_batch * tok * d * stages * e2, 3e7),
        )(*recv, h_own, h_par, cos_t, sin_t)
        kv_other_g = lax.ppermute(kv_par_g, 'core', swap)
        recv_kv = lax.all_to_all(send_kv, 'x', 0, 0, tiled=True)
        shard_kv = jnp.sum(recv_kv.astype(F32), axis=0).astype(BF16)

        nb2 = nb
        t2_spec = pl.BlockSpec((nb2, tok, d), lambda b, _: (b, 0, 0))
        block_out = pl.pallas_call(
            functools.partial(out_kernel, stages=stages),
            out_shape=jax.ShapeDtypeStruct((n_batch, tok, d), BF16),
            grid_spec=pltpu.PrefetchScalarGridSpec(
                num_scalar_prefetch=1, grid=(n_batch // nb2,),
                in_specs=[t2_spec, pl.BlockSpec((n_heads * e, d), lambda b, _: (0, 0))]
                + [pl.BlockSpec((1, nb2, rows, tok), lambda b, _: (0, b, 0, 0))] * (2 * stages),
                out_specs=t2_spec, scratch_shapes=[pltpu.VMEM((nb2 * tok, n_heads * e), BF16)]),
            compiler_params=params(), name='out_proj',
            cost_estimate=cost(2 * n_batch * tok * d * n_heads * e, 3e7),
        )(ids, hidden, w_o, *own, *par)

        grad_hidden, gn = pl.pallas_call(
            functools.partial(norm_grad_kernel, stages=stages),
            out_shape=(jax.ShapeDtypeStruct((n_batch, tok, d), BF16), jax.ShapeDtypeStruct((8, d), F32)),
            grid_spec=pltpu.PrefetchScalarGridSpec(
                num_scalar_prefetch=1, grid=(n_batch // nb2,),
                in_specs=[t2_spec, t2_spec, pl.BlockSpec((1, d), lambda b, _: (0, 0)),
                          pl.BlockSpec(w_qkv.shape, lambda b, _: (0, 0))]
                + [pl.BlockSpec((nb2, stages * e2, tok), lambda b, _: (b, 0, 0))] * 2
                + [pl.BlockSpec((1, nb2, rows, tok), lambda b, _: (1, b, 0, 0))] * (2 * stages),
                out_specs=(t2_spec, pl.BlockSpec((8, d), lambda b, _: (0, 0))),
                scratch_shapes=[pltpu.VMEM((nb2 * tok, w_qkv.shape[1]), BF16), pltpu.VMEM((nb2 * tok, d), F32)]),
            compiler_params=params(), name='norm_grad',
            cost_estimate=cost(2 * n_batch * tok * d * w_qkv.shape[1], 4e7),
        )(ids, hidden, grad_out, norm2, w_qkv, kv_own_g, kv_other_g, *own, *par)

        gn_row = jnp.sum(gn, axis=0, keepdims=True)
        gn_hi = gn_row.astype(BF16)
        gn_lo = (gn_row - gn_hi.astype(F32)).astype(BF16)
        pad = jnp.zeros((14, d), BF16)
        tail = lax.all_gather(jnp.concatenate([shard_kv, gn_hi, gn_lo, pad], axis=0), ('x', 'core'))
        tail = tail.reshape(chips, CORES, -1, d)
        n_kv = shard_kv.shape[0]
        n_q = rows // chips
        main = [lax.all_gather(s, ('x', 'core')).reshape(chips, CORES, n_w, d) for s in shards]
        w_cols, grad_w_out = pl.pallas_call(
            functools.partial(assemble_main_kernel, stages=stages, n_q=n_q),
            out_shape=(jax.ShapeDtypeStruct(w_qkv.shape, F32), jax.ShapeDtypeStruct((n_heads, e, d), F32)),
            grid=(CORES, stages),
            in_specs=[pl.BlockSpec((chips, 1, n_w, d), lambda p, s: (0, p, 0, 0))] * stages,
            out_specs=(pl.BlockSpec((d, rows), lambda p, s: (0, p * stages + s)),
                       pl.BlockSpec((reps, e, d), lambda p, s: (p * stages + s, 0, 0))),
            compiler_params=params(2), name='assemble_main', cost_estimate=cost(2e9, 6e7),
        )(*main)
        kcol = 2 * q_half // kv_half
        grad_w_qkv = pl.pallas_call(
            assemble_tail_kernel,
            out_shape=jax.ShapeDtypeStruct(w_qkv.shape, F32),
            grid=(CORES, 2),
            in_specs=[pl.BlockSpec((chips, 1, e, d), lambda p, k: (0, p, k, 0)), pl.BlockSpec(memory_space=pl.ANY)],
            out_specs=pl.BlockSpec((d, kv_half), lambda p, k: (0, kcol + k * CORES + p)),
            input_output_aliases={1: 0},
            compiler_params=params(2), name='assemble_tail', cost_estimate=cost(1e9, 2e7),
        )(tail, w_cols)
        gn_all = tail[:, :, n_kv:n_kv + 2].astype(F32)
        grad_norm_w = jnp.sum(gn_all, axis=(0, 1, 2))
        return block_out, grad_hidden, grad_w_qkv, grad_w_out, grad_norm_w

    tok_spec = P('dp', ('x', 'core'), None)
    return jax.shard_map(device_step, mesh=mesh2,
                         in_specs=(tok_spec, P(), P(), P(), P(), tok_spec),
                         out_specs=(tok_spec, tok_spec, P('dp', None), P('dp', None, None), P('dp')),
                         check_vma=False)
```

time: 818 us -> 639 us (0.78)
  local copies, waits for them, and re-layouts: 88.7 us -> 10.6 us
  blocking collectives: 306 us -> 252 us
  other arithmetic: 42.9 us -> 15.6 us
  starting transfers between devices: 65.3 us -> 46.8 us
    all_to_all x3, blocking collectives: 306 us -> 252 us  [device_step(): recv.append(lax.all_to_all(send_s, 'x', 0, 0, tiled=True))]
    unnamed x26 -> x10, local copies, waits for them, and re-layouts: 47.8 us -> 6.03 us
    pallas_call x4, Pallas kernels: 119 us -> 94.1 us  [attention(): pl.pallas_call(attn_kernel, out_shape=(jax.ShapeDtypeStruct((2, n_batch,...]
    transpose x2 -> x0, other arithmetic: 24.1 us -> none  [the longest x1 20.3 us: device_step(): grad_w_qkv = jnp.concatenate([q_cols, k_cols, v_cols], axis=0).astype(F32).T]
    pallas_call x4, Pallas kernels: 37.6 us -> 57 us  [the longest x1 19.6 us: device_step(): pl.pallas_call(functools.partial(assemble_main_kernel, stages=stages, n_q...]
    all_to_all x1, starting transfers between devices: 58.3 us -> 40.1 us  [device_step(): recv.append(lax.all_to_all(send_s, 'x', 0, 0, tiled=True))]
    another operation x4 -> x0, local copies, waits for them, and re-layouts: 18.1 us -> none  [device_step(): o_part = jnp.stack([m[:, :, n_q:] for m in main])]
    transpose x4 -> x0, local copies, waits for them, and re-layouts: 12 us -> none  [the longest x1 8.59 us: device_step(): q_cols = jnp.transpose(q_part, (2, 0, 1, 3, 4)).reshape(n_heads * e, d)]
  transfers between devices with their start and end apart: 18 -> 18, of which waited for: 2 -> 1; matrix products, arithmetic and copies ran while one was open for 9% -> 3% of each run, Pallas kernels for 27% -> 34%
where the time goes in v2:
time: 639 us; the launch traced here: 634 us
  blocking collectives  252 us (39%)
  Pallas kernels  229 us (36%)
  waiting for transfers between devices  65.6 us (10%)
  starting transfers between devices  46.8 us (7%)
  other arithmetic  15.6 us (2%)
  between operations  14.3 us (2%)
  local copies, waits for them, and re-layouts  10.6 us (2%)
    all_to_all x3, blocking collectives, device_step(): recv.append(lax.all_to_all(send_s, 'x', 0, 0, tiled=True))  252 us
    pallas_call x4, Pallas kernels, attention(): pl.pallas_call(attn_kernel, out_shape=(jax.ShapeDtypeStruct((2, n_batch,...  94.1 us
    all_to_all x1, waiting for transfers between devices, device_step(): recv.append(lax.all_to_all(send_s, 'x', 0, 0, tiled=True))  65 us
    all_to_all x1, starting transfers between devices, device_step(): recv.append(lax.all_to_all(send_s, 'x', 0, 0, tiled=True))  40.1 us
    pallas_call x1, Pallas kernels, device_step(): pl.pallas_call(functools.partial(norm_grad_kernel, stages=stages), out_sh...  31.3 us
    pallas_call x1, Pallas kernels, device_step(): pl.pallas_call(functools.partial(assemble_main_kernel, stages=stages, n_q...  19.6 us
    pallas_call x1, Pallas kernels, device_step(): pl.pallas_call(functools.partial(out_kernel, stages=stages), out_shape=ja...  17.9 us
    pallas_call x1, Pallas kernels, q_proj(): pl.pallas_call(drop_scalar(q_proj_kernel), out_shape=q_shapes, grid_spec=...  15.9 us
  transfers between devices with their start and end apart: 18, of which 1 were waited for; matrix products, arithmetic and copies ran while one was open for 3% of the time, Pallas kernels for 34%

profile of v2, /device:TPU:112, one launch (start us, length us, event | category | flops | bytes accessed | tf_op | source)
XLA Modules:
  0.0 633.7 jit_solution(16411036828292710701)
XLA Ops:
  11.0 7.5 %kv_proj.2 = (bf16[8,128,2048]{2,1,0:T(8,128)(2,1)}, bf16[4,8,128,128]{3,2,1,0:T(8,128)(2,1)}) custom-call(s32[2]{0:T(128)} %pad_add_fusion._.ids, bf16[8,128,2048]{2,1,0:T(8,128)(2,1)} %x_ref.3, bf16[1,2048]{1,0:T(2,128)(2,1)} %reshape.94.refs_1_.g_ref, bf16[2048,3072]{1,0:T(8,128)(2,1)} %w_ref.1, bf16[2048,3072]{1,0:T(8,128)(2,1)} %w_ref.1, ...), custom_call_target="tpu_custom_call" | custom-call | flops 2147483648 | bytes 12582912 | tf_op jit(solution)/shard_map/kv_proj/pallas_call | solution.py:414
  19.8 7.5 %kv_proj.3 = (bf16[8,128,2048]{2,1,0:T(8,128)(2,1)}, bf16[4,8,128,128]{3,2,1,0:T(8,128)(2,1)}) custom-call(s32[2]{0:T(128)} %pad_add_fusion._.ids, bf16[8,128,2048]{2,1,0:T(8,128)(2,1)} %collective-permute-done.refs_0_, bf16[1,2048]{1,0:T(2,128)(2,1)} %reshape.94.refs_1_.g_ref, bf16[2048,3072]{1,0:T(8,128)(2,1)} %w_ref.1, bf16[2048,3072]{1,0:T(8,128)(2,1)} %w_ref.1, ...), custom_call_target="tpu_custom_call" | custom-call | flops 2147483648 | bytes 12582912 | tf_op jit(solution)/shard_map/kv_proj/pallas_call | solution.py:414
  32.5 15.9 %q_proj.1 = (bf16[8,1024,128]{2,1,0:T(8,128)(2,1)}, bf16[8,1024,128]{2,1,0:T(8,128)(2,1)}) custom-call(s32[2]{0:T(128)} %pad_add_fusion._.ids, bf16[8,128,2048]{2,1,0:T(8,128)(2,1)} %get-tuple-element.32.refs_0_.h0_ref.refs_4_, bf16[8,128,2048]{2,1,0:T(8,128)(2,1)} %get-tuple-element.33.refs_1_.h1_ref.refs_5_, bf16[2048,3072]{1,0:T(8,128)(2,1)} %w_ref.1, ...), custom_call_target="tpu_custom_call" | custom-call | flops 8589934592 | bytes 25165824 | tf_op jit(solution)/shard_map/q_proj/pallas_call | solution.py:437
  48.4 15.2 %do_proj.1 = (bf16[8,1024,128]{2,1,0:T(8,128)(2,1)}, bf16[8,1024,128]{2,1,0:T(8,128)(2,1)}) custom-call(s32[2]{0:T(128)} %pad_add_fusion._.ids, bf16[8,128,2048]{2,1,0:T(8,128)(2,1)} %go_ref.1, bf16[8,128,2048]{2,1,0:T(8,128)(2,1)} %collective-permute-done.1.refs_1_.g1_ref, bf16[2048,2048]{1,0:T(8,128)(2,1)} %bitcast.30), custom_call_target="tpu_custom_call" | custom-call | flops 8589934592 | bytes 25165824 | tf_op jit(solution)/shard_map/do_proj/pallas_call | solution.py:448
  63.5 23.7 %shard_map.101 = (bf16[2,8,256,128]{3,2,1,0:T(8,128)(2,1)}, bf16[2,8,256,128]{3,2,1,0:T(8,128)(2,1)}, bf16[4,256,2048]{2,1,0:T(8,128)(2,1)}) custom-call(s32[2]{0:T(128)} %pad_add_fusion._.ids, bf16[8,1024,128]{2,1,0:T(8,128)(2,1)} %get-tuple-element.34.q0_ref, bf16[8,1024,128]{2,1,0:T(8,128)(2,1)} %get-tuple-element.35.q1_ref, ...), custom_call_target="tpu_custom_call" | custom-call | flops 40000000000 | bytes 30000000 | tf_op jit(solution)/shard_map/pallas_call | solution.py:472
  87.3 40.1 %all-to-all-start = ((bf16[4,256,2048]{2,1,0:T(8,128)(2,1)}), bf16[4,256,2048]{2,1,0:T(8,128)(2,1)}, u32[]{:S(2)}, u32[]{:S(2)}) async-start(bf16[4,256,2048]{2,1,0:T(8,128)(2,1)} %get-tuple-element.48), calls=%async_computation | async-start | bytes 8388608 | tf_op jit(solution)/shard_map/all_to_all | solution.py:494
  128.4 65.0 %all-to-all-done.refs_0_ = bf16[4,256,2048]{2,1,0:T(8,128)(2,1)} async-done(((bf16[4,256,2048]{2,1,0:T(8,128)(2,1)}), bf16[4,256,2048]{2,1,0:T(8,128)(2,1)}, u32[]{:S(2)}, u32[]{:S(2)}) %all-to-all-start) | async-done | bytes 4194336 | tf_op jit(solution)/shard_map/all_to_all | solution.py:494
  193.3 2.9 slice_reduce_fusion.3
  196.4 23.4 %shard_map.102 = (bf16[2,8,256,128]{3,2,1,0:T(8,128)(2,1)}, bf16[2,8,256,128]{3,2,1,0:T(8,128)(2,1)}, bf16[4,256,2048]{2,1,0:T(8,128)(2,1)}) custom-call(s32[2]{0:T(128)} %pad_add_fusion._.ids, bf16[8,1024,128]{2,1,0:T(8,128)(2,1)} %get-tuple-element.34.q0_ref, bf16[8,1024,128]{2,1,0:T(8,128)(2,1)} %get-tuple-element.35.q1_ref, ...), custom_call_target="tpu_custom_call" | custom-call | flops 40000000000 | bytes 30000000 | tf_op jit(solution)/shard_map/pallas_call | solution.py:472
  219.8 85.1 %all_to_all.25.refs_1_ = bf16[4,256,2048]{2,1,0:T(8,128)(2,1)S(1)} all-to-all(bf16[4,256,2048]{2,1,0:T(8,128)(2,1)} %get-tuple-element.49), channel_id=1, replica_groups=mesh['dp'=2,'x'=4,'core'=2] {'x'}, dimensions={0} | all-to-all | bytes 8388608 | tf_op jit(solution)/shard_map/all_to_all | solution.py:494
  304.9 2.0 copy-done
  308.3 23.6 %shard_map.103 = (bf16[2,8,256,128]{3,2,1,0:T(8,128)(2,1)}, bf16[2,8,256,128]{3,2,1,0:T(8,128)(2,1)}, bf16[4,256,2048]{2,1,0:T(8,128)(2,1)}) custom-call(s32[2]{0:T(128)} %pad_add_fusion._.ids, bf16[8,1024,128]{2,1,0:T(8,128)(2,1)} %get-tuple-element.34.q0_ref, bf16[8,1024,128]{2,1,0:T(8,128)(2,1)} %get-tuple-element.35.q1_ref, ...), custom_call_target="tpu_custom_call" | custom-call | flops 40000000000 | bytes 30000000 | tf_op jit(solution)/shard_map/pallas_call | solution.py:472
  331.9 83.9 %all_to_all.26.refs_2_ = bf16[4,256,2048]{2,1,0:T(8,128)(2,1)S(1)} all-to-all(bf16[4,256,2048]{2,1,0:T(8,128)(2,1)} %get-tuple-element.50), channel_id=1, replica_groups=mesh['dp'=2,'x'=4,'core'=2] {'x'}, dimensions={0} | all-to-all | bytes 8388608 | tf_op jit(solution)/shard_map/all_to_all | solution.py:494
  415.8 2.0 copy-done.1
  419.2 23.4 %shard_map.104 = (bf16[2,8,256,128]{3,2,1,0:T(8,128)(2,1)}, bf16[2,8,256,128]{3,2,1,0:T(8,128)(2,1)}, bf16[4,256,2048]{2,1,0:T(8,128)(2,1)}) custom-call(s32[2]{0:T(128)} %pad_add_fusion._.ids, bf16[8,1024,128]{2,1,0:T(8,128)(2,1)} %get-tuple-element.34.q0_ref, bf16[8,1024,128]{2,1,0:T(8,128)(2,1)} %get-tuple-element.35.q1_ref, ...), custom_call_target="tpu_custom_call" | custom-call | flops 40000000000 | bytes 30000000 | tf_op jit(solution)/shard_map/pallas_call | solution.py:472
  442.6 83.2 %all_to_all.27.refs_3_ = bf16[4,256,2048]{2,1,0:T(8,128)(2,1)S(1)} all-to-all(bf16[4,256,2048]{2,1,0:T(8,128)(2,1)} %get-tuple-element.51), channel_id=1, replica_groups=mesh['dp'=2,'x'=4,'core'=2] {'x'}, dimensions={0} | all-to-all | bytes 8388608 | tf_op jit(solution)/shard_map/all_to_all | solution.py:494
  525.8 2.0 copy-done.2
  530.2 13.4 %kv_grad.1 = (bf16[8,512,128]{2,1,0:T(8,128)(2,1)}, bf16[8,512,128]{2,1,0:T(8,128)(2,1)}, bf16[4,128,2048]{2,1,0:T(8,128)(2,1)}) custom-call(bf16[4,256,2048]{2,1,0:T(8,128)(2,1)} %all-to-all-done.refs_0_, bf16[4,256,2048]{2,1,0:T(8,128)(2,1)} %copy-done, bf16[4,256,2048]{2,1,0:T(8,128)(2,1)} %copy-done.1, bf16[4,256,2048]{2,1,0:T(8,128)(2,1)} %copy-done.2, ...), custom_call_target="tpu_custom_call" | custom-call | flops 4294967296 | bytes 30000000 | tf_op jit(solution)/shard_map/kv_grad/pallas_call | solution.py:500
  543.9 3.7 all-to-all-start.4
  547.7 31.3 %norm_grad.1 = (bf16[8,128,2048]{2,1,0:T(8,128)(2,1)}, f32[8,2048]{1,0:T(8,128)}) custom-call(s32[2]{0:T(128)} %pad_add_fusion._.ids, bf16[8,128,2048]{2,1,0:T(8,128)(2,1)} %x_ref.3, bf16[8,128,2048]{2,1,0:T(8,128)(2,1)} %go_ref.1, bf16[1,2048]{1,0:T(2,128)(2,1)} %reshape.94.refs_1_.g_ref, bf16[2048,3072]{1,0:T(8,128)(2,1)} %w_ref.1, ...), custom_call_target="tpu_custom_call" | custom-call | flops 12884901888 | bytes 40000000 | tf_op jit(solution)/shard_map/norm_grad/pallas_call | solution.py:531
  581.4 17.9 %out_proj.1 = bf16[8,128,2048]{2,1,0:T(8,128)(2,1)} custom-call(s32[2]{0:T(128)} %pad_add_fusion._.ids, bf16[8,128,2048]{2,1,0:T(8,128)(2,1)} %x_ref.3, bf16[2048,2048]{1,0:T(8,128)(2,1)} %bitcast.31, bf16[2,8,256,128]{3,2,1,0:T(8,128)(2,1)} %get-tuple-element.40.refs_0_, bf16[2,8,256,128]{3,2,1,0:T(8,128)(2,1)} %get-tuple-element.41.refs_1_, ...), custom_call_target="tpu_custom_call" | custom-call | flops 8589934592 | bytes 30000000 | tf_op jit(solution)/shard_map/out_proj/pallas_call | solution.py:519
  599.4 19.6 %assemble_main.1 = (f32[2048,3072]{1,0:T(8,128)}, f32[32,64,2048]{2,1,0:T(8,128)}) custom-call(bf16[4,2,128,2048]{3,2,1,0:T(8,128)(2,1)} %bitcast.24, bf16[4,2,128,2048]{3,2,1,0:T(8,128)(2,1)} %bitcast.25, bf16[4,2,128,2048]{3,2,1,0:T(8,128)(2,1)} %bitcast.26, bf16[4,2,128,2048]{3,2,1,0:T(8,128)(2,1)} %bitcast.27), custom_call_target="tpu_custom_call" | custom-call | flops 2000000000 | bytes 60000000 | tf_op jit(solution)/shard_map/assemble_main/pallas_call | solution.py:555
  619.0 1.6 convert_reduce_fusion
  620.6 6.4 %assemble_tail.1 = f32[2048,3072]{1,0:T(8,128)} custom-call(bf16[4,2,144,2048]{3,2,1,0:T(8,128)(2,1)} %bitcast.23, f32[2048,3072]{1,0:T(8,128)} %get-tuple-element.57._), custom_call_target="tpu_custom_call", output_to_operand_aliasing={{}: (1, {})} | custom-call | flops 1000000000 | bytes 20000000 | tf_op jit(solution)/shard_map/assemble_tail/pallas_call | solution.py:565
  (72 shorter events, 19.2 us)
Async XLA Ops:
  7.2 56.4 %all-gather.19.cloned.1.call-start = ((), (), s32[]{:S(2)}) async-start(), calls=%async_computation.5 | async-start | bytes 2621440 | tf_op jit(solution)/shard_map/all_gather | solution.py:462
  7.2 12.5 %collective-permute-start = (bf16[8,128,2048]{2,1,0:T(8,128)(2,1)}, bf16[8,128,2048]{2,1,0:T(8,128)(2,1)}, u32[]{:S(2)}, u32[]{:S(2)}) collective-permute-start(bf16[8,128,2048]{2,1,0:T(8,128)(2,1)} %x_ref.3), channel_id=1, source_target_pairs={{0,1},{1,0},{2,3},{3,2},{4,5},{5,4},{6,7},{7,6},{8,9},{9,8},{10,11... | collective-permute-start | bytes 12582920 | tf_op jit(solution)/shard_map/ppermute | solution.py:397
  10.3 8.2 %copy-start.3 = (f32[2,32,128]{2,1,0:T(8,128)}, f32[2,32,128]{2,1,0:T(8,128)S(1)}, u32[]{:S(2)}) copy-start(f32[2,32,128]{2,1,0:T(8,128)S(1)} %get-tuple-element.71.refs_4_.sin_ref.refs_7_) | copy-start | bytes 98308
  10.3 8.1 %copy-start.4 = (f32[2,32,128]{2,1,0:T(8,128)}, f32[2,32,128]{2,1,0:T(8,128)S(1)}, u32[]{:S(2)}) copy-start(f32[2,32,128]{2,1,0:T(8,128)S(1)} %get-tuple-element.72.refs_3_.cos_ref.refs_6_) | copy-start | bytes 98308
  29.4 167.0 %all-gather.21.cloned.1.call-start = ((), (), s32[]{:S(2)}) async-start(), calls=%async_computation.6 | async-start | bytes 2621440 | tf_op jit(solution)/shard_map/all_gather | solution.py:462
  29.5 18.9 %collective-permute-start.1 = (bf16[8,128,2048]{2,1,0:T(8,128)(2,1)}, bf16[8,128,2048]{2,1,0:T(8,128)(2,1)}, u32[]{:S(2)}, u32[]{:S(2)}) collective-permute-start(bf16[8,128,2048]{2,1,0:T(8,128)(2,1)} %go_ref.1), channel_id=1, source_target_pairs={{0,1},{1,0},{2,3},{3,2},{4,5},{5,4},{6,7},{7,6},{8,9},{9,8},{10,11... | collective-permute-start | bytes 12582920 | tf_op jit(solution)/shard_map/ppermute | solution.py:398
  31.0 277.3 %all-gather.23.cloned.1.call-start = ((), (), s32[]{:S(2)}) async-start(), calls=%async_computation.7 | async-start | bytes 2621440 | tf_op jit(solution)/shard_map/all_gather | solution.py:462
  87.3 106.1 %all-to-all-start = ((bf16[4,256,2048]{2,1,0:T(8,128)(2,1)}), bf16[4,256,2048]{2,1,0:T(8,128)(2,1)}, u32[]{:S(2)}, u32[]{:S(2)}) async-start(bf16[4,256,2048]{2,1,0:T(8,128)(2,1)} %get-tuple-element.48), calls=%async_computation | async-start | bytes 8388608 | tf_op jit(solution)/shard_map/all_to_all | solution.py:494
  127.4 291.8 %all-gather.25.cloned.1.call-start = ((), (), s32[]{:S(2)}) async-start(), calls=%async_computation.8 | async-start | bytes 2621440 | tf_op jit(solution)/shard_map/all_gather | solution.py:462
  128.3 471.0 %all-gather.29.cloned.1.call-start = ((), (), s32[]{:S(2)}) async-start(), calls=%async_computation.10 | async-start | bytes 4718592 | tf_op jit(solution)/shard_map/all_gather | solution.py:554
  196.3 403.0 %all-gather.31.cloned.1.call-start = ((), (), s32[]{:S(2)}) async-start(), calls=%async_computation.11 | async-start | bytes 4718592 | tf_op jit(solution)/shard_map/all_gather | solution.py:554
  304.9 2.0 copy-start
  308.2 291.2 %all-gather.33.cloned.1.call-start = ((), (), s32[]{:S(2)}) async-start(), calls=%async_computation.12 | async-start | bytes 4718592 | tf_op jit(solution)/shard_map/all_gather | solution.py:554
  415.8 2.0 copy-start.1
  419.1 180.3 %all-gather.35.cloned.1.call-start = ((), (), s32[]{:S(2)}) async-start(), calls=%async_computation.13 | async-start | bytes 4718592 | tf_op jit(solution)/shard_map/all_gather | solution.py:554
  525.8 2.0 copy-start.2
  529.1 18.6 %collective-permute-start.2 = (bf16[2,8,256,128]{3,2,1,0:T(8,128)(2,1)}, bf16[2,8,256,128]{3,2,1,0:T(8,128)(2,1)}, u32[]{:S(2)}, u32[]{:S(2)}) collective-permute-start(bf16[2,8,256,128]{3,2,1,0:T(8,128)(2,1)} %get-tuple-element.44), channel_id=1, source_target_pairs={{0,1},{1,0},{2,3},{3,2},{4,5},{5,4},{6,7},{7,6},{8,9},{9,8},{10,11... | collective-permute-start | bytes 3145736 | tf_op jit(solution)/shard_map/ppermute | solution.py:493
  529.2 18.5 %collective-permute-start.3 = (bf16[2,8,256,128]{3,2,1,0:T(8,128)(2,1)}, bf16[2,8,256,128]{3,2,1,0:T(8,128)(2,1)}, u32[]{:S(2)}, u32[]{:S(2)}) collective-permute-start(bf16[2,8,256,128]{3,2,1,0:T(8,128)(2,1)} %get-tuple-element.45), channel_id=1, source_target_pairs={{0,1},{1,0},{2,3},{3,2},{4,5},{5,4},{6,7},{7,6},{8,9},{9,8},{10,11... | collective-permute-start | bytes 3145736 | tf_op jit(solution)/shard_map/ppermute | solution.py:493
  529.7 18.0 %collective-permute-start.4 = (bf16[2,8,256,128]{3,2,1,0:T(8,128)(2,1)}, bf16[2,8,256,128]{3,2,1,0:T(8,128)(2,1)}, u32[]{:S(2)}, u32[]{:S(2)}) collective-permute-start(bf16[2,8,256,128]{3,2,1,0:T(8,128)(2,1)} %get-tuple-element.46), channel_id=1, source_target_pairs={{0,1},{1,0},{2,3},{3,2},{4,5},{5,4},{6,7},{7,6},{8,9},{9,8},{10,11... | collective-permute-start | bytes 3145736 | tf_op jit(solution)/shard_map/ppermute | solution.py:493
  529.8 17.9 %collective-permute-start.5 = (bf16[2,8,256,128]{3,2,1,0:T(8,128)(2,1)}, bf16[2,8,256,128]{3,2,1,0:T(8,128)(2,1)}, u32[]{:S(2)}, u32[]{:S(2)}) collective-permute-start(bf16[2,8,256,128]{3,2,1,0:T(8,128)(2,1)} %get-tuple-element.47), channel_id=1, source_target_pairs={{0,1},{1,0},{2,3},{3,2},{4,5},{5,4},{6,7},{7,6},{8,9},{9,8},{10,11... | collective-permute-start | bytes 3145736 | tf_op jit(solution)/shard_map/ppermute | solution.py:493
  543.6 4.1 collective-permute-start.6
  543.9 36.1 %all-to-all-start.4 = ((bf16[4,128,2048]{2,1,0:T(8,128)(2,1)}), bf16[4,128,2048]{2,1,0:T(8,128)(2,1)S(1)}, u32[]{:S(2)}, u32[]{:S(2)}) async-start(bf16[4,128,2048]{2,1,0:T(8,128)(2,1)} %get-tuple-element.55), calls=%async_computation.4 | async-start | bytes 4194304 | tf_op jit(solution)/shard_map/all_to_all | solution.py:514
  547.6 71.4 %all-gather.27.cloned.1.call-start = ((), (), s32[]{:S(2)}) async-start(), calls=%async_computation.9 | async-start | bytes 5308416 | tf_op jit(solution)/shard_map/all_gather | solution.py:550
Sparse Core Ops, SparseCore 0:
  29.6 29.6 all-gather.18
  61.4 26.6 all-gather.20
  89.7 26.6 all-gather.22
  129.4 64.7 all-gather.24
  196.4 28.4 all-gather.28
  308.3 28.0 all-gather.30
  419.2 28.0 all-gather.32
  529.2 31.8 all-gather.34
  581.5 32.3 all-gather.26

commit v3 on v2

--- a/solution.py
+++ b/solution.py
@@ -42,9 +42,11 @@
     return jnp.concatenate([a * cos - b * s, b * cos + a * s], axis=0)
 
 
-def kv_proj_kernel(x_ref, g_ref, wk_ref, wv_ref, cos_ref, sin_ref, h_ref, kv_ref):
+def kv_proj_kernel(x_ref, g_ref, wk_ref, wv_ref, cos_ref, sin_ref, *refs):
     nb, tok, d = x_ref.shape
-    kvh, _, e2, _ = kv_ref.shape
+    stages = (wk_ref.shape[1] // (2 * cos_ref.shape[0]))
+    h_ref, kv_refs = refs[-stages - 1], refs[-stages:]
+    e2 = kv_refs[0].shape[2]
     e = e2 // 2
     x = x_ref[...].reshape(nb * tok, d).astype(F32)
     inv = lax.rsqrt(jnp.mean(x * x, axis=-1, keepdims=True) + NORM_EPS)
@@ -52,13 +54,11 @@
     h_ref[...] = h.reshape(nb, tok, d)
     cos, sin = cos_ref[...], sin_ref[...]
     k = dot(h, wk_ref[...]).T
-    for i in range(kvh):
+    v = dot(h, wv_ref[...]).T
+    for i in range(stages):
         for b in range(nb):
-            kv_ref[i, b, 0:e] = rope_rows(k[i * e:(i + 1) * e, b * tok:(b + 1) * tok], cos, sin, 1.0).astype(BF16)
-    v = dot(h, wv_ref[...]).T
-    for i in range(kvh):
-        for b in range(nb):
-            kv_ref[i, b, e:2 * e] = v[i * e:(i + 1) * e, b * tok:(b + 1) * tok].astype(BF16)
+            kv_refs[i][0, b, 0:e] = rope_rows(k[i * e:(i + 1) * e, b * tok:(b + 1) * tok], cos, sin, 1.0).astype(BF16)
+            kv_refs[i][0, b, e:2 * e] = v[i * e:(i + 1) * e, b * tok:(b + 1) * tok].astype(BF16)
 
 
 def q_proj_kernel(h0_ref, h1_ref, w_ref, cos_ref, sin_ref, q0_ref, q1_ref):
@@ -86,7 +86,7 @@
 def do_proj_kernel(g0_ref, g1_ref, w_ref, o0_ref, o1_ref):
     nb, tok, d = g0_ref.shape
     rows = w_ref.shape[0]
-    step = 256
+    step = 512
 
     def run(g_ref, o_ref):
         g = g_ref[...].reshape(nb * tok, d)
@@ -108,7 +108,9 @@
 
 
 def attn_kernel(ids, q0_ref, q1_ref, do0_ref, do1_ref, kv_ref, h0_ref, h1_ref, g0_ref, g1_ref, cos_ref, sin_ref,
-                own_ref, par_ref, send_ref, s_ref, acc_ref, kvt_ref, lhs_ref, gacc_ref):
+                own_ref, par_ref, *refs):
+    sends, (s_ref, p_ref, ds_ref, acc_ref, ml_ref, kvt_ref, lhs_ref, gacc_ref) = refs[:-8], refs[-8:]
+    send_ref, g_send_ref = sends[0], sends[-1]
     chip, core = ids[0], ids[1]
     b_id = pl.program_id(0)
     chips = kv_ref.shape[0]
@@ -121,88 +123,96 @@
         full = jnp.concatenate([first_ref[0], second_ref[0]], axis=1)
         return jnp.concatenate([full[i * e:(i + 1) * e] for i in range(reps)], axis=1)
 
-    qt = heads_to_lanes(q0_ref, q1_ref)
-    dot_t = heads_to_lanes(do0_ref, do1_ref)
-    zero = jnp.zeros_like(qt)
-    q_pad = jnp.concatenate([qt, zero], axis=0)
-    do_pad = jnp.concatenate([zero, dot_t], axis=0)
     head_cols = [slice(i * blk, (i + 1) * blk) for i in range(reps)]
 
-    def kv_block(j):
-        return jnp.concatenate([kv_ref[j, 0, 0], kv_ref[j, 1, 0]], axis=1)
-
-    def scores(j, masked):
-        kvt = kv_block(j).T
-        kvt_ref[j] = kvt
+    def kv_block(i):
+        return jnp.concatenate([kv_ref[chip - i, 0, 0], kv_ref[chip - i, 1, 0]], axis=1)
+
+    def scores(i):
+        qt = heads_to_lanes(q0_ref, q1_ref)
+        q_pad = jnp.concatenate([qt, jnp.zeros_like(qt)], axis=0)
+        kvt = kv_block(i).T
+        kvt_ref[i] = kvt
         tops = []
         for cols in head_cols:
             t = dot(kvt, q_pad[:, cols])
-            if masked:
+            if i == 0:
                 r = lax.broadcasted_iota(jnp.int32, (blk, blk), 0)
                 c = lax.broadcasted_iota(jnp.int32, (blk, blk), 1)
                 shift = (1 - 2 * core) * tok
                 k_pos = jnp.where(r < tok, r, r - tok + shift)
                 q_pos = jnp.where(c < tok, c, c - tok + shift)
                 t = jnp.where(k_pos <= q_pos, t, MASK_VALUE)
-            s_ref[j, :, cols] = t
+            s_ref[i, :, cols] = t
             tops.append(jnp.max(t, axis=0, keepdims=True))
         return jnp.concatenate(tops, axis=1) * LOG2E
 
-    def accumulate(j, m):
-        v_t = kv_block(j)[e:2 * e]
+    def accumulate(i, m):
+        v_t = kv_block(i)[e:2 * e]
         sums, outs = [], []
         for cols in head_cols:
-            p = jnp.exp2(s_ref[j, :, cols] * LOG2E - m[:, cols])
+            p = jnp.exp2(s_ref[i, :, cols] * LOG2E - m[:, cols])
             sums.append(jnp.sum(p, axis=0, keepdims=True))
             outs.append(dot(v_t, p.astype(BF16)))
         return jnp.concatenate(sums, axis=1), jnp.concatenate(outs, axis=1)
 
+    ml_ref[0:1] = scores(0)
+    ml_ref[1:2] = jnp.zeros_like(ml_ref[1:2])
     acc_ref[...] = jnp.zeros_like(acc_ref)
-    m = scores(chip, True)
-
-    def forward_step(j, carry):
-        m, l = carry
-        prev = jnp.where(j == 0, chip, j - 1)
-        add_l, add_o = accumulate(prev, m)
-        m_new = jnp.maximum(m, scores(j, False))
-        alpha = jnp.exp2(m - m_new)
-        acc_ref[...] = (acc_ref[...] + add_o) * alpha
-        return m_new, (l + add_l) * alpha
-
-    m, l = lax.fori_loop(0, chip, forward_step, (m, jnp.zeros_like(m)))
-    add_l, add_o = accumulate(jnp.where(chip == 0, chip, chip - 1), m)
-    l = l + add_l
-
+
+    for i in range(1, chips):
+        @pl.when(i <= chip)
+        def _(i=i):
+            m = ml_ref[0:1]
+            add_l, add_o = accumulate(i - 1, m)
+            m_new = jnp.maximum(m, scores(i))
+            alpha = jnp.exp2(m - m_new)
+            acc_ref[...] = (acc_ref[...] + add_o) * alpha
+            ml_ref[1:2] = (ml_ref[1:2] + add_l) * alpha
+            ml_ref[0:1] = m_new
+
+    m = ml_ref[0:1]
+    add_l, add_o = accumulate(chip, m)
+    l = ml_ref[1:2] + add_l
     o_t = (acc_ref[...] + add_o) * (1.0 / l)
-    delta = jnp.sum(o_t * dot_t.astype(F32), axis=0, keepdims=True)
-    lse = m + jnp.log2(l)
+    dot_t = heads_to_lanes(do0_ref, do1_ref)
+    ml_ref[1:2] = jnp.sum(o_t * dot_t.astype(F32), axis=0, keepdims=True)
+    ml_ref[0:1] = m + jnp.log2(l)
     o_b = o_t.astype(BF16)
-
-    def backward_block(j, first):
-        kvt = kvt_ref[j]
-        k_t = kv_block(j)[0:e]
-        dk = jnp.zeros((e, blk), F32)
-        dv = jnp.zeros((e, blk), F32)
+    o_full = jnp.concatenate([o_b[:, cols] for cols in head_cols], axis=0)
+    odd = lax.rem(b_id, 2)
+    lhs_ref[odd, rows:2 * rows] = o_full
+    own_ref[0, 0] = o_full[:, :tok]
+    par_ref[0, 0] = o_full[:, tok:]
+    acc_ref[...] = jnp.zeros_like(acc_ref)
+
+    def score_grads(i):
+        dot_t = heads_to_lanes(do0_ref, do1_ref)
+        do_pad = jnp.concatenate([jnp.zeros_like(dot_t), dot_t], axis=0)
+        kvt = kvt_ref[i]
         for cols in head_cols:
-            p = jnp.exp2(s_ref[j, :, cols] * LOG2E - lse[:, cols])
+            p = jnp.exp2(s_ref[i, :, cols] * LOG2E - ml_ref[0:1, cols])
             dp = dot(kvt, do_pad[:, cols])
-            ds = (p * (dp - delta[:, cols])).astype(BF16)
-            dv = dv + dot(dot_t[:, cols], p.astype(BF16), NT)
-            dk = dk + dot(qt[:, cols], ds, NT)
-            dq = dot(k_t, ds)
-            if first:
-                acc_ref[:, cols] = dq
-            else:
-                acc_ref[:, cols] = acc_ref[:, cols] + dq
-        send_ref[j, 0:2 * e, pl.ds(pl.multiple_of(b_id * blk, blk), blk)] = jnp.concatenate([dk, dv], axis=0).astype(BF16)
-
-    backward_block(chip, True)
-
-    def backward_step(j, carry):
-        backward_block(j, False)
-        return carry
-
-    lax.fori_loop(0, chip, backward_step, 0)
+            p_ref[i, :, cols] = p.astype(BF16)
+            ds_ref[i, :, cols] = (p * (dp - ml_ref[1:2, cols])).astype(BF16)
+
+    def input_grads(i):
+        qt = heads_to_lanes(q0_ref, q1_ref)
+        dot_t = heads_to_lanes(do0_ref, do1_ref)
+        k_t = kv_block(i)[0:e]
+        dv = dot(dot_t, p_ref[i], NT)
+        dk = dot(qt, ds_ref[i], NT)
+        send_ref[chip - i, 0:2 * e, pl.ds(pl.multiple_of(b_id * blk, blk), blk)] = jnp.concatenate([dk, dv], axis=0).astype(BF16)
+        acc_ref[...] += dot(k_t, ds_ref[i])
+
+    score_grads(0)
+    for i in range(1, chips):
+        @pl.when(i <= chip)
+        def _(i=i):
+            input_grads(i - 1)
+            score_grads(i)
+
+    input_grads(chip)
 
     def zero_step(j, carry):
         send_ref[j, 0:2 * e, pl.ds(pl.multiple_of(b_id * blk, blk), blk)] = jnp.zeros((2 * e, blk), BF16)
@@ -216,18 +226,13 @@
     for cols in head_cols:
         dq = (acc_ref[:, cols] * (e ** -0.5)).astype(BF16).astype(F32)
         dq_rows.append(rope_rows(dq, cos, sin, -1.0).astype(BF16))
-    o_full = jnp.concatenate([o_b[:, cols] for cols in head_cols], axis=0)
     dq_full = jnp.concatenate(dq_rows, axis=0)
-    own_ref[0, 0] = o_full[:, :tok]
-    par_ref[0, 0] = o_full[:, tok:]
     own_ref[1, 0] = dq_full[:, :tok]
     par_ref[1, 0] = dq_full[:, tok:]
 
     d = h0_ref.shape[2]
     step = 512
-    odd = lax.rem(b_id, 2)
     lhs_ref[odd, 0:rows] = dq_full
-    lhs_ref[odd, rows:2 * rows] = o_full
 
     def weight_grads(first):
         for c in range(0, d, step):
@@ -248,19 +253,19 @@
     def _():
         for j in range(chips):
             n = rows // chips
-            send_ref[j, 2 * e:2 * e + n] = gacc_ref[j * n:(j + 1) * n].astype(BF16)
-            send_ref[j, 2 * e + n:2 * e + 2 * n] = gacc_ref[rows + j * n:rows + (j + 1) * n].astype(BF16)
+            base = 2 * e if len(sends) == 1 else 0
+            g_send_ref[j, base:base + n] = gacc_ref[j * n:(j + 1) * n].astype(BF16)
+            g_send_ref[j, base + n:base + 2 * n] = gacc_ref[rows + j * n:rows + (j + 1) * n].astype(BF16)
 
 
 def kv_grad_kernel(*refs, stages):
     recv = refs[:stages]
     h0_ref, h1_ref, cos_ref, sin_ref, own_ref, par_ref, send_ref, gacc_ref = refs[stages:]
-    b_id = pl.program_id(0)
-    tok = h0_ref.shape[1]
+    nb, tok, d = h0_ref.shape
     e2 = own_ref.shape[1] // stages
     e = e2 // 2
-    cos = jnp.concatenate([cos_ref[0], cos_ref[1]], axis=1)
-    sin = jnp.concatenate([sin_ref[0], sin_ref[1]], axis=1)
+    side = jnp.concatenate([cos_ref[0], cos_ref[1]], axis=1), jnp.concatenate([sin_ref[0], sin_ref[1]], axis=1)
+    cos, sin = (jnp.concatenate([t] * nb, axis=1) for t in side)
     parts = []
     for r in recv:
         total = r[0].astype(F32)
@@ -269,21 +274,24 @@
         total = total.astype(BF16).astype(F32)
         parts.append(jnp.concatenate([rope_rows(total[0:e], cos, sin, -1.0), total[e:2 * e]], axis=0).astype(BF16))
     gf = jnp.concatenate(parts, axis=0)
-    own_ref[0] = gf[:, :tok]
-    par_ref[0] = gf[:, tok:]
-
-    @pl.when(b_id == 0)
-    def _():
-        gacc_ref[...] = jnp.zeros_like(gacc_ref)
-
-    d = h0_ref.shape[2]
-    step = 512
-    for c in range(0, d, step):
-        cs = slice(c, c + step)
-        hh = jnp.concatenate([h0_ref[0, :, cs], h1_ref[0, :, cs]], axis=0)
-        gacc_ref[:, cs] += dot(gf, hh)
-
-    @pl.when(b_id == pl.num_programs(0) - 1)
+    for b in range(nb):
+        own_ref[b] = gf[:, 2 * b * tok:(2 * b + 1) * tok]
+        par_ref[b] = gf[:, (2 * b + 1) * tok:(2 * b + 2) * tok]
+
+    def weight_grads(first):
+        step = 512
+        for c in range(0, d, step):
+            cs = slice(c, c + step)
+            hh = jnp.concatenate([r[b, :, cs] for b in range(nb) for r in (h0_ref, h1_ref)], axis=0)
+            if first:
+                gacc_ref[:, cs] = dot(gf, hh)
+            else:
+                gacc_ref[:, cs] += dot(gf, hh)
+
+    pl.when(pl.program_id(0) == 0)(lambda: weight_grads(True))
+    pl.when(pl.program_id(0) > 0)(lambda: weight_grads(False))
+
+    @pl.when(pl.program_id(0) == pl.num_programs(0) - 1)
     def _():
         n = send_ref.shape[1]
         for j in range(send_ref.shape[0]):
@@ -409,20 +417,27 @@
         tok_spec = pl.BlockSpec((nb, tok, d), lambda i, _: (i, 0, 0))
         rot_spec = pl.BlockSpec((half_rot, tok), lambda i, _: (0, 0))
 
-        def kv_proj(x, side):
+        def kv_proj(x, side, filled):
             kb = 2 * q_half // kv_half
+            kt = 4
+            kn = n_batch // kt
+            x_spec = pl.BlockSpec((kn, tok, d), lambda i, _: (i, 0, 0))
+            any_spec = pl.BlockSpec(memory_space=pl.ANY)
             return pl.pallas_call(
                 drop_scalar(kv_proj_kernel),
-                out_shape=(jax.ShapeDtypeStruct((n_batch, tok, d), BF16), jax.ShapeDtypeStruct((stages, n_batch, e2, tok), BF16)),
+                out_shape=[jax.ShapeDtypeStruct((n_batch, tok, d), BF16)]
+                + [jax.ShapeDtypeStruct((2, n_batch, e2, tok), BF16)] * stages,
                 grid_spec=pltpu.PrefetchScalarGridSpec(
-                    num_scalar_prefetch=1, grid=(tiles,),
-                    in_specs=[tok_spec, pl.BlockSpec((1, d), lambda i, _: (0, 0)),
+                    num_scalar_prefetch=1, grid=(kt,),
+                    in_specs=[x_spec, pl.BlockSpec((1, d), lambda i, _: (0, 0)),
                               pl.BlockSpec((d, kv_half), lambda i, c: (0, kb + c[1])),
-                              pl.BlockSpec((d, kv_half), lambda i, c: (0, kb + CORES + c[1])), rot_spec, rot_spec],
-                    out_specs=(tok_spec, pl.BlockSpec((stages, nb, e2, tok), lambda i, _: (0, i, 0, 0)))),
+                              pl.BlockSpec((d, kv_half), lambda i, c: (0, kb + CORES + c[1])), rot_spec, rot_spec]
+                    + [any_spec] * len(filled),
+                    out_specs=[x_spec] + [pl.BlockSpec((1, kn, e2, tok), lambda i, _: (side, i, 0, 0))] * stages),
+                input_output_aliases={7 + i: 1 + i for i in range(len(filled))},
                 compiler_params=params(), name='kv_proj',
                 cost_estimate=cost(2 * n_batch * tok * d * 2 * kv_half, 3 * n_batch * tok * d * 2),
-            )(ids, x, norm2, w_qkv, w_qkv, cos_t[side], sin_t[side])
+            )(ids, x, norm2, w_qkv, w_qkv, cos_t[side], sin_t[side], *filled)
 
         first = lambda i: jnp.minimum(i, tiles - 1)
         second = lambda i: jnp.maximum(i - tiles, 0)
@@ -455,31 +470,35 @@
                 cost_estimate=cost(4 * n_batch * tok * d * q_half, 6 * n_batch * tok * d * 2),
             )(ids, g0, g1, w_o)
 
-        h_own, kv_own = kv_proj(hidden, 0)
-        h_par, kv_par = kv_proj(x_par, 1)
+        h_own, *kv_sides = kv_proj(hidden, 0, [])
+        h_par, *kv_sides = kv_proj(x_par, 1, kv_sides)
         gathered = []
         for s in range(stages):
-            gathered.append(lax.all_gather(jnp.stack([kv_own[s], kv_par[s]]), 'x'))
+            gathered.append(lax.all_gather(kv_sides[s], 'x'))
         q_own, q_par = q_proj(h_own, h_par)
         do_own, do_par = do_proj(grad_out, go_par)
 
         def attention(s):
             blk = 2 * tok
+            n_g = 2 * rows // chips
+            parts = [e2, n_g] if s == stages - 1 else [e2 + n_g]
             q_spec = pl.BlockSpec((1, rows, tok), lambda b, _: (b, s, 0))
             t_spec = pl.BlockSpec((2, tok, d), lambda b, _: (b // 2, 0, 0))
             r_spec = pl.BlockSpec((2, half_rot, tok), lambda b, _: (0, 0, 0))
             o_spec = pl.BlockSpec((2, 1, rows, tok), lambda b, _: (0, b, 0, 0))
             return pl.pallas_call(
                 attn_kernel,
-                out_shape=(jax.ShapeDtypeStruct((2, n_batch, rows, tok), BF16), jax.ShapeDtypeStruct((2, n_batch, rows, tok), BF16),
-                           jax.ShapeDtypeStruct((chips, e2 + 2 * rows // chips, d), BF16)),
+                out_shape=[jax.ShapeDtypeStruct((2, n_batch, rows, tok), BF16)] * 2
+                + [jax.ShapeDtypeStruct((chips, n, d), BF16) for n in parts],
                 grid_spec=pltpu.PrefetchScalarGridSpec(
                     num_scalar_prefetch=1, grid=(n_batch,),
                     in_specs=[q_spec, q_spec, q_spec, q_spec,
                               pl.BlockSpec((chips, 2, 1, e2, tok), lambda b, _: (0, 0, b, 0, 0)),
                               t_spec, t_spec, t_spec, t_spec, r_spec, r_spec],
-                    out_specs=(o_spec, o_spec, pl.BlockSpec((chips, e2 + 2 * rows // chips, d), lambda b, _: (0, 0, 0))),
-                    scratch_shapes=[pltpu.VMEM((chips, blk, reps * blk), F32), pltpu.VMEM((e, reps * blk), F32),
+                    out_specs=[o_spec, o_spec] + [pl.BlockSpec((chips, n, d), lambda b, _: (0, 0, 0)) for n in parts],
+                    scratch_shapes=[pltpu.VMEM((chips, blk, reps * blk), F32), pltpu.VMEM((chips, blk, reps * blk), BF16),
+                                    pltpu.VMEM((chips, blk, reps * blk), BF16), pltpu.VMEM((e, reps * blk), F32),
+                                    pltpu.VMEM((8, reps * blk), F32),
                                     pltpu.VMEM((chips, blk, e2), BF16), pltpu.VMEM((2, 2 * rows, blk), BF16),
                                     pltpu.VMEM((2 * rows, d), F32)]),
                 compiler_params=params(),
@@ -488,24 +507,26 @@
 
         own, par, recv = [], [], []
         for s in range(stages):
-            own_s, par_s, send_s = attention(s)
+            own_s, par_s, *sends = attention(s)
             own.append(own_s)
             par.append(lax.ppermute(par_s, 'core', swap))
-            recv.append(lax.all_to_all(send_s, 'x', 0, 0, tiled=True))
-
+            recv.append(lax.all_to_all(sends[0], 'x', 0, 0, tiled=True))
+
+        g_send, recv[-1] = lax.optimization_barrier((sends[1], recv[-1]))
+        recv_g = lax.all_to_all(g_send, 'x', 0, 0, tiled=True)
         n_w = 2 * rows // chips
-        shards = [jnp.sum(r[:, e2:].astype(F32), axis=0).astype(BF16) for r in recv]
-
-        blk = 2 * tok
+        shards = [jnp.sum(r.astype(F32), axis=0).astype(BF16) for r in [r[:, e2:] for r in recv[:-1]] + [recv_g]]
+
+        gb = 2
+        gf_spec = pl.BlockSpec((gb, stages * e2, tok), lambda b: (b, 0, 0))
         kv_own_g, kv_par_g, send_kv = pl.pallas_call(
             functools.partial(kv_grad_kernel, stages=stages),
-            out_shape=(jax.ShapeDtypeStruct((n_batch, stages * e2, tok), BF16), jax.ShapeDtypeStruct((n_batch, stages * e2, tok), BF16),
-                       jax.ShapeDtypeStruct((chips, stages * e2 // chips, d), BF16)),
-            grid=(n_batch,),
-            in_specs=[pl.BlockSpec((chips, e2, blk), lambda b: (0, 0, b))] * stages
-            + [pl.BlockSpec((1, tok, d), lambda b: (b, 0, 0))] * 2 + [pl.BlockSpec((2, half_rot, tok), lambda b: (0, 0, 0))] * 2,
-            out_specs=(pl.BlockSpec((1, stages * e2, tok), lambda b: (b, 0, 0)), pl.BlockSpec((1, stages * e2, tok), lambda b: (b, 0, 0)),
-                       pl.BlockSpec((chips, stages * e2 // chips, d), lambda b: (0, 0, 0))),
+            out_shape=[jax.ShapeDtypeStruct((n_batch, stages * e2, tok), BF16)] * 2
+            + [jax.ShapeDtypeStruct((chips, stages * e2 // chips, d), BF16)],
+            grid=(n_batch // gb,),
+            in_specs=[pl.BlockSpec((chips, e2, 2 * tok * gb), lambda b: (0, 0, b))] * stages
+            + [pl.BlockSpec((gb, tok, d), lambda b: (b, 0, 0))] * 2 + [pl.BlockSpec((2, half_rot, tok), lambda b: (0, 0, 0))] * 2,
+            out_specs=[gf_spec, gf_spec, pl.BlockSpec((chips, stages * e2 // chips, d), lambda b: (0, 0, 0))],
             scratch_shapes=[pltpu.VMEM((stages * e2, d), F32)],
             compiler_params=params(), name='kv_grad',
             cost_estimate=cost(2 * 2 * n_batch * tok * d * stages * e2, 3e7),
@@ -514,7 +535,7 @@
         recv_kv = lax.all_to_all(send_kv, 'x', 0, 0, tiled=True)
         shard_kv = jnp.sum(recv_kv.astype(F32), axis=0).astype(BF16)
 
-        nb2 = nb
+        nb2 = 2
         t2_spec = pl.BlockSpec((nb2, tok, d), lambda b, _: (b, 0, 0))
         block_out = pl.pallas_call(
             functools.partial(out_kernel, stages=stages),
@@ -528,6 +549,8 @@
             cost_estimate=cost(2 * n_batch * tok * d * n_heads * e, 3e7),
         )(ids, hidden, w_o, *own, *par)
 
+        nb2 = nb
+        t2_spec = pl.BlockSpec((nb2, tok, d), lambda b, _: (b, 0, 0))
         grad_hidden, gn = pl.pallas_call(
             functools.partial(norm_grad_kernel, stages=stages),
             out_shape=(jax.ShapeDtypeStruct((n_batch, tok, d), BF16), jax.ShapeDtypeStruct((8, d), F32)),

time: 639 us -> 616 us (0.964)
  blocking collectives: 252 us -> 239 us
    all_to_all x3 -> x4, blocking collectives: 252 us -> 239 us  [the longest x3 214 us: device_step(): recv.append(lax.all_to_all(sends[0], 'x', 0, 0, tiled=True))]
  transfers between devices with their start and end apart: 18 -> 18, of which waited for: 1 -> 2; matrix products, arithmetic and copies ran while one was open for 3% -> 2% of each run, Pallas kernels for 34% -> 35%
where the time goes in v3:
time: 616 us; the launch traced here: 607 us
  blocking collectives  239 us (39%)
  Pallas kernels  227 us (37%)
  waiting for transfers between devices  68.1 us (11%)
  starting transfers between devices  40.6 us (7%)
  between operations  14.3 us (2%)
  other arithmetic  12.2 us (2%)
    all_to_all x3, blocking collectives, device_step(): recv.append(lax.all_to_all(sends[0], 'x', 0, 0, tiled=True))  214 us
    pallas_call x4, Pallas kernels, attention(): pl.pallas_call(attn_kernel, out_shape=[jax.ShapeDtypeStruct((2, n_batch,...  94.5 us
    all_to_all x1, waiting for transfers between devices, device_step(): recv.append(lax.all_to_all(sends[0], 'x', 0, 0, tiled=True))  65.8 us
    all_to_all x1, starting transfers between devices, device_step(): recv.append(lax.all_to_all(sends[0], 'x', 0, 0, tiled=True))  34.5 us
    pallas_call x1, Pallas kernels, device_step(): pl.pallas_call(functools.partial(norm_grad_kernel, stages=stages), out_sh...  31.6 us
    all_to_all x1, blocking collectives, device_step(): recv_g = lax.all_to_all(g_send, 'x', 0, 0, tiled=True)  25.1 us
    pallas_call x1, Pallas kernels, device_step(): pl.pallas_call(functools.partial(assemble_main_kernel, stages=stages, n_q...  19.8 us
    pallas_call x1, Pallas kernels, device_step(): pl.pallas_call(functools.partial(out_kernel, stages=stages), out_shape=ja...  16.6 us
  transfers between devices with their start and end apart: 18, of which 2 were waited for; matrix products, arithmetic and copies ran while one was open for 2% of the time, Pallas kernels for 35%

profile of v3, /device:TPU:112, one launch (start us, length us, event | category | flops | bytes accessed | tf_op | source)
XLA Modules:
  0.0 607.4 jit_solution(14280685400848900049)
XLA Ops:
  10.9 7.8 %kv_proj.2 = (bf16[8,128,2048]{2,1,0:T(8,128)(2,1)}, bf16[2,8,128,128]{3,2,1,0:T(8,128)(2,1)}, bf16[2,8,128,128]{3,2,1,0:T(8,128)(2,1)}, bf16[2,8,128,128]{3,2,1,0:T(8,128)(2,1)}, bf16[2,8,128,128]{3,2,1,0:T(8,128)(2,1)}) custom-call(s32[2]{0:T(128)} %pad_add_fusion._.ids, bf16[8,128,2048]{2,1,0:T(8,128)(2,1)} %x_ref.3, ...), custom_call_target="tpu_custom_call" | custom-call | flops 2147483648 | bytes 12582912 | tf_op jit(solution)/shard_map/kv_proj/pallas_call | solution.py:426
  18.8 7.9 %kv_proj.3 = (bf16[8,128,2048]{2,1,0:T(8,128)(2,1)}, bf16[2,8,128,128]{3,2,1,0:T(8,128)(2,1)}, bf16[2,8,128,128]{3,2,1,0:T(8,128)(2,1)}, bf16[2,8,128,128]{3,2,1,0:T(8,128)(2,1)}, bf16[2,8,128,128]{3,2,1,0:T(8,128)(2,1)}) custom-call(s32[2]{0:T(128)} %pad_add_fusion._.ids, ...), custom_call_target="tpu_custom_call", output_to_operand_aliasing={{1}: (7, {}), {2}: (8, {}), {3}: (9, {}), {4}: (10, {})} | custom-call | flops 2147483648 | bytes 12582912 | tf_op jit(solution)/shard_map/kv_proj/pallas_call | solution.py:426
  28.3 15.9 %q_proj.1 = (bf16[8,1024,128]{2,1,0:T(8,128)(2,1)}, bf16[8,1024,128]{2,1,0:T(8,128)(2,1)}) custom-call(s32[2]{0:T(128)} %pad_add_fusion._.ids, bf16[8,128,2048]{2,1,0:T(8,128)(2,1)} %get-tuple-element.41.refs_0_.h0_ref.refs_4_, bf16[8,128,2048]{2,1,0:T(8,128)(2,1)} %get-tuple-element.46.refs_1_.h1_ref.refs_5_, bf16[2048,3072]{1,0:T(8,128)(2,1)} %w_ref.1, ...), custom_call_target="tpu_custom_call" | custom-call | flops 8589934592 | bytes 25165824 | tf_op jit(solution)/shard_map/q_proj/pallas_call | solution.py:452
  44.2 15.2 %do_proj.1 = (bf16[8,1024,128]{2,1,0:T(8,128)(2,1)}, bf16[8,1024,128]{2,1,0:T(8,128)(2,1)}) custom-call(s32[2]{0:T(128)} %pad_add_fusion._.ids, bf16[8,128,2048]{2,1,0:T(8,128)(2,1)} %go_ref.1, bf16[8,128,2048]{2,1,0:T(8,128)(2,1)} %collective-permute-done.1.refs_1_.g1_ref, bf16[2048,2048]{1,0:T(8,128)(2,1)} %bitcast.30), custom_call_target="tpu_custom_call" | custom-call | flops 8589934592 | bytes 25165824 | tf_op jit(solution)/shard_map/do_proj/pallas_call | solution.py:463
  59.4 23.5 %shard_map.101 = (bf16[2,8,256,128]{3,2,1,0:T(8,128)(2,1)}, bf16[2,8,256,128]{3,2,1,0:T(8,128)(2,1)}, bf16[4,256,2048]{2,1,0:T(8,128)(2,1)}) custom-call(s32[2]{0:T(128)} %pad_add_fusion._.ids, bf16[8,1024,128]{2,1,0:T(8,128)(2,1)} %get-tuple-element.47.q0_ref, bf16[8,1024,128]{2,1,0:T(8,128)(2,1)} %get-tuple-element.48.q1_ref, ...), custom_call_target="tpu_custom_call" | custom-call | flops 40000000000 | bytes 30000000 | tf_op jit(solution)/shard_map/pallas_call | solution.py:489
  83.0 34.5 %all-to-all-start = ((bf16[4,256,2048]{2,1,0:T(8,128)(2,1)}), bf16[4,256,2048]{2,1,0:T(8,128)(2,1)}, u32[]{:S(2)}, u32[]{:S(2)}) async-start(bf16[4,256,2048]{2,1,0:T(8,128)(2,1)} %get-tuple-element.63), calls=%async_computation | async-start | bytes 8388608 | tf_op jit(solution)/shard_map/all_to_all | solution.py:513
  118.2 65.8 %all-to-all-done.refs_0_ = bf16[4,256,2048]{2,1,0:T(8,128)(2,1)} async-done(((bf16[4,256,2048]{2,1,0:T(8,128)(2,1)}), bf16[4,256,2048]{2,1,0:T(8,128)(2,1)}, u32[]{:S(2)}, u32[]{:S(2)}) %all-to-all-start) | async-done | bytes 4194336 | tf_op jit(solution)/shard_map/all_to_all | solution.py:513
  184.0 2.9 slice_reduce_fusion.2
  187.0 23.6 %shard_map.102 = (bf16[2,8,256,128]{3,2,1,0:T(8,128)(2,1)}, bf16[2,8,256,128]{3,2,1,0:T(8,128)(2,1)}, bf16[4,256,2048]{2,1,0:T(8,128)(2,1)}) custom-call(s32[2]{0:T(128)} %pad_add_fusion._.ids, bf16[8,1024,128]{2,1,0:T(8,128)(2,1)} %get-tuple-element.47.q0_ref, bf16[8,1024,128]{2,1,0:T(8,128)(2,1)} %get-tuple-element.48.q1_ref, ...), custom_call_target="tpu_custom_call" | custom-call | flops 40000000000 | bytes 30000000 | tf_op jit(solution)/shard_map/pallas_call | solution.py:489
  210.6 79.9 %all_to_all.30.refs_1_ = bf16[4,256,2048]{2,1,0:T(8,128)(2,1)S(1)} all-to-all(bf16[4,256,2048]{2,1,0:T(8,128)(2,1)} %get-tuple-element.64), channel_id=1, replica_groups=mesh['dp'=2,'x'=4,'core'=2] {'x'}, dimensions={0} | all-to-all | bytes 8388608 | tf_op jit(solution)/shard_map/all_to_all | solution.py:513
  290.6 2.0 copy-done
  293.9 23.6 %shard_map.103 = (bf16[2,8,256,128]{3,2,1,0:T(8,128)(2,1)}, bf16[2,8,256,128]{3,2,1,0:T(8,128)(2,1)}, bf16[4,256,2048]{2,1,0:T(8,128)(2,1)}) custom-call(s32[2]{0:T(128)} %pad_add_fusion._.ids, bf16[8,1024,128]{2,1,0:T(8,128)(2,1)} %get-tuple-element.47.q0_ref, bf16[8,1024,128]{2,1,0:T(8,128)(2,1)} %get-tuple-element.48.q1_ref, ...), custom_call_target="tpu_custom_call" | custom-call | flops 40000000000 | bytes 30000000 | tf_op jit(solution)/shard_map/pallas_call | solution.py:489
  317.6 78.6 %all_to_all.31.refs_2_ = bf16[4,256,2048]{2,1,0:T(8,128)(2,1)S(1)} all-to-all(bf16[4,256,2048]{2,1,0:T(8,128)(2,1)} %get-tuple-element.65), channel_id=1, replica_groups=mesh['dp'=2,'x'=4,'core'=2] {'x'}, dimensions={0} | all-to-all | bytes 8388608 | tf_op jit(solution)/shard_map/all_to_all | solution.py:513
  396.2 2.0 copy-done.1
  399.6 23.8 %shard_map.104 = (bf16[2,8,256,128]{3,2,1,0:T(8,128)(2,1)}, bf16[2,8,256,128]{3,2,1,0:T(8,128)(2,1)}, bf16[4,128,2048]{2,1,0:T(8,128)(2,1)}, bf16[4,128,2048]{2,1,0:T(8,128)(2,1)}) custom-call(s32[2]{0:T(128)} %pad_add_fusion._.ids, bf16[8,1024,128]{2,1,0:T(8,128)(2,1)} %get-tuple-element.47.q0_ref, bf16[8,1024,128]{2,1,0:T(8,128)(2,1)} %get-tuple-element.48.q1_ref, ...), custom_call_target="tpu_custom_call" | custom-call | flops 40000000000 | bytes 30000000 | tf_op jit(solution)/shard_map/pallas_call | solution.py:489
  423.4 55.0 %all_to_all.32.refs_3_ = bf16[4,128,2048]{2,1,0:T(8,128)(2,1)} all-to-all(bf16[4,128,2048]{2,1,0:T(8,128)(2,1)} %get-tuple-element.67), channel_id=1, replica_groups=mesh['dp'=2,'x'=4,'core'=2] {'x'}, dimensions={0} | all-to-all | bytes 4194304 | tf_op jit(solution)/shard_map/all_to_all | solution.py:513
  478.5 25.1 %all_to_all.33 = bf16[4,128,2048]{2,1,0:T(8,128)(2,1)S(1)} all-to-all(bf16[4,128,2048]{2,1,0:T(8,128)(2,1)S(1)} %copy-done.2), channel_id=1, replica_groups=mesh['dp'=2,'x'=4,'core'=2] {'x'}, dimensions={0} | all-to-all | bytes 4194304 | tf_op jit(solution)/shard_map/all_to_all | solution.py:516
  506.0 11.8 %kv_grad.1 = (bf16[8,512,128]{2,1,0:T(8,128)(2,1)}, bf16[8,512,128]{2,1,0:T(8,128)(2,1)}, bf16[4,128,2048]{2,1,0:T(8,128)(2,1)}) custom-call(bf16[4,256,2048]{2,1,0:T(8,128)(2,1)} %all-to-all-done.refs_0_, bf16[4,256,2048]{2,1,0:T(8,128)(2,1)} %copy-done, bf16[4,256,2048]{2,1,0:T(8,128)(2,1)} %copy-done.1, bf16[4,128,2048]{2,1,0:T(8,128)(2,1)} %all_to_all.32.refs_3_, ...), custom_call_target="tpu_custom_call" | custom-call | flops 4294967296 | bytes 30000000 | tf_op jit(solution)/shard_map/kv_grad/pallas_call | solution.py:522
  518.0 3.7 all-to-all-start.4
  521.9 31.6 %norm_grad.1 = (bf16[8,128,2048]{2,1,0:T(8,128)(2,1)}, f32[8,2048]{1,0:T(8,128)}) custom-call(s32[2]{0:T(128)} %pad_add_fusion._.ids, bf16[8,128,2048]{2,1,0:T(8,128)(2,1)} %x_ref.3, bf16[8,128,2048]{2,1,0:T(8,128)(2,1)} %go_ref.1, bf16[1,2048]{1,0:T(2,128)(2,1)} %reshape.94.refs_1_.g_ref, bf16[2048,3072]{1,0:T(8,128)(2,1)} %w_ref.1, ...), custom_call_target="tpu_custom_call" | custom-call | flops 12884901888 | bytes 40000000 | tf_op jit(solution)/shard_map/norm_grad/pallas_call | solution.py:554
  556.2 16.6 %out_proj.1 = bf16[8,128,2048]{2,1,0:T(8,128)(2,1)} custom-call(s32[2]{0:T(128)} %pad_add_fusion._.ids, bf16[8,128,2048]{2,1,0:T(8,128)(2,1)} %x_ref.3, bf16[2048,2048]{1,0:T(8,128)(2,1)} %bitcast.31, bf16[2,8,256,128]{3,2,1,0:T(8,128)(2,1)} %get-tuple-element.52.refs_0_, bf16[2,8,256,128]{3,2,1,0:T(8,128)(2,1)} %get-tuple-element.54.refs_1_, ...), custom_call_target="tpu_custom_call" | custom-call | flops 8589934592 | bytes 30000000 | tf_op jit(solution)/shard_map/out_proj/pallas_call | solution.py:540
  572.9 19.8 %assemble_main.1 = (f32[2048,3072]{1,0:T(8,128)}, f32[32,64,2048]{2,1,0:T(8,128)}) custom-call(bf16[4,2,128,2048]{3,2,1,0:T(8,128)(2,1)} %bitcast.24, bf16[4,2,128,2048]{3,2,1,0:T(8,128)(2,1)} %bitcast.25, bf16[4,2,128,2048]{3,2,1,0:T(8,128)(2,1)} %bitcast.26, bf16[4,2,128,2048]{3,2,1,0:T(8,128)(2,1)} %bitcast.27), custom_call_target="tpu_custom_call" | custom-call | flops 2000000000 | bytes 60000000 | tf_op jit(solution)/shard_map/assemble_main/pallas_call | solution.py:578
  592.7 1.6 convert_reduce_fusion
  594.3 6.4 %assemble_tail.1 = f32[2048,3072]{1,0:T(8,128)} custom-call(bf16[4,2,144,2048]{3,2,1,0:T(8,128)(2,1)} %bitcast.23, f32[2048,3072]{1,0:T(8,128)} %get-tuple-element.75._), custom_call_target="tpu_custom_call", output_to_operand_aliasing={{}: (1, {})} | custom-call | flops 1000000000 | bytes 20000000 | tf_op jit(solution)/shard_map/assemble_tail/pallas_call | solution.py:588
  (67 shorter events, 14.3 us)
Async XLA Ops:
  7.2 52.3 %all-gather.19.cloned.1.call-start = ((), (), s32[]{:S(2)}) async-start(), calls=%async_computation.6 | async-start | bytes 2621440 | tf_op jit(solution)/shard_map/all_gather | solution.py:477
  7.2 11.5 %collective-permute-start = (bf16[8,128,2048]{2,1,0:T(8,128)(2,1)}, bf16[8,128,2048]{2,1,0:T(8,128)(2,1)}, u32[]{:S(2)}, u32[]{:S(2)}) collective-permute-start(bf16[8,128,2048]{2,1,0:T(8,128)(2,1)} %x_ref.3), channel_id=1, source_target_pairs={{0,1},{1,0},{2,3},{3,2},{4,5},{5,4},{6,7},{7,6},{8,9},{9,8},{10,11... | collective-permute-start | bytes 12582920 | tf_op jit(solution)/shard_map/ppermute | solution.py:405
  10.3 8.5 %copy-start.3 = (f32[2,32,128]{2,1,0:T(8,128)}, f32[2,32,128]{2,1,0:T(8,128)S(1)}, u32[]{:S(2)}) copy-start(f32[2,32,128]{2,1,0:T(8,128)S(1)} %get-tuple-element.81.refs_4_.sin_ref.refs_7_) | copy-start | bytes 98308
  10.3 8.5 %copy-start.4 = (f32[2,32,128]{2,1,0:T(8,128)}, f32[2,32,128]{2,1,0:T(8,128)S(1)}, u32[]{:S(2)}) copy-start(f32[2,32,128]{2,1,0:T(8,128)S(1)} %get-tuple-element.82.refs_3_.cos_ref.refs_6_) | copy-start | bytes 98308
  26.7 160.3 %all-gather.21.cloned.1.call-start = ((), (), s32[]{:S(2)}) async-start(), calls=%async_computation.7 | async-start | bytes 2621440 | tf_op jit(solution)/shard_map/all_gather | solution.py:477
  26.8 17.5 %collective-permute-start.1 = (bf16[8,128,2048]{2,1,0:T(8,128)(2,1)}, bf16[8,128,2048]{2,1,0:T(8,128)(2,1)}, u32[]{:S(2)}, u32[]{:S(2)}) collective-permute-start(bf16[8,128,2048]{2,1,0:T(8,128)(2,1)} %go_ref.1), channel_id=1, source_target_pairs={{0,1},{1,0},{2,3},{3,2},{4,5},{5,4},{6,7},{7,6},{8,9},{9,8},{10,11... | collective-permute-start | bytes 12582920 | tf_op jit(solution)/shard_map/ppermute | solution.py:406
  27.5 266.4 %all-gather.23.cloned.1.call-start = ((), (), s32[]{:S(2)}) async-start(), calls=%async_computation.8 | async-start | bytes 2621440 | tf_op jit(solution)/shard_map/all_gather | solution.py:477
  83.0 101.0 %all-to-all-start = ((bf16[4,256,2048]{2,1,0:T(8,128)(2,1)}), bf16[4,256,2048]{2,1,0:T(8,128)(2,1)}, u32[]{:S(2)}, u32[]{:S(2)}) async-start(bf16[4,256,2048]{2,1,0:T(8,128)(2,1)} %get-tuple-element.63), calls=%async_computation | async-start | bytes 8388608 | tf_op jit(solution)/shard_map/all_to_all | solution.py:513
  117.5 282.1 %all-gather.25.cloned.1.call-start = ((), (), s32[]{:S(2)}) async-start(), calls=%async_computation.9 | async-start | bytes 2621440 | tf_op jit(solution)/shard_map/all_gather | solution.py:477
  118.1 454.7 %all-gather.29.cloned.1.call-start = ((), (), s32[]{:S(2)}) async-start(), calls=%async_computation.11 | async-start | bytes 4718592 | tf_op jit(solution)/shard_map/all_gather | solution.py:577
  186.9 385.9 %all-gather.31.cloned.1.call-start = ((), (), s32[]{:S(2)}) async-start(), calls=%async_computation.12 | async-start | bytes 4718592 | tf_op jit(solution)/shard_map/all_gather | solution.py:577
  290.6 2.0 copy-start
  293.8 279.0 %all-gather.33.cloned.1.call-start = ((), (), s32[]{:S(2)}) async-start(), calls=%async_computation.13 | async-start | bytes 4718592 | tf_op jit(solution)/shard_map/all_gather | solution.py:577
  396.2 2.0 copy-start.1
  399.5 173.4 %all-gather.35.cloned.1.call-start = ((), (), s32[]{:S(2)}) async-start(), calls=%async_computation.14 | async-start | bytes 4718592 | tf_op jit(solution)/shard_map/all_gather | solution.py:577
  423.4 55.1 %copy-start.2 = (bf16[4,128,2048]{2,1,0:T(8,128)(2,1)S(1)}, bf16[4,128,2048]{2,1,0:T(8,128)(2,1)}, u32[]{:S(2)}) copy-start(bf16[4,128,2048]{2,1,0:T(8,128)(2,1)} %get-tuple-element.74) | copy-start | bytes 6291460
  504.9 16.9 %collective-permute-start.2 = (bf16[2,8,256,128]{3,2,1,0:T(8,128)(2,1)}, bf16[2,8,256,128]{3,2,1,0:T(8,128)(2,1)}, u32[]{:S(2)}, u32[]{:S(2)}) collective-permute-start(bf16[2,8,256,128]{3,2,1,0:T(8,128)(2,1)} %get-tuple-element.59), channel_id=1, source_target_pairs={{0,1},{1,0},{2,3},{3,2},{4,5},{5,4},{6,7},{7,6},{8,9},{9,8},{10,11... | collective-permute-start | bytes 3145736 | tf_op jit(solution)/shard_map/ppermute | solution.py:512
  505.0 16.8 %collective-permute-start.3 = (bf16[2,8,256,128]{3,2,1,0:T(8,128)(2,1)}, bf16[2,8,256,128]{3,2,1,0:T(8,128)(2,1)}, u32[]{:S(2)}, u32[]{:S(2)}) collective-permute-start(bf16[2,8,256,128]{3,2,1,0:T(8,128)(2,1)} %get-tuple-element.60), channel_id=1, source_target_pairs={{0,1},{1,0},{2,3},{3,2},{4,5},{5,4},{6,7},{7,6},{8,9},{9,8},{10,11... | collective-permute-start | bytes 3145736 | tf_op jit(solution)/shard_map/ppermute | solution.py:512
  505.5 16.3 %collective-permute-start.4 = (bf16[2,8,256,128]{3,2,1,0:T(8,128)(2,1)}, bf16[2,8,256,128]{3,2,1,0:T(8,128)(2,1)}, u32[]{:S(2)}, u32[]{:S(2)}) collective-permute-start(bf16[2,8,256,128]{3,2,1,0:T(8,128)(2,1)} %get-tuple-element.61), channel_id=1, source_target_pairs={{0,1},{1,0},{2,3},{3,2},{4,5},{5,4},{6,7},{7,6},{8,9},{9,8},{10,11... | collective-permute-start | bytes 3145736 | tf_op jit(solution)/shard_map/ppermute | solution.py:512
  505.6 16.2 %collective-permute-start.5 = (bf16[2,8,256,128]{3,2,1,0:T(8,128)(2,1)}, bf16[2,8,256,128]{3,2,1,0:T(8,128)(2,1)}, u32[]{:S(2)}, u32[]{:S(2)}) collective-permute-start(bf16[2,8,256,128]{3,2,1,0:T(8,128)(2,1)} %get-tuple-element.62), channel_id=1, source_target_pairs={{0,1},{1,0},{2,3},{3,2},{4,5},{5,4},{6,7},{7,6},{8,9},{9,8},{10,11... | collective-permute-start | bytes 3145736 | tf_op jit(solution)/shard_map/ppermute | solution.py:512
  517.8 4.0 collective-permute-start.6
  518.0 36.7 %all-to-all-start.4 = ((bf16[4,128,2048]{2,1,0:T(8,128)(2,1)}), bf16[4,128,2048]{2,1,0:T(8,128)(2,1)S(1)}, u32[]{:S(2)}, u32[]{:S(2)}) async-start(bf16[4,128,2048]{2,1,0:T(8,128)(2,1)} %get-tuple-element.72), calls=%async_computation.4 | async-start | bytes 4194304 | tf_op jit(solution)/shard_map/all_to_all | solution.py:535
  521.8 70.9 %all-gather.27.cloned.1.call-start = ((), (), s32[]{:S(2)}) async-start(), calls=%async_computation.10 | async-start | bytes 5308416 | tf_op jit(solution)/shard_map/all_gather | solution.py:573
Sparse Core Ops, SparseCore 0:
  26.8 29.6 all-gather.18
  58.7 26.6 all-gather.20
  87.0 26.7 all-gather.22
  119.5 65.1 all-gather.24
  187.0 28.4 all-gather.28
  294.0 28.2 all-gather.30
  399.6 28.3 all-gather.32
  505.1 34.3 all-gather.34
  556.3 32.4 all-gather.26

commit v4 on v3

v4 whole, which is shorter than its diff:
```python
import functools
import math

import jax
import jax.numpy as jnp
from jax import lax
from jax.experimental import pallas as pl
from jax.experimental.pallas import tpu as pltpu
from jax.sharding import Mesh, PartitionSpec as P


NORM_EPS = 1e-5
ROPE_BASE = 10000.0
ROPE_GAIN = math.sqrt(1.0 + math.log(32.0) / math.log(4096.0))
MASK_VALUE = -1e30
LOG2E = math.log2(math.e)
CORES = 2
PAIR = 2
BF16 = jnp.bfloat16
F32 = jnp.float32
VMEM_LIMIT = 60 * 1024 * 1024

NN = (((1,), (0,)), ((), ()))
NT = (((1,), (1,)), ((), ()))


cat_rows = functools.partial(jnp.concatenate, axis=0)
cat_lanes = functools.partial(jnp.concatenate, axis=1)
column_max = functools.partial(jnp.max, axis=0, keepdims=True)
column_sum = functools.partial(jnp.sum, axis=0, keepdims=True)
row_mean = functools.partial(jnp.mean, axis=-1, keepdims=True)


def whole(*shape):
    return pl.BlockSpec(shape, lambda *_: (0,) * len(shape))


def along(axis, *shape):
    return pl.BlockSpec(shape, lambda i, *_: tuple(i if n == axis else 0 for n in range(len(shape))))


def dot(a, b, dims=NN):
    return lax.dot_general(a, b, dims, preferred_element_type=F32)


def cost(flops, nbytes, trans=0):
    return pl.CostEstimate(flops=int(flops), bytes_accessed=int(nbytes), transcendentals=int(trans))


def params(n_axes=1):
    return pltpu.CompilerParams(dimension_semantics=("arbitrary",) * n_axes, vmem_limit_bytes=VMEM_LIMIT)


def rope_rows(block, cos, sin, direction):
    half = cos.shape[0]
    a, b = block[:half], block[half:PAIR * half]
    s = sin * direction
    return cat_rows([a * cos - b * s, b * cos + a * s])


def kv_proj_kernel(x_ref, g_ref, wk_ref, wv_ref, cos_ref, sin_ref, *refs):
    nb, tok, d = x_ref.shape
    stages = (wk_ref.shape[1] // (PAIR * cos_ref.shape[0]))
    h_ref, kv_refs = refs[-stages - 1], refs[-stages:]
    e2 = kv_refs[0].shape[2]
    e = e2 // 2
    x = x_ref[:].reshape(nb * tok, d).astype(F32)
    inv = lax.rsqrt(row_mean(x * x) + NORM_EPS)
    h = (x * inv * g_ref[:].astype(F32)).astype(BF16)
    h_ref[:] = h.reshape(nb, tok, d)
    cos, sin = cos_ref[:], sin_ref[:]
    k = dot(h, wk_ref[:]).T
    v = dot(h, wv_ref[:]).T
    for i in range(stages):
        for b in range(nb):
            kv_refs[i][0, b, 0:e] = rope_rows(k[i * e:(i + 1) * e, b * tok:(b + 1) * tok], cos, sin, 1.0).astype(BF16)
            kv_refs[i][0, b, e:PAIR * e] = v[i * e:(i + 1) * e, b * tok:(b + 1) * tok].astype(BF16)


def q_proj_kernel(h0_ref, h1_ref, w_ref, cos_ref, sin_ref, q0_ref, q1_ref):
    nb, tok, d = h0_ref.shape
    e = PAIR * cos_ref.shape[1]
    rows = w_ref.shape[1]
    scale = e ** -0.5
    step = 4 * e

    def run(h_ref, q_ref, side):
        h = h_ref[:].reshape(nb * tok, d)
        cos, sin = cos_ref[side], sin_ref[side]
        for r in range(0, rows, step):
            blk = dot(h, w_ref[:, r:r + step]).T
            for i in range(0, step, e):
                for b in range(nb):
                    q_ref[b, r + i:r + i + e] = (rope_rows(blk[i:i + e, b * tok:(b + 1) * tok], cos, sin, 1.0).astype(BF16)
                                                 * scale).astype(BF16)

    half = pl.num_programs(0) // 2
    pl.when(pl.program_id(0) < half)(lambda: run(h0_ref, q0_ref, 0))
    pl.when(pl.program_id(0) >= half)(lambda: run(h1_ref, q1_ref, 1))


def do_proj_kernel(g0_ref, g1_ref, w_ref, o0_ref, o1_ref):
    nb, tok, d = g0_ref.shape
    rows = w_ref.shape[0]
    step = 512

    def run(g_ref, o_ref):
        g = g_ref[:].reshape(nb * tok, d)
        for r in range(0, rows, step):
            blk = dot(w_ref[r:r + step], g, NT)
            for b in range(nb):
                o_ref[b, r:r + step] = blk[:, b * tok:(b + 1) * tok].astype(BF16)

    half = pl.num_programs(0) // 2
    pl.when(pl.program_id(0) < half)(lambda: run(g0_ref, o0_ref))
    pl.when(pl.program_id(0) >= half)(lambda: run(g1_ref, o1_ref))


def drop_scalar(kernel):
    def wrapped(_, *refs):
        kernel(*refs)

    return wrapped


def ring_peers(chips):
    chip, core = lax.axis_index('x'), lax.axis_index('core')
    return chip, lax.rem(chip + 1, chips), lax.rem(chip + chips - 1, chips), lax.rem(chip + 2, chips), core, 1 - core


def ring_barrier(chips):
    _, right, left, _, _, mate = ring_peers(chips)
    sem = pltpu.get_barrier_semaphore()
    for who in ({'x': right}, {'x': left}, {'core': mate}):
        pl.semaphore_signal(sem, inc=1, device_id=who, device_id_type=pl.DeviceIdType.MESH)
    pl.semaphore_wait(sem, 3)


class RingSum:
    @staticmethod
    def scratch(chips, rows, d):
        half = rows // 2
        return [pltpu.VMEM((2, half, d), BF16), pltpu.VMEM((2, half, d), BF16), pltpu.VMEM((rows, d), BF16),
                pltpu.VMEM((2, rows, d), BF16), pltpu.SemaphoreType.DMA((6,)), pltpu.SemaphoreType.DMA((6,)),
                pltpu.SemaphoreType.DMA((3,))]

    def __init__(self, send_ref, total_ref, mid, buf, own, recv, s_sem, r_sem, l_sem):
        chips, rows, _ = send_ref.shape
        half = rows // 2
        chip, right, left, far, _, _ = ring_peers(chips)
        top, low = pl.ds(0, half), pl.ds(half, half)

        def remote(n, src, dst, who):
            return pltpu.make_async_remote_copy(src_ref=src, dst_ref=dst, send_sem=s_sem.at[n], recv_sem=r_sem.at[n],
                                                device_id={'x': who}, device_id_type=pl.DeviceIdType.MESH)

        self.first = [remote(0, send_ref.at[far, top], mid.at[0], right), remote(1, send_ref.at[far, low], mid.at[1], left),
                      remote(2, send_ref.at[left, top], recv.at[1, top], left),
                      remote(3, send_ref.at[right, low], recv.at[0, low], right)]
        self.second = [remote(4, buf.at[0], recv.at[0, top], right), remote(5, buf.at[1], recv.at[1, low], left)]
        self.local = [pltpu.make_async_copy(send_ref.at[right, top], buf.at[0], l_sem.at[0]),
                      pltpu.make_async_copy(send_ref.at[left, low], buf.at[1], l_sem.at[1]),
                      pltpu.make_async_copy(send_ref.at[chip], own, l_sem.at[2])]
        self.mid, self.buf, self.own, self.recv, self.total_ref = mid, buf, own, recv, total_ref

    def start(self):
        for c in self.first[:2] + self.local:
            c.start()

    def start_direct(self):
        for c in self.first[2:]:
            c.start()

    def merge(self):
        for i in range(2):
            self.local[i].wait()
            self.first[i].wait_recv()
            self.buf[i] = (self.buf[i].astype(F32) + self.mid[i].astype(F32)).astype(BF16)

    def send(self):
        for c in self.second:
            c.start()

    def finish(self):
        self.local[2].wait()
        for c in self.first[2:] + self.second:
            c.wait_recv()
        self.total_ref[:] = (self.own[:].astype(F32) + self.recv[0].astype(F32) + self.recv[1].astype(F32)).astype(BF16)
        for c in self.first + self.second:
            c.wait_send()


class RingGather:
    @staticmethod
    def scratch():
        return [pltpu.SemaphoreType.DMA((8,)), pltpu.SemaphoreType.DMA((8,)), pltpu.SemaphoreType.DMA((1,))]

    def __init__(self, block_ref, out_ref, s_sem, r_sem, l_sem):
        chips, rows = out_ref.shape[1], out_ref.shape[2]
        chip, right, left, far, core, mate = ring_peers(chips)
        top, low = pl.ds(0, rows // 2), pl.ds(rows // 2, rows // 2)

        def remote(n, src, dst, who):
            return pltpu.make_async_remote_copy(src_ref=src, dst_ref=dst, send_sem=s_sem.at[n], recv_sem=r_sem.at[n],
                                                device_id=who, device_id_type=pl.DeviceIdType.MESH)

        mine = out_ref.at[core]
        self.local = pltpu.make_async_copy(block_ref, mine.at[chip], l_sem.at[0])
        self.first = [remote(0, block_ref, mine.at[chip], {'x': right}), remote(1, block_ref, mine.at[chip], {'x': left})]
        self.second = [remote(2, mine.at[left, top], mine.at[left, top], {'x': right}),
                       remote(3, mine.at[right, low], mine.at[right, low], {'x': left})]
        self.mate = [remote(4, block_ref, mine.at[chip], {'core': mate})] + [
            remote(5 + i, mine.at[j], mine.at[j], {'core': mate}) for i, j in enumerate((left, right, far))]

    def start(self):
        for c in [self.local, *self.first, self.mate[0]]:
            c.start()

    def forward(self):
        for c in self.first:
            c.wait_recv()
        for c in self.second + self.mate[1:3]:
            c.start()

    def last(self):
        for c in self.second:
            c.wait_recv()
        self.mate[3].start()

    def finish(self):
        self.local.wait()
        for c in self.mate:
            c.wait_recv()
        for c in self.first + self.second + self.mate:
            c.wait_send()


def run_at(step, n, *actions):
    @pl.when(step == n)
    def _():
        for a in actions:
            a()


def host_rings(ring_sum, gather, step, plan, chips):
    if ring_sum is None and gather is None:
        return
    direct, merge, forward = plan
    run_at(step, 0, lambda: ring_barrier(chips), *([ring_sum.start] if ring_sum else []), *([gather.start] if gather else []))
    if ring_sum:
        run_at(step, direct, ring_sum.start_direct)
        run_at(step, merge + 1, ring_sum.send)
    if gather:
        run_at(step, forward, gather.forward)


def finish_rings(ring_sum, gather, step, plan, final):
    if ring_sum:
        run_at(step, plan[1], ring_sum.merge)
    last = ([gather.last] if gather else []) + ([ring_sum.finish] if ring_sum else []) + ([gather.finish] if gather else [])
    if last:
        run_at(step, final, *last)


def comm_params(cid, n_axes=1):
    return pltpu.CompilerParams(dimension_semantics=("arbitrary",) * n_axes, vmem_limit_bytes=VMEM_LIMIT,
                                collective_id=cid, has_side_effects=True)


def attn_kernel(q0_ref, q1_ref, do0_ref, do1_ref, kv_ref, h0_ref, h1_ref, g0_ref, g1_ref, cos_ref, sin_ref, *refs,
                has_sum, has_gather):
    refs = list(refs)
    ring_sum = gather = None
    prev_ref = refs.pop(0) if has_sum else None
    shard_ref = refs.pop(0) if has_gather else None
    own_ref, par_ref, send_ref = refs[:3]
    refs = refs[3:]
    total_ref = refs.pop(0) if has_sum else None
    all_ref = refs.pop(0) if has_gather else None
    s_ref, p_ref, ds_ref, acc_ref, ml_ref, kvt_ref, lhs_ref, gacc_ref = refs[:8]
    refs = refs[8:]
    if has_sum:
        ring_sum = RingSum(prev_ref, total_ref, *refs[:7])
        refs = refs[7:]
    if has_gather:
        gather = RingGather(shard_ref, all_ref, *refs)
    g_send_ref = send_ref
    chip, core = lax.axis_index('x'), lax.axis_index('core')
    b_id = pl.program_id(0)
    plan = (2, 3, 4)
    host_rings(ring_sum, gather, b_id, plan, kv_ref.shape[0])
    chips = kv_ref.shape[0]
    rows, tok = q0_ref.shape[1], q0_ref.shape[2]
    e = kv_ref.shape[3] // 2
    reps = rows // e
    blk = PAIR * tok

    def heads_to_lanes(first_ref, second_ref):
        full = cat_lanes([first_ref[0], second_ref[0]])
        return cat_lanes([full[i * e:(i + 1) * e] for i in range(reps)])

    head_cols = [slice(i * blk, (i + 1) * blk) for i in range(reps)]

    def kv_block(i):
        return cat_lanes([kv_ref[chip - i, 0, 0], kv_ref[chip - i, 1, 0]])

    def scores(i):
        qt = heads_to_lanes(q0_ref, q1_ref)
        q_pad = cat_rows([qt, jnp.zeros_like(qt)])
        kvt = kv_block(i).T
        kvt_ref[i] = kvt
        tops = []
        for cols in head_cols:
            t = dot(kvt, q_pad[:, cols])
            if i == 0:
                r = lax.broadcasted_iota(jnp.int32, (blk, blk), 0)
                c = lax.broadcasted_iota(jnp.int32, (blk, blk), 1)
                shift = (1 - PAIR * core) * tok
                k_pos = jnp.where(r < tok, r, r - tok + shift)
                q_pos = jnp.where(c < tok, c, c - tok + shift)
                t = jnp.where(k_pos <= q_pos, t, MASK_VALUE)
            s_ref[i, :, cols] = t
            tops.append(column_max(t))
        return cat_lanes(tops) * LOG2E

    def accumulate(i, m):
        v_t = kv_block(i)[e:PAIR * e]
        sums, outs = [], []
        for cols in head_cols:
            p = jnp.exp2(s_ref[i, :, cols] * LOG2E - m[:, cols])
            sums.append(column_sum(p))
            outs.append(dot(v_t, p.astype(BF16)))
        return cat_lanes(sums), cat_lanes(outs)

    ml_ref[0:1] = scores(0)
    ml_ref[1:2] = jnp.zeros_like(ml_ref[1:2])
    acc_ref[:] = jnp.zeros_like(acc_ref)

    for i in range(1, chips):
        @pl.when(i <= chip)
        def _(i=i):
            m = ml_ref[0:1]
            add_l, add_o = accumulate(i - 1, m)
            m_new = jnp.maximum(m, scores(i))
            alpha = jnp.exp2(m - m_new)
            acc_ref[:] = (acc_ref[:] + add_o) * alpha
            ml_ref[1:2] = (ml_ref[1:2] + add_l) * alpha
            ml_ref[0:1] = m_new

    m = ml_ref[0:1]
    add_l, add_o = accumulate(chip, m)
    l = ml_ref[1:2] + add_l
    o_t = (acc_ref[:] + add_o) * (1.0 / l)
    dot_t = heads_to_lanes(do0_ref, do1_ref)
    ml_ref[1:2] = column_sum(o_t * dot_t.astype(F32))
    ml_ref[0:1] = m + jnp.log2(l)
    o_b = o_t.astype(BF16)
    o_full = cat_rows([o_b[:, cols] for cols in head_cols])
    odd = lax.rem(b_id, 2)
    lhs_ref[odd, rows:PAIR * rows] = o_full
    own_ref[0, 0] = o_full[:, :tok]
    par_ref[0, 0] = o_full[:, tok:]
    acc_ref[:] = jnp.zeros_like(acc_ref)

    def score_grads(i):
        dot_t = heads_to_lanes(do0_ref, do1_ref)
        do_pad = cat_rows([jnp.zeros_like(dot_t), dot_t])
        kvt = kvt_ref[i]
        for cols in head_cols:
            p = jnp.exp2(s_ref[i, :, cols] * LOG2E - ml_ref[0:1, cols])
            dp = dot(kvt, do_pad[:, cols])
            p_ref[i, :, cols] = p.astype(BF16)
            ds_ref[i, :, cols] = (p * (dp - ml_ref[1:2, cols])).astype(BF16)

    def input_grads(i):
        qt = heads_to_lanes(q0_ref, q1_ref)
        dot_t = heads_to_lanes(do0_ref, do1_ref)
        k_t = kv_block(i)[0:e]
        dv = dot(dot_t, p_ref[i], NT)
        dk = dot(qt, ds_ref[i], NT)
        send_ref[chip - i, 0:PAIR * e, pl.ds(pl.multiple_of(b_id * blk, blk), blk)] = cat_rows([dk, dv]).astype(BF16)
        acc_ref[:] += dot(k_t, ds_ref[i])

    score_grads(0)
    for i in range(1, chips):
        @pl.when(i <= chip)
        def _(i=i):
            input_grads(i - 1)
            score_grads(i)

    input_grads(chip)

    def zero_step(j, carry):
        send_ref[j, 0:PAIR * e, pl.ds(pl.multiple_of(b_id * blk, blk), blk)] = jnp.zeros((PAIR * e, blk), BF16)
        return carry

    lax.fori_loop(chip + 1, chips, zero_step, 0)

    cos = cat_lanes([cos_ref[0], cos_ref[1]])
    sin = cat_lanes([sin_ref[0], sin_ref[1]])
    dq_rows = []
    for cols in head_cols:
        dq = (acc_ref[:, cols] * (e ** -0.5)).astype(BF16).astype(F32)
        dq_rows.append(rope_rows(dq, cos, sin, -1.0).astype(BF16))
    dq_full = cat_rows(dq_rows)
    own_ref[1, 0] = dq_full[:, :tok]
    par_ref[1, 0] = dq_full[:, tok:]

    d = h0_ref.shape[2]
    step = 512
    lhs_ref[odd, 0:rows] = dq_full

    def weight_grads(first):
        for c in range(0, d, step):
            cs = slice(c, c + step)
            for r, (a_ref, b_ref) in enumerate(((h0_ref, h1_ref), (g0_ref, g1_ref))):
                rs = slice(r * rows, (r + 1) * rows)
                lhs = cat_lanes([lhs_ref[0, rs], lhs_ref[1, rs]])
                rhs = cat_rows([a_ref[0, :, cs], b_ref[0, :, cs], a_ref[1, :, cs], b_ref[1, :, cs]])
                if first:
                    gacc_ref[rs, cs] = dot(lhs, rhs)
                else:
                    gacc_ref[rs, cs] += dot(lhs, rhs)

    pl.when(b_id == 1)(lambda: weight_grads(True))
    pl.when((odd == 1) & (b_id > 1))(lambda: weight_grads(False))

    @pl.when(b_id == pl.num_programs(0) - 1)
    def _():
        for j in range(chips):
            n = rows // chips
            base = PAIR * e
            g_send_ref[j, base:base + n] = gacc_ref[j * n:(j + 1) * n].astype(BF16)
            g_send_ref[j, base + n:base + PAIR * n] = gacc_ref[rows + j * n:rows + (j + 1) * n].astype(BF16)

    finish_rings(ring_sum, gather, b_id, plan, pl.num_programs(0) - 1)


def kv_grad_kernel(*refs, stages):
    recv = refs[:stages]
    h0_ref, h1_ref, cos_ref, sin_ref, shard_ref, own_ref, par_ref, send_ref, all_ref, gacc_ref = refs[stages:stages + 10]
    gather = RingGather(shard_ref, all_ref, *refs[stages + 10:])
    plan = (0, 0, 3)
    host_rings(None, gather, pl.program_id(0), plan, all_ref.shape[1])
    nb, tok, d = h0_ref.shape
    e2 = own_ref.shape[1] // stages
    e = e2 // 2
    side = cat_lanes([cos_ref[0], cos_ref[1]]), cat_lanes([sin_ref[0], sin_ref[1]])
    cos, sin = (cat_lanes([t] * nb) for t in side)
    parts = []
    for r in recv:
        total = r[:].astype(F32)
        parts.append(cat_rows([rope_rows(total[0:e], cos, sin, -1.0), total[e:PAIR * e]]).astype(BF16))
    gf = cat_rows(parts)
    for b in range(nb):
        own_ref[b] = gf[:, PAIR * b * tok:(PAIR * b + 1) * tok]
        par_ref[b] = gf[:, (PAIR * b + 1) * tok:(PAIR * b + 2) * tok]

    def weight_grads(first):
        step = 512
        for c in range(0, d, step):
            cs = slice(c, c + step)
            hh = cat_rows([r[b, :, cs] for b in range(nb) for r in (h0_ref, h1_ref)])
            if first:
                gacc_ref[:, cs] = dot(gf, hh)
            else:
                gacc_ref[:, cs] += dot(gf, hh)

    pl.when(pl.program_id(0) == 0)(lambda: weight_grads(True))
    pl.when(pl.program_id(0) > 0)(lambda: weight_grads(False))

    @pl.when(pl.program_id(0) == pl.num_programs(0) - 1)
    def _():
        n = send_ref.shape[1]
        for j in range(send_ref.shape[0]):
            send_ref[j] = gacc_ref[j * n:(j + 1) * n].astype(BF16)

    finish_rings(None, gather, pl.program_id(0), plan, pl.num_programs(0) - 1)


def out_kernel(x_ref, w_ref, prev_ref, *refs, stages):
    core = lax.axis_index('core')
    o_refs, (y_ref, total_ref, lhs_ref) = refs[:PAIR * stages], refs[PAIR * stages:PAIR * stages + 3]
    ring_sum = RingSum(prev_ref, total_ref, *refs[PAIR * stages + 3:])
    plan = (1, 2, 0)
    host_rings(ring_sum, None, pl.program_id(0), plan, prev_ref.shape[0])
    nb, tok, d = x_ref.shape
    rows = o_refs[0].shape[2]
    half = stages * rows
    for side in range(2):
        base = (core if side == 0 else 1 - core) * half
        for s in range(stages):
            for b in range(nb):
                lhs_ref[b * tok:(b + 1) * tok, pl.ds(pl.multiple_of(base + s * rows, rows), rows)] = o_refs[side * stages + s][0, b].T
    lhs = lhs_ref[:]
    step = 512
    for c in range(0, d, step):
        prod = dot(lhs, w_ref[:, c:c + step])
        y_ref[:, :, c:c + step] = (x_ref[:, :, c:c + step].astype(F32) + prod.reshape(nb, tok, step)).astype(BF16)

    finish_rings(ring_sum, None, pl.program_id(0), plan, pl.num_programs(0) - 1)


def norm_grad_kernel(x_ref, go_ref, g_ref, w_ref, kv0_ref, kv1_ref, prev_ref, shard_ref, *refs, stages):
    core = lax.axis_index('core')
    q_refs = refs[:PAIR * stages]
    gh_ref, gn_ref, total_ref, all_ref, lhs_ref, tot_ref = refs[PAIR * stages:PAIR * stages + 6]
    ring_sum = RingSum(prev_ref, total_ref, *refs[PAIR * stages + 6:PAIR * stages + 13])
    gather = RingGather(shard_ref, all_ref, *refs[PAIR * stages + 13:])
    plan = (1, 0, 2)
    host_rings(ring_sum, gather, pl.program_id(0), plan, prev_ref.shape[0])
    nb, tok, d = x_ref.shape
    rows = q_refs[0].shape[2]
    half = stages * rows
    e2 = kv0_ref.shape[1] // stages
    e = e2 // 2
    kv_half = stages * e
    for side in range(2):
        who = core if side == 0 else 1 - core
        kv_ref = kv0_ref if side == 0 else kv1_ref
        for b in range(nb):
            ts = slice(b * tok, (b + 1) * tok)
            for s in range(stages):
                lhs_ref[ts, pl.ds(pl.multiple_of(who * half + s * rows, rows), rows)] = q_refs[side * stages + s][0, b].T
            ks = cat_rows([kv_ref[b, i * e2:i * e2 + e] for i in range(stages)])
            vs = cat_rows([kv_ref[b, i * e2 + e:(i + 1) * e2] for i in range(stages)])
            base = PAIR * half
            lhs_ref[ts, pl.ds(pl.multiple_of(base + who * kv_half, kv_half), kv_half)] = ks.T
            base = base + PAIR * kv_half
            lhs_ref[ts, pl.ds(pl.multiple_of(base + who * kv_half, kv_half), kv_half)] = vs.T
    lhs = lhs_ref[:]
    step = 256
    for c in range(0, d, step):
        tot_ref[:, c:c + step] = dot(lhs, w_ref[c:c + step, :], NT)

    @pl.when(pl.program_id(0) == 0)
    def _():
        gn_ref[:] = jnp.zeros_like(gn_ref)

    g = g_ref[:].astype(F32)
    for b in range(nb):
        total = tot_ref[b * tok:(b + 1) * tok]
        x = x_ref[b].astype(F32)
        inv = lax.rsqrt(row_mean(x * x) + NORM_EPS)
        unit = x * inv
        gu = total * g
        mean_dot = row_mean(gu * unit)
        gh_ref[b] = (go_ref[b].astype(F32) + inv * (gu - unit * mean_dot)).astype(BF16)
        gn_ref[:] += jnp.sum((total * unit).reshape(tok // 8, 8, d), axis=0)

    finish_rings(ring_sum, gather, pl.program_id(0), plan, pl.num_programs(0) - 1)


def transpose_to(out_ref, blk):
    for c in range(0, blk.shape[1], 256):
        out_ref[c:c + 256, :] = blk[:, c:c + 256].astype(F32).T


def assemble_main_kernel(*refs, stages, n_q):
    ins, (y_ref, gh_ref, wq_ref, wo_ref, y_out, gh_out) = refs[:stages], refs[stages:]
    y_out[:] = y_ref[:]
    gh_out[:] = gh_ref[:]
    for s in range(stages):
        @pl.when(pl.program_id(1) == s)
        def _(ref=ins[s]):
            _, chips, n, d = ref.shape
            transpose_to(wq_ref, ref[0, :, 0:n_q].reshape(chips * n_q, d))
            wo_ref[:] = ref[0, :, n_q:n].astype(F32)


def assemble_tail_kernel(in_ref, _, out_ref):
    chips, _, n, d = in_ref.shape
    transpose_to(out_ref, in_ref[:, 0].reshape(chips * n, d))


def solution(mesh):
    chips = mesh.shape['sp'] // CORES
    mesh2 = Mesh(mesh.devices.reshape(mesh.shape['dp'], chips, CORES), ('dp', 'x', 'core'))
    swap = [(i, CORES - 1 - i) for i in range(CORES)]

    def device_step(hidden, norm_w, w_qkv, w_out, long_factor, grad_out):
        n_batch, tok, d = hidden.shape
        n_heads, e = w_out.shape[0], w_out.shape[1]
        kv_heads = (w_qkv.shape[1] // e - n_heads) // 2
        reps = n_heads // kv_heads
        stages = kv_heads // CORES
        rows = reps * e
        q_half = stages * rows
        kv_half = stages * e
        e2 = PAIR * e
        half_rot = long_factor.shape[0]
        chip = lax.axis_index('x')
        core = lax.axis_index('core')
        ids = jnp.stack([chip, core]).astype(jnp.int32)
        tiles = 2
        nb = n_batch // tiles

        x_par = lax.ppermute(hidden, 'core', swap)
        go_par = lax.ppermute(grad_out, 'core', swap)
        w_o = w_out.reshape(n_heads * e, d)
        norm2 = norm_w.reshape(1, d)

        exponent = jnp.arange(half_rot, dtype=F32) / half_rot
        inv_freq = 1.0 / (long_factor * jnp.power(ROPE_BASE, exponent))
        sides = jnp.stack([core, 1 - core])
        positions = ((chip * CORES + sides)[:, None] * tok + jnp.arange(tok)[None, :]).astype(F32)
        angles = inv_freq[None, :, None] * positions[:, None, :]
        cos_t, sin_t = jnp.cos(angles) * ROPE_GAIN, jnp.sin(angles) * ROPE_GAIN

        tok_spec = along(0, nb, tok, d)
        rot_spec = whole(half_rot, tok)

        def kv_proj(x, side, filled):
            kb = PAIR * q_half // kv_half
            kt = 4
            kn = n_batch // kt
            x_spec = along(0, kn, tok, d)
            any_spec = pl.BlockSpec(memory_space=pl.ANY)
            return pl.pallas_call(
                drop_scalar(kv_proj_kernel),
                out_shape=[jax.ShapeDtypeStruct((n_batch, tok, d), BF16)]
                + [jax.ShapeDtypeStruct((2, n_batch, e2, tok), BF16)] * stages,
                grid_spec=pltpu.PrefetchScalarGridSpec(
                    num_scalar_prefetch=1, grid=(kt,),
                    in_specs=[x_spec, whole(1, d),
                              pl.BlockSpec((d, kv_half), lambda i, c: (0, kb + c[1])),
                              pl.BlockSpec((d, kv_half), lambda i, c: (0, kb + CORES + c[1])), rot_spec, rot_spec]
                    + [any_spec] * len(filled),
                    out_specs=[x_spec] + [pl.BlockSpec((1, kn, e2, tok), lambda i, _: (side, i, 0, 0))] * stages),
                input_output_aliases={7 + i: 1 + i for i in range(len(filled))},
                compiler_params=params(), name='kv_proj',
                cost_estimate=cost(PAIR * n_batch * tok * d * PAIR * kv_half, 3 * n_batch * tok * d * 2),
            )(ids, x, norm2, w_qkv, w_qkv, cos_t[side], sin_t[side], *filled)

        first = lambda i: jnp.minimum(i, tiles - 1)
        second = lambda i: jnp.maximum(i - tiles, 0)
        own_spec = pl.BlockSpec((nb, tok, d), lambda i, _: (first(i), 0, 0))
        par_spec = pl.BlockSpec((nb, tok, d), lambda i, _: (second(i), 0, 0))
        own_out = pl.BlockSpec((nb, q_half, tok), lambda i, _: (first(i), 0, 0))
        par_out = pl.BlockSpec((nb, q_half, tok), lambda i, _: (second(i), 0, 0))
        both_rot = whole(2, half_rot, tok)
        q_shapes = (jax.ShapeDtypeStruct((n_batch, q_half, tok), BF16), jax.ShapeDtypeStruct((n_batch, q_half, tok), BF16))

        def q_proj(h0, h1):
            return pl.pallas_call(
                drop_scalar(q_proj_kernel), out_shape=q_shapes,
                grid_spec=pltpu.PrefetchScalarGridSpec(
                    num_scalar_prefetch=1, grid=(PAIR * tiles,),
                    in_specs=[own_spec, par_spec, pl.BlockSpec((d, q_half), lambda i, c: (0, c[1])), both_rot, both_rot],
                    out_specs=(own_out, par_out)),
                compiler_params=params(), name='q_proj',
                cost_estimate=cost(4 * n_batch * tok * d * q_half, 6 * n_batch * tok * d * 2),
            )(ids, h0, h1, w_qkv, cos_t, sin_t)

        def do_proj(g0, g1):
            return pl.pallas_call(
                drop_scalar(do_proj_kernel), out_shape=q_shapes,
                grid_spec=pltpu.PrefetchScalarGridSpec(
                    num_scalar_prefetch=1, grid=(PAIR * tiles,),
                    in_specs=[own_spec, par_spec, pl.BlockSpec((q_half, d), lambda i, c: (c[1], 0))],
                    out_specs=(own_out, par_out)),
                compiler_params=params(), name='do_proj',
                cost_estimate=cost(4 * n_batch * tok * d * q_half, 6 * n_batch * tok * d * 2),
            )(ids, g0, g1, w_o)

        h_own, *kv_sides = kv_proj(hidden, 0, [])
        h_par, *kv_sides = kv_proj(x_par, 1, kv_sides)
        gathered = []
        for s in range(stages):
            gathered.append(lax.all_gather(kv_sides[s], 'x'))
        q_own, q_par = q_proj(h_own, h_par)
        do_own, do_par = do_proj(grad_out, go_par)

        n_g = PAIR * rows // chips
        n_s = e2 + n_g
        hbm = pl.BlockSpec(memory_space=pl.ANY)
        shard_spec = lambda n: whole(n, d)

        def gathered_shape(n):
            return jax.ShapeDtypeStruct((CORES, chips, n, d), BF16)

        def attention(s, prev, shard):
            blk = PAIR * tok
            has_sum, has_gather = prev is not None, shard is not None
            q_spec = pl.BlockSpec((1, rows, tok), lambda b: (b, s, 0))
            t_spec = pl.BlockSpec((2, tok, d), lambda b: (b // 2, 0, 0))
            r_spec = whole(2, half_rot, tok)
            o_spec = along(1, 2, 1, rows, tok)
            return pl.pallas_call(
                functools.partial(attn_kernel, has_sum=has_sum, has_gather=has_gather),
                out_shape=[jax.ShapeDtypeStruct((2, n_batch, rows, tok), BF16)] * 2
                + [jax.ShapeDtypeStruct((chips, n_s, d), BF16)]
                + [jax.ShapeDtypeStruct((n_s, d), BF16)] * has_sum + [gathered_shape(n_g)] * has_gather,
                grid=(n_batch,),
                in_specs=[q_spec, q_spec, q_spec, q_spec, along(2, chips, 2, 1, e2, tok),
                          t_spec, t_spec, t_spec, t_spec, r_spec, r_spec]
                + [hbm] * has_sum + [shard_spec(n_g)] * has_gather,
                out_specs=[o_spec, o_spec, whole(chips, n_s, d)]
                + [shard_spec(n_s)] * has_sum + [hbm] * has_gather,
                scratch_shapes=[pltpu.VMEM((chips, blk, reps * blk), F32), pltpu.VMEM((chips, blk, reps * blk), BF16),
                                pltpu.VMEM((chips, blk, reps * blk), BF16), pltpu.VMEM((e, reps * blk), F32),
                                pltpu.VMEM((8, reps * blk), F32),
                                pltpu.VMEM((chips, blk, e2), BF16), pltpu.VMEM((2, PAIR * rows, blk), BF16),
                                pltpu.VMEM((PAIR * rows, d), F32)]
                + (RingSum.scratch(chips, n_s, d) if has_sum else []) + (RingGather.scratch() if has_gather else []),
                compiler_params=comm_params(s) if has_sum else params(),
                cost_estimate=cost(4e10, 3e7, 3e7),
            )(q_own, q_par, do_own, do_par, gathered[s], h_own, h_par, grad_out, go_par, cos_t, sin_t,
              *([prev] if has_sum else []), *([shard] if has_gather else []))

        own, par, totals, main = [], [], [], []
        prev = None
        for s in range(stages):
            shard = totals[s - 2][e2:] if s >= 2 else None
            outs = attention(s, prev, shard)
            own.append(outs[0])
            par.append(lax.ppermute(outs[1], 'core', swap))
            prev = outs[2]
            totals += outs[3:4]
            main += outs[4:5]

        nb2 = 2
        t2_spec = along(0, nb2, tok, d)
        block_out, total = pl.pallas_call(
            functools.partial(out_kernel, stages=stages),
            out_shape=[jax.ShapeDtypeStruct((n_batch, tok, d), BF16), jax.ShapeDtypeStruct((n_s, d), BF16)],
            grid=(n_batch // nb2,),
            in_specs=[t2_spec, whole(n_heads * e, d), hbm]
            + [along(1, 1, nb2, rows, tok)] * (PAIR * stages),
            out_specs=[t2_spec, shard_spec(n_s)],
            scratch_shapes=[pltpu.VMEM((nb2 * tok, n_heads * e), BF16)] + RingSum.scratch(chips, n_s, d),
            compiler_params=comm_params(stages), name='out_proj',
            cost_estimate=cost(PAIR * n_batch * tok * d * n_heads * e, 3e7),
        )(hidden, w_o, prev, *own, *par)
        totals.append(total)

        gb = 2
        gf_spec = along(0, gb, stages * e2, tok)
        n_kv = stages * e2 // chips
        kv_own_g, kv_par_g, send_kv, main_2 = pl.pallas_call(
            functools.partial(kv_grad_kernel, stages=stages),
            out_shape=[jax.ShapeDtypeStruct((n_batch, stages * e2, tok), BF16)] * 2
            + [jax.ShapeDtypeStruct((chips, n_kv, d), BF16), gathered_shape(n_g)],
            grid=(n_batch // gb,),
            in_specs=[along(1, e2, PAIR * tok * gb)] * stages
            + [along(0, gb, tok, d)] * 2 + [whole(2, half_rot, tok)] * 2
            + [shard_spec(n_g)],
            out_specs=[gf_spec, gf_spec, whole(chips, n_kv, d), hbm],
            scratch_shapes=[pltpu.VMEM((stages * e2, d), F32)] + RingGather.scratch(),
            compiler_params=comm_params(stages + 1), name='kv_grad',
            cost_estimate=cost(PAIR * PAIR * n_batch * tok * d * stages * e2, 3e7),
        )(*totals, h_own, h_par, cos_t, sin_t, totals[-2][e2:])
        main.append(main_2)
        kv_other_g = lax.ppermute(kv_par_g, 'core', swap)

        nb3 = 2
        t3_spec = along(0, nb3, tok, d)
        grad_hidden, gn, shard_kv, main_3 = pl.pallas_call(
            functools.partial(norm_grad_kernel, stages=stages),
            out_shape=[jax.ShapeDtypeStruct((n_batch, tok, d), BF16), jax.ShapeDtypeStruct((8, d), F32),
                       jax.ShapeDtypeStruct((n_kv, d), BF16), gathered_shape(n_g)],
            grid=(n_batch // nb3,),
            in_specs=[t3_spec, t3_spec, whole(1, d), whole(*w_qkv.shape)]
            + [along(0, nb3, stages * e2, tok)] * 2 + [hbm, shard_spec(n_g)]
            + [pl.BlockSpec((1, nb3, rows, tok), lambda b: (1, b, 0, 0))] * (PAIR * stages),
            out_specs=[t3_spec, whole(8, d), shard_spec(n_kv), hbm],
            scratch_shapes=[pltpu.VMEM((nb3 * tok, w_qkv.shape[1]), BF16), pltpu.VMEM((nb3 * tok, d), F32)]
            + RingSum.scratch(chips, n_kv, d) + RingGather.scratch(),
            compiler_params=comm_params(stages + 2), name='norm_grad',
            cost_estimate=cost(PAIR * n_batch * tok * d * w_qkv.shape[1], 4e7),
        )(hidden, grad_out, norm2, w_qkv, kv_own_g, kv_other_g, send_kv, totals[-1][e2:], *own, *par)
        main.append(main_3)

        gn_row = jnp.sum(gn, axis=0, keepdims=True)
        gn_hi = gn_row.astype(BF16)
        gn_lo = (gn_row - gn_hi.astype(F32)).astype(BF16)
        n_t = n_kv + 16
        tail_block = cat_rows([shard_kv, gn_hi, gn_lo, jnp.zeros((n_t - n_kv - 2, d), BF16)])
        tail = lax.all_gather(tail_block, ('x', 'core')).reshape(chips, CORES, n_t, d)
        n_q = rows // chips
        b_spec = pl.BlockSpec((n_batch // (CORES * stages), tok, d), lambda p, s: (p * stages + s, 0, 0))
        w_cols, grad_w_out, block_out, grad_hidden = pl.pallas_call(
            functools.partial(assemble_main_kernel, stages=stages, n_q=n_q),
            out_shape=[jax.ShapeDtypeStruct(w_qkv.shape, F32), jax.ShapeDtypeStruct((n_heads, e, d), F32)]
            + [jax.ShapeDtypeStruct((n_batch, tok, d), BF16)] * PAIR,
            grid=(CORES, stages),
            in_specs=[along(0, 1, chips, n_g, d)] * stages + [b_spec] * PAIR,
            out_specs=[pl.BlockSpec((d, rows), lambda p, s: (0, p * stages + s)),
                       pl.BlockSpec((reps, e, d), lambda p, s: (p * stages + s, 0, 0)), b_spec, b_spec],
            compiler_params=params(2), name='assemble_main', cost_estimate=cost(2e9, 6e7),
        )(*main, block_out, grad_hidden)
        kcol = PAIR * q_half // kv_half
        grad_w_qkv = pl.pallas_call(
            assemble_tail_kernel,
            out_shape=jax.ShapeDtypeStruct(w_qkv.shape, F32),
            grid=(CORES, 2),
            in_specs=[pl.BlockSpec((chips, 1, e, d), lambda p, k: (0, p, k, 0)), pl.BlockSpec(memory_space=pl.ANY)],
            out_specs=pl.BlockSpec((d, kv_half), lambda p, k: (0, kcol + k * CORES + p)),
            input_output_aliases={1: 0},
            compiler_params=params(2), name='assemble_tail', cost_estimate=cost(1e9, 2e7),
        )(tail, w_cols)
        gn_all = tail[:, :, n_kv:n_kv + 2].astype(F32)
        grad_norm_w = jnp.sum(gn_all, axis=(0, 1, 2))
        return block_out, grad_hidden, grad_w_qkv, grad_w_out, grad_norm_w

    tok_spec = P('dp', ('x', 'core'), None)
    return jax.shard_map(device_step, mesh=mesh2,
                         in_specs=(tok_spec, P(), P(), P(), P(), tok_spec),
                         out_specs=(tok_spec, tok_spec, P('dp', None), P('dp', None, None), P('dp')),
                         check_vma=False)
```

time: 616 us -> 493 us (0.80)
  blocking collectives: 239 us -> 0 us
  Pallas kernels: 227 us -> 435 us
  waiting for transfers between devices: 68.1 us -> 16 us
  starting transfers between devices: 40.6 us -> 2.49 us
    all_to_all x4 -> x0, blocking collectives: 239 us -> none  [the longest x3 214 us: device_step(): recv.append(lax.all_to_all(sends[0], 'x', 0, 0, tiled=True))]
    pallas_call x5, Pallas kernels: 111 us -> 282 us  [the longest x4 237 us: attention(): pl.pallas_call(functools.partial(attn_kernel, has_sum=has_sum, has_gather...]
    all_to_all x2 -> x0, waiting for transfers between devices: 66.2 us -> none  [the longest x1 65.8 us: device_step(): recv.append(lax.all_to_all(sends[0], 'x', 0, 0, tiled=True))]
    all_to_all x2 -> x0, starting transfers between devices: 38.3 us -> none  [the longest x1 34.5 us: device_step(): recv.append(lax.all_to_all(sends[0], 'x', 0, 0, tiled=True))]
    pallas_call x1, Pallas kernels: 11.8 us -> 28.2 us  [device_step(): pl.pallas_call(functools.partial(kv_grad_kernel, stages=stages), out_shap...]
    pallas_call x1, Pallas kernels: 31.6 us -> 47.8 us  [device_step(): pl.pallas_call(functools.partial(norm_grad_kernel, stages=stages), out_sh...]
    reduce_sum x5 -> x0, other arithmetic: 7.09 us -> none  [the longest x4 6.66 us: device_step(): jnp.sum(r.astype(F32), axis=0).astype(BF16)]
    slice x0 -> x4, local copies, waits for them, and re-layouts: none -> 6.49 us  [the longest x2 3.76 us: device_step(): shard = totals[s - 2][e2:] if s >= 2 else None]
  transfers between devices with their start and end apart: 18 -> 12, of which waited for: 2 -> 6; matrix products, arithmetic and copies ran while one was open for 2% -> 2% of each run, Pallas kernels for 35% -> 49%
where the time goes in v4:
time: 493 us; the launch traced here: 484 us
  Pallas kernels  435 us (88%)
  waiting for transfers between devices  16 us (3%)
  between operations  14.1 us (3%)
  local copies, waits for them, and re-layouts  10.5 us (2%)
  other arithmetic  6.2 us (1%)
    pallas_call x4, Pallas kernels, attention(): pl.pallas_call(functools.partial(attn_kernel, has_sum=has_sum, has_gather...  237 us
    pallas_call x1, Pallas kernels, device_step(): pl.pallas_call(functools.partial(norm_grad_kernel, stages=stages), out_sh...  47.8 us
    pallas_call x1, Pallas kernels, device_step(): pl.pallas_call(functools.partial(out_kernel, stages=stages), out_shape=[j...  44.6 us
    pallas_call x1, Pallas kernels, device_step(): pl.pallas_call(functools.partial(kv_grad_kernel, stages=stages), out_shap...  28.2 us
    pallas_call x1, Pallas kernels, device_step(): pl.pallas_call(functools.partial(assemble_main_kernel, stages=stages, n_q...  24.1 us
    pallas_call x1, Pallas kernels, q_proj(): pl.pallas_call(drop_scalar(q_proj_kernel), out_shape=q_shapes, grid_spec=...  15.9 us
    pallas_call x2, Pallas kernels, kv_proj(): pl.pallas_call(drop_scalar(kv_proj_kernel), out_shape=[jax.ShapeDtypeStru...  15.7 us
    pallas_call x1, Pallas kernels, do_proj(): pl.pallas_call(drop_scalar(do_proj_kernel), out_shape=q_shapes, grid_spec...  15.2 us
  transfers between devices with their start and end apart: 12, of which 6 were waited for; matrix products, arithmetic and copies ran while one was open for 2% of the time, Pallas kernels for 49%

profile of v4, /device:TPU:112, one launch (start us, length us, event | category | flops | bytes accessed | tf_op | source)
XLA Modules:
  0.0 484.5 jit_solution(6827973163430939994)
XLA Ops:
  11.0 7.8 %kv_proj.2 = (bf16[8,128,2048]{2,1,0:T(8,128)(2,1)}, bf16[2,8,128,128]{3,2,1,0:T(8,128)(2,1)}, bf16[2,8,128,128]{3,2,1,0:T(8,128)(2,1)}, bf16[2,8,128,128]{3,2,1,0:T(8,128)(2,1)}, bf16[2,8,128,128]{3,2,1,0:T(8,128)(2,1)}) custom-call(s32[2]{0:T(128)} %pad_add_fusion._, bf16[8,128,2048]{2,1,0:T(8,128)(2,1)} %x_ref.3, bf16[1,2048]{1,0:T(2,128)(2,1)} %reshape.81.refs_1_.g_ref, ...), custom_call_target="tpu_custom_call" | custom-call | flops 2147483648 | bytes 12582912 | tf_op jit(solution)/shard_map/kv_proj/pallas_call | solution.py:619
  18.8 7.9 %kv_proj.3 = (bf16[8,128,2048]{2,1,0:T(8,128)(2,1)}, bf16[2,8,128,128]{3,2,1,0:T(8,128)(2,1)}, bf16[2,8,128,128]{3,2,1,0:T(8,128)(2,1)}, bf16[2,8,128,128]{3,2,1,0:T(8,128)(2,1)}, bf16[2,8,128,128]{3,2,1,0:T(8,128)(2,1)}) custom-call(s32[2]{0:T(128)} %pad_add_fusion._, ...), custom_call_target="tpu_custom_call", output_to_operand_aliasing={{1}: (7, {}), {2}: (8, {}), {3}: (9, {}), {4}: (10, {})} | custom-call | flops 2147483648 | bytes 12582912 | tf_op jit(solution)/shard_map/kv_proj/pallas_call | solution.py:619
  29.1 15.9 %q_proj.1 = (bf16[8,1024,128]{2,1,0:T(8,128)(2,1)}, bf16[8,1024,128]{2,1,0:T(8,128)(2,1)}) custom-call(s32[2]{0:T(128)} %pad_add_fusion._, bf16[8,128,2048]{2,1,0:T(8,128)(2,1)} %get-tuple-element.50.refs_0_.h0_ref.refs_4_, bf16[8,128,2048]{2,1,0:T(8,128)(2,1)} %get-tuple-element.55.refs_1_.h1_ref.refs_5_, bf16[2048,3072]{1,0:T(8,128)(2,1)} %w_ref.1, ...), custom_call_target="tpu_custom_call" | custom-call | flops 8589934592 | bytes 25165824 | tf_op jit(solution)/shard_map/q_proj/pallas_call | solution.py:645
  44.9 15.2 %do_proj.1 = (bf16[8,1024,128]{2,1,0:T(8,128)(2,1)}, bf16[8,1024,128]{2,1,0:T(8,128)(2,1)}) custom-call(s32[2]{0:T(128)} %pad_add_fusion._, bf16[8,128,2048]{2,1,0:T(8,128)(2,1)} %go_ref.1, bf16[8,128,2048]{2,1,0:T(8,128)(2,1)} %collective-permute-done.1.refs_1_.g1_ref, bf16[2048,2048]{1,0:T(8,128)(2,1)} %bitcast.22), custom_call_target="tpu_custom_call" | custom-call | flops 8589934592 | bytes 25165824 | tf_op jit(solution)/shard_map/do_proj/pallas_call | solution.py:656
  60.1 23.0 %shard_map.101 = (bf16[2,8,256,128]{3,2,1,0:T(8,128)(2,1)}, bf16[2,8,256,128]{3,2,1,0:T(8,128)(2,1)}, bf16[4,256,2048]{2,1,0:T(8,128)(2,1)}) custom-call(bf16[8,1024,128]{2,1,0:T(8,128)(2,1)} %get-tuple-element.56.q0_ref, bf16[8,1024,128]{2,1,0:T(8,128)(2,1)} %get-tuple-element.57.q1_ref, bf16[8,1024,128]{2,1,0:T(8,128)(2,1)} %get-tuple-element.58.do0_ref, ...), custom_call_target="tpu_custom_call" | custom-call | flops 40000000000 | bytes 30000000 | tf_op jit(solution)/shard_map/pallas_call | solution.py:689
  83.1 1.8 all-gather.13.cloned.1.call-done
  84.9 89.2 %shard_map.102 = (bf16[2,8,256,128]{3,2,1,0:T(8,128)(2,1)}, bf16[2,8,256,128]{3,2,1,0:T(8,128)(2,1)}, bf16[4,256,2048]{2,1,0:T(8,128)(2,1)}, bf16[256,2048]{1,0:T(8,128)(2,1)}) custom-call(bf16[8,1024,128]{2,1,0:T(8,128)(2,1)} %get-tuple-element.56.q0_ref, bf16[8,1024,128]{2,1,0:T(8,128)(2,1)} %get-tuple-element.57.q1_ref, ...), custom_call_target="tpu_custom_call" | custom-call | flops 40000000000 | bytes 30000000 | tf_op jit(solution)/shard_map/pallas_call | solution.py:689
  174.1 1.9 slice.31.refs_1_
  176.0 62.6 %shard_map.103 = (bf16[2,8,256,128]{3,2,1,0:T(8,128)(2,1)}, bf16[2,8,256,128]{3,2,1,0:T(8,128)(2,1)}, bf16[4,256,2048]{2,1,0:T(8,128)(2,1)}, bf16[256,2048]{1,0:T(8,128)(2,1)}, bf16[2,4,128,2048]{3,2,1,0:T(8,128)(2,1)}) custom-call(bf16[8,1024,128]{2,1,0:T(8,128)(2,1)} %get-tuple-element.56.q0_ref, bf16[8,1024,128]{2,1,0:T(8,128)(2,1)} %get-tuple-element.57.q1_ref, ...), custom_call_target="tpu_custom_call" | custom-call | flops 40000000000 | bytes 30000000 | tf_op jit(solution)/shard_map/pallas_call | solution.py:689
  238.6 1.9 slice.32.refs_1_
  240.5 62.7 %shard_map.104 = (bf16[2,8,256,128]{3,2,1,0:T(8,128)(2,1)}, bf16[2,8,256,128]{3,2,1,0:T(8,128)(2,1)}, bf16[4,256,2048]{2,1,0:T(8,128)(2,1)}, bf16[256,2048]{1,0:T(8,128)(2,1)}, bf16[2,4,128,2048]{3,2,1,0:T(8,128)(2,1)}) custom-call(bf16[8,1024,128]{2,1,0:T(8,128)(2,1)} %get-tuple-element.56.q0_ref, bf16[8,1024,128]{2,1,0:T(8,128)(2,1)} %get-tuple-element.57.q1_ref, ...), custom_call_target="tpu_custom_call" | custom-call | flops 40000000000 | bytes 30000000 | tf_op jit(solution)/shard_map/pallas_call | solution.py:689
  304.3 1.9 slice.33.refs_8_
  306.2 1.5 collective-permute-done.4.refs_6_
  307.6 1.5 collective-permute-done.3.refs_5_
  309.1 1.5 collective-permute-done.2.refs_4_
  311.6 44.6 %out_proj.1 = (bf16[8,128,2048]{2,1,0:T(8,128)(2,1)}, bf16[256,2048]{1,0:T(8,128)(2,1)}) custom-call(bf16[8,128,2048]{2,1,0:T(8,128)(2,1)} %x_ref.3, bf16[2048,2048]{1,0:T(8,128)(2,1)} %bitcast.23, bf16[4,256,2048]{2,1,0:T(8,128)(2,1)} %get-tuple-element.72.prev_ref, bf16[2,8,256,128]{3,2,1,0:T(8,128)(2,1)} %get-tuple-element.73.refs_0_, ...), custom_call_target="tpu_custom_call" | custom-call | flops 8589934592 | bytes 30000000 | tf_op jit(solution)/shard_map/out_proj/pallas_call | solution.py:724
  356.2 28.2 %kv_grad.1 = (bf16[8,512,128]{2,1,0:T(8,128)(2,1)}, bf16[8,512,128]{2,1,0:T(8,128)(2,1)}, bf16[4,128,2048]{2,1,0:T(8,128)(2,1)}, bf16[2,4,128,2048]{3,2,1,0:T(8,128)(2,1)}) custom-call(bf16[256,2048]{1,0:T(8,128)(2,1)} %get-tuple-element.65.refs_0_, bf16[256,2048]{1,0:T(8,128)(2,1)} %get-tuple-element.69.refs_1_, ...), custom_call_target="tpu_custom_call" | custom-call | flops 4294967296 | bytes 30000000 | tf_op jit(solution)/shard_map/kv_grad/pallas_call | solution.py:740
  385.8 1.6 collective-permute-done.6.kv1_ref
  388.4 47.8 %norm_grad.1 = (bf16[8,128,2048]{2,1,0:T(8,128)(2,1)}, f32[8,2048]{1,0:T(8,128)}, bf16[128,2048]{1,0:T(8,128)(2,1)}, bf16[2,4,128,2048]{3,2,1,0:T(8,128)(2,1)}) custom-call(bf16[8,128,2048]{2,1,0:T(8,128)(2,1)} %x_ref.3, bf16[8,128,2048]{2,1,0:T(8,128)(2,1)} %go_ref.1, bf16[1,2048]{1,0:T(2,128)(2,1)} %reshape.81.refs_1_.g_ref, bf16[2048,3072]{1,0:T(8,128)(2,1)} %w_ref.1, ...), custom_call_target="tpu_custom_call" | custom-call | flops 12884901888 | bytes 40000000 | tf_op jit(solution)/shard_map/norm_grad/pallas_call | solution.py:758
  437.1 2.0 maximum_maximum_fusion
  439.2 24.1 %assemble_main.1 = (f32[2048,3072]{1,0:T(8,128)}, f32[32,64,2048]{2,1,0:T(8,128)}, bf16[8,128,2048]{2,1,0:T(8,128)(2,1)}, bf16[8,128,2048]{2,1,0:T(8,128)(2,1)}) custom-call(bf16[2,4,128,2048]{3,2,1,0:T(8,128)(2,1)} %get-tuple-element.66.refs_0_, bf16[2,4,128,2048]{3,2,1,0:T(8,128)(2,1)} %get-tuple-element.70.refs_1_, ...), custom_call_target="tpu_custom_call" | custom-call | flops 2000000000 | bytes 60000000 | tf_op jit(solution)/shard_map/assemble_main/pallas_call | solution.py:782
  463.2 6.5 %all-gather.19.cloned.1.call-done = bf16[1152,2048]{1,0:T(8,128)(2,1)} async-done(((bf16[144,2048]{1,0:T(8,128)(2,1)}), bf16[1152,2048]{1,0:T(8,128)(2,1)}) %all-gather.19.cloned.1.call-update) | async-done | bytes 4718608 | tf_op jit(solution)/shard_map/all_gather | solution.py:779
  469.8 1.6 convert_reduce_fusion
  471.4 6.4 %assemble_tail.1 = f32[2048,3072]{1,0:T(8,128)} custom-call(bf16[4,2,144,2048]{3,2,1,0:T(8,128)(2,1)} %bitcast.19, f32[2048,3072]{1,0:T(8,128)} %get-tuple-element.93._), custom_call_target="tpu_custom_call", output_to_operand_aliasing={{}: (1, {})} | custom-call | flops 1000000000 | bytes 20000000 | tf_op jit(solution)/shard_map/assemble_tail/pallas_call | solution.py:793
  (54 shorter events, 11.4 us)
Async XLA Ops:
  7.2 52.9 %all-gather.15.cloned.1.call-start = ((), (), s32[]{:S(2)}) async-start(), calls=%async_computation.2 | async-start | bytes 2621440 | tf_op jit(solution)/shard_map/all_gather | solution.py:670
  7.2 11.6 %collective-permute-start = (bf16[8,128,2048]{2,1,0:T(8,128)(2,1)}, bf16[8,128,2048]{2,1,0:T(8,128)(2,1)}, u32[]{:S(2)}, u32[]{:S(2)}) collective-permute-start(bf16[8,128,2048]{2,1,0:T(8,128)(2,1)} %x_ref.3), channel_id=1, source_target_pairs={{0,1},{1,0},{2,3},{3,2},{4,5},{5,4},{6,7},{7,6},{8,9},{9,8},{10,11... | collective-permute-start | bytes 12582920 | tf_op jit(solution)/shard_map/ppermute | solution.py:598
  10.3 8.5 %copy-start.1 = (f32[2,32,128]{2,1,0:T(8,128)}, f32[2,32,128]{2,1,0:T(8,128)S(1)}, u32[]{:S(2)}) copy-start(f32[2,32,128]{2,1,0:T(8,128)S(1)} %get-tuple-element.99.refs_4_.sin_ref.refs_7_) | copy-start | bytes 98308
  10.3 8.5 %copy-start.2 = (f32[2,32,128]{2,1,0:T(8,128)}, f32[2,32,128]{2,1,0:T(8,128)S(1)}, u32[]{:S(2)}) copy-start(f32[2,32,128]{2,1,0:T(8,128)S(1)} %get-tuple-element.100.refs_3_.cos_ref.refs_6_) | copy-start | bytes 98308
  26.8 58.1 %all-gather.13.cloned.1.call-start = ((), (), s32[]{:S(2)}) async-start(), calls=%async_computation.1 | async-start | bytes 2621440 | tf_op jit(solution)/shard_map/all_gather | solution.py:670
  27.6 148.4 %all-gather.11.cloned.1.call-start = ((), (), s32[]{:S(2)}) async-start(), calls=%async_computation | async-start | bytes 2621440 | tf_op jit(solution)/shard_map/all_gather | solution.py:670
  27.7 17.3 %collective-permute-start.1 = (bf16[8,128,2048]{2,1,0:T(8,128)(2,1)}, bf16[8,128,2048]{2,1,0:T(8,128)(2,1)}, u32[]{:S(2)}, u32[]{:S(2)}) collective-permute-start(bf16[8,128,2048]{2,1,0:T(8,128)(2,1)} %go_ref.1), channel_id=1, source_target_pairs={{0,1},{1,0},{2,3},{3,2},{4,5},{5,4},{6,7},{7,6},{8,9},{9,8},{10,11... | collective-permute-start | bytes 12582920 | tf_op jit(solution)/shard_map/ppermute | solution.py:599
  28.4 212.1 %all-gather.17.cloned.1.call-start = ((), (), s32[]{:S(2)}) async-start(), calls=%async_computation.3 | async-start | bytes 2621440 | tf_op jit(solution)/shard_map/all_gather | solution.py:670
  29.0 440.8 %all-gather.19.cloned.1.call-start = ((), (), s32[]{:S(2)}) async-start(), calls=%async_computation.4 | async-start | bytes 5308416 | tf_op jit(solution)/shard_map/all_gather | solution.py:779
  240.5 63.7 %copy-start.3 = (bf16[2,8,256,128]{3,2,1,0:T(8,128)(2,1)S(1)}, bf16[2,8,256,128]{3,2,1,0:T(8,128)(2,1)}, u32[]{:S(2)}) copy-start(bf16[2,8,256,128]{3,2,1,0:T(8,128)(2,1)} %get-tuple-element.77) | copy-start | bytes 3145732
  303.2 3.0 collective-permute-start.5
  303.6 4.0 collective-permute-start.4
  303.7 5.4 %collective-permute-start.3 = (bf16[2,8,256,128]{3,2,1,0:T(8,128)(2,1)}, bf16[2,8,256,128]{3,2,1,0:T(8,128)(2,1)S(1)}, u32[]{:S(2)}, u32[]{:S(2)}) collective-permute-start(bf16[2,8,256,128]{3,2,1,0:T(8,128)(2,1)} %get-tuple-element.78), channel_id=1, source_target_pairs={{0,1},{1,0},{2,3},{3,2},{4,5},{5,4},{6,7},{7,6},{8,9},{9,8},{10,11... | collective-permute-start | bytes 3145736 | tf_op jit(solution)/shard_map/ppermute | solution.py:717
  304.1 6.5 %collective-permute-start.2 = (bf16[2,8,256,128]{3,2,1,0:T(8,128)(2,1)S(1)}, bf16[2,8,256,128]{3,2,1,0:T(8,128)(2,1)S(1)}, u32[]{:S(2)}, u32[]{:S(2)}) collective-permute-start(bf16[2,8,256,128]{3,2,1,0:T(8,128)(2,1)S(1)} %copy-done.3), channel_id=1, source_target_pairs={{0,1},{1,0},{2,3},{3,2},{4,5},{5,4},{6,7},{7,6},{8,9},{9,8},{10,11... | collective-permute-start | bytes 3145736 | tf_op jit(solution)/shard_map/ppermute | solution.py:717
  306.2 5.4 %copy-start.4 = (bf16[2,8,256,128]{3,2,1,0:T(8,128)(2,1)}, bf16[2,8,256,128]{3,2,1,0:T(8,128)(2,1)S(1)}, u32[]{:S(2)}) copy-start(bf16[2,8,256,128]{3,2,1,0:T(8,128)(2,1)S(1)} %collective-permute-done.5.refs_7_) | copy-start | bytes 3145732
  307.6 4.0 copy-start.5
  309.1 1.5 copy-start.6
  310.6 1.0 copy-start.7
  356.2 28.8 %copy-start = (bf16[256,2048]{1,0:T(8,128)(2,1)S(1)}, bf16[256,2048]{1,0:T(8,128)(2,1)}, u32[]{:S(2)}) copy-start(bf16[256,2048]{1,0:T(8,128)(2,1)} %get-tuple-element.81.refs_3_) | copy-start | bytes 3145732
  384.4 3.0 collective-permute-start.6
  387.4 1.0 copy-start.8
Sparse Core Ops, SparseCore 0:
  26.9 29.6 all-gather.14
  58.2 26.6 all-gather.12
  86.5 27.0 all-gather.10
  114.9 43.2 all-gather.16
  439.3 30.4 all-gather.18

commit v5 on v4

--- a/solution.py
+++ b/solution.py
@@ -129,110 +129,84 @@
 
 
 def ring_barrier(chips):
-    _, right, left, _, _, mate = ring_peers(chips)
+    _, right, left, _, _, _ = ring_peers(chips)
     sem = pltpu.get_barrier_semaphore()
-    for who in ({'x': right}, {'x': left}, {'core': mate}):
-        pl.semaphore_signal(sem, inc=1, device_id=who, device_id_type=pl.DeviceIdType.MESH)
-    pl.semaphore_wait(sem, 3)
+    for who in (right, left):
+        pl.semaphore_signal(sem, inc=1, device_id={'x': who}, device_id_type=pl.DeviceIdType.MESH)
+    pl.semaphore_wait(sem, 2)
 
 
 class RingSum:
     @staticmethod
-    def scratch(chips, rows, d):
+    def scratch(rows, d):
         half = rows // 2
-        return [pltpu.VMEM((2, half, d), BF16), pltpu.VMEM((2, half, d), BF16), pltpu.VMEM((rows, d), BF16),
-                pltpu.VMEM((2, rows, d), BF16), pltpu.SemaphoreType.DMA((6,)), pltpu.SemaphoreType.DMA((6,)),
+        return [pltpu.VMEM((PAIR, half, d), BF16), pltpu.VMEM((PAIR, half, d), BF16), pltpu.VMEM((rows, d), BF16),
+                pltpu.VMEM((PAIR, rows, d), BF16), pltpu.SemaphoreType.DMA((6,)), pltpu.SemaphoreType.DMA((6,)),
                 pltpu.SemaphoreType.DMA((3,))]
 
-    def __init__(self, send_ref, total_ref, mid, buf, own, recv, s_sem, r_sem, l_sem):
-        chips, rows, _ = send_ref.shape
+    def __init__(self, send_ref, totals, plan, base, mid, buf, own, recv, s_sem, r_sem, l_sem):
+        self.chips = chips = send_ref.shape[0]
+        rows = own.shape[0]
         half = rows // 2
         chip, right, left, far, _, _ = ring_peers(chips)
         top, low = pl.ds(0, half), pl.ds(half, half)
+        from_top, from_low = pl.ds(base, half), pl.ds(base + half, half)
 
         def remote(n, src, dst, who):
             return pltpu.make_async_remote_copy(src_ref=src, dst_ref=dst, send_sem=s_sem.at[n], recv_sem=r_sem.at[n],
                                                 device_id={'x': who}, device_id_type=pl.DeviceIdType.MESH)
 
-        self.first = [remote(0, send_ref.at[far, top], mid.at[0], right), remote(1, send_ref.at[far, low], mid.at[1], left),
-                      remote(2, send_ref.at[left, top], recv.at[1, top], left),
-                      remote(3, send_ref.at[right, low], recv.at[0, low], right)]
+        self.far = [remote(0, send_ref.at[far, from_top], mid.at[0], right),
+                    remote(1, send_ref.at[far, from_low], mid.at[1], left)]
+        self.direct = [remote(2, send_ref.at[left, from_top], recv.at[1, top], left),
+                       remote(3, send_ref.at[right, from_low], recv.at[0, low], right)]
         self.second = [remote(4, buf.at[0], recv.at[0, top], right), remote(5, buf.at[1], recv.at[1, low], left)]
-        self.local = [pltpu.make_async_copy(send_ref.at[right, top], buf.at[0], l_sem.at[0]),
-                      pltpu.make_async_copy(send_ref.at[left, low], buf.at[1], l_sem.at[1]),
-                      pltpu.make_async_copy(send_ref.at[chip], own, l_sem.at[2])]
-        self.mid, self.buf, self.own, self.recv, self.total_ref = mid, buf, own, recv, total_ref
+        self.local = [pltpu.make_async_copy(send_ref.at[right, from_top], buf.at[0], l_sem.at[0]),
+                      pltpu.make_async_copy(send_ref.at[left, from_low], buf.at[1], l_sem.at[1]),
+                      pltpu.make_async_copy(send_ref.at[chip, pl.ds(base, rows)], own, l_sem.at[2])]
+        self.mid, self.buf, self.own, self.recv, self.totals = mid, buf, own, recv, totals
+        self.plan = plan
 
     def start(self):
-        for c in self.first[:2] + self.local:
+        ring_barrier(self.chips)
+        for c in self.far + self.local:
             c.start()
 
     def start_direct(self):
-        for c in self.first[2:]:
+        for c in self.direct:
             c.start()
 
     def merge(self):
-        for i in range(2):
-            self.local[i].wait()
-            self.first[i].wait_recv()
-            self.buf[i] = (self.buf[i].astype(F32) + self.mid[i].astype(F32)).astype(BF16)
+        for far, local, buf, mid in zip(self.far, self.local, (self.buf.at[0], self.buf.at[1]), (self.mid.at[0], self.mid.at[1])):
+            local.wait()
+            far.wait_recv()
+            buf[:] = (buf[:].astype(F32) + mid[:].astype(F32)).astype(BF16)
 
     def send(self):
         for c in self.second:
             c.start()
 
     def finish(self):
-        self.local[2].wait()
-        for c in self.first[2:] + self.second:
+        self.local[-1].wait()
+        for c in self.direct + self.second:
             c.wait_recv()
-        self.total_ref[:] = (self.own[:].astype(F32) + self.recv[0].astype(F32) + self.recv[1].astype(F32)).astype(BF16)
-        for c in self.first + self.second:
+        row = 0
+        for ref in self.totals:
+            r = slice(row, row + ref.shape[0])
+            ref[:] = (self.own[r].astype(F32) + self.recv[0, r].astype(F32) + self.recv[1, r].astype(F32)).astype(BF16)
+            row += ref.shape[0]
+        for c in self.far + self.direct + self.second:
             c.wait_send()
 
-
-class RingGather:
-    @staticmethod
-    def scratch():
-        return [pltpu.SemaphoreType.DMA((8,)), pltpu.SemaphoreType.DMA((8,)), pltpu.SemaphoreType.DMA((1,))]
-
-    def __init__(self, block_ref, out_ref, s_sem, r_sem, l_sem):
-        chips, rows = out_ref.shape[1], out_ref.shape[2]
-        chip, right, left, far, core, mate = ring_peers(chips)
-        top, low = pl.ds(0, rows // 2), pl.ds(rows // 2, rows // 2)
-
-        def remote(n, src, dst, who):
-            return pltpu.make_async_remote_copy(src_ref=src, dst_ref=dst, send_sem=s_sem.at[n], recv_sem=r_sem.at[n],
-                                                device_id=who, device_id_type=pl.DeviceIdType.MESH)
-
-        mine = out_ref.at[core]
-        self.local = pltpu.make_async_copy(block_ref, mine.at[chip], l_sem.at[0])
-        self.first = [remote(0, block_ref, mine.at[chip], {'x': right}), remote(1, block_ref, mine.at[chip], {'x': left})]
-        self.second = [remote(2, mine.at[left, top], mine.at[left, top], {'x': right}),
-                       remote(3, mine.at[right, low], mine.at[right, low], {'x': left})]
-        self.mate = [remote(4, block_ref, mine.at[chip], {'core': mate})] + [
-            remote(5 + i, mine.at[j], mine.at[j], {'core': mate}) for i, j in enumerate((left, right, far))]
-
-    def start(self):
-        for c in [self.local, *self.first, self.mate[0]]:
-            c.start()
-
-    def forward(self):
-        for c in self.first:
-            c.wait_recv()
-        for c in self.second + self.mate[1:3]:
-            c.start()
-
-    def last(self):
-        for c in self.second:
-            c.wait_recv()
-        self.mate[3].start()
-
-    def finish(self):
-        self.local.wait()
-        for c in self.mate:
-            c.wait_recv()
-        for c in self.first + self.second + self.mate:
-            c.wait_send()
+    def ahead(self, step):
+        direct, merge = self.plan
+        run_at(step, 0, self.start)
+        run_at(step, direct, self.start_direct)
+        run_at(step, merge + 1, self.send)
+
+    def behind(self, step, final):
+        run_at(step, self.plan[1], self.merge)
+        run_at(step, final, self.finish)
 
 
 def run_at(step, n, *actions):
@@ -242,53 +216,24 @@
             a()
 
 
-def host_rings(ring_sum, gather, step, plan, chips):
-    if ring_sum is None and gather is None:
-        return
-    direct, merge, forward = plan
-    run_at(step, 0, lambda: ring_barrier(chips), *([ring_sum.start] if ring_sum else []), *([gather.start] if gather else []))
-    if ring_sum:
-        run_at(step, direct, ring_sum.start_direct)
-        run_at(step, merge + 1, ring_sum.send)
-    if gather:
-        run_at(step, forward, gather.forward)
-
-
-def finish_rings(ring_sum, gather, step, plan, final):
-    if ring_sum:
-        run_at(step, plan[1], ring_sum.merge)
-    last = ([gather.last] if gather else []) + ([ring_sum.finish] if ring_sum else []) + ([gather.finish] if gather else [])
-    if last:
-        run_at(step, final, *last)
-
-
 def comm_params(cid, n_axes=1):
     return pltpu.CompilerParams(dimension_semantics=("arbitrary",) * n_axes, vmem_limit_bytes=VMEM_LIMIT,
                                 collective_id=cid, has_side_effects=True)
 
 
 def attn_kernel(q0_ref, q1_ref, do0_ref, do1_ref, kv_ref, h0_ref, h1_ref, g0_ref, g1_ref, cos_ref, sin_ref, *refs,
-                has_sum, has_gather):
+                has_sum):
     refs = list(refs)
-    ring_sum = gather = None
     prev_ref = refs.pop(0) if has_sum else None
-    shard_ref = refs.pop(0) if has_gather else None
     own_ref, par_ref, send_ref = refs[:3]
     refs = refs[3:]
-    total_ref = refs.pop(0) if has_sum else None
-    all_ref = refs.pop(0) if has_gather else None
+    totals = [refs.pop(0), refs.pop(0)] if has_sum else []
     s_ref, p_ref, ds_ref, acc_ref, ml_ref, kvt_ref, lhs_ref, gacc_ref = refs[:8]
-    refs = refs[8:]
-    if has_sum:
-        ring_sum = RingSum(prev_ref, total_ref, *refs[:7])
-        refs = refs[7:]
-    if has_gather:
-        gather = RingGather(shard_ref, all_ref, *refs)
-    g_send_ref = send_ref
     chip, core = lax.axis_index('x'), lax.axis_index('core')
     b_id = pl.program_id(0)
-    plan = (2, 3, 4)
-    host_rings(ring_sum, gather, b_id, plan, kv_ref.shape[0])
+    if has_sum:
+        ring_sum = RingSum(prev_ref, totals, (2, 3), 0, *refs[8:])
+        ring_sum.ahead(b_id)
     chips = kv_ref.shape[0]
     rows, tok = q0_ref.shape[1], q0_ref.shape[2]
     e = kv_ref.shape[3] // 2
@@ -430,18 +375,18 @@
         for j in range(chips):
             n = rows // chips
             base = PAIR * e
-            g_send_ref[j, base:base + n] = gacc_ref[j * n:(j + 1) * n].astype(BF16)
-            g_send_ref[j, base + n:base + PAIR * n] = gacc_ref[rows + j * n:rows + (j + 1) * n].astype(BF16)
-
-    finish_rings(ring_sum, gather, b_id, plan, pl.num_programs(0) - 1)
+            send_ref[j, base:base + n] = gacc_ref[j * n:(j + 1) * n].astype(BF16)
+            send_ref[j, base + n:base + PAIR * n] = gacc_ref[rows + j * n:rows + (j + 1) * n].astype(BF16)
+
+    if has_sum:
+        ring_sum.behind(b_id, pl.num_programs(0) - 1)
 
 
 def kv_grad_kernel(*refs, stages):
     recv = refs[:stages]
-    h0_ref, h1_ref, cos_ref, sin_ref, shard_ref, own_ref, par_ref, send_ref, all_ref, gacc_ref = refs[stages:stages + 10]
-    gather = RingGather(shard_ref, all_ref, *refs[stages + 10:])
-    plan = (0, 0, 3)
-    host_rings(None, gather, pl.program_id(0), plan, all_ref.shape[1])
+    h0_ref, h1_ref, cos_ref, sin_ref, prev_ref, own_ref, par_ref, send_ref, shard_ref, gacc_ref = refs[stages:stages + 10]
+    ring_sum = RingSum(prev_ref, [shard_ref], (1, 2), own_ref.shape[1] // stages, *refs[stages + 10:])
+    ring_sum.ahead(pl.program_id(0))
     nb, tok, d = h0_ref.shape
     e2 = own_ref.shape[1] // stages
     e = e2 // 2
@@ -475,15 +420,14 @@
         for j in range(send_ref.shape[0]):
             send_ref[j] = gacc_ref[j * n:(j + 1) * n].astype(BF16)
 
-    finish_rings(None, gather, pl.program_id(0), plan, pl.num_programs(0) - 1)
+    ring_sum.behind(pl.program_id(0), pl.num_programs(0) - 1)
 
 
 def out_kernel(x_ref, w_ref, prev_ref, *refs, stages):
     core = lax.axis_index('core')
     o_refs, (y_ref, total_ref, lhs_ref) = refs[:PAIR * stages], refs[PAIR * stages:PAIR * stages + 3]
-    ring_sum = RingSum(prev_ref, total_ref, *refs[PAIR * stages + 3:])
-    plan = (1, 2, 0)
-    host_rings(ring_sum, None, pl.program_id(0), plan, prev_ref.shape[0])
+    ring_sum = RingSum(prev_ref, [total_ref], (1, 2), 0, *refs[PAIR * stages + 3:])
+    ring_sum.ahead(pl.program_id(0))
     nb, tok, d = x_ref.shape
     rows = o_refs[0].shape[2]
     half = stages * rows
@@ -498,17 +442,15 @@
         prod = dot(lhs, w_ref[:, c:c + step])
         y_ref[:, :, c:c + step] = (x_ref[:, :, c:c + step].astype(F32) + prod.reshape(nb, tok, step)).astype(BF16)
 
-    finish_rings(ring_sum, None, pl.program_id(0), plan, pl.num_programs(0) - 1)
-
-
-def norm_grad_kernel(x_ref, go_ref, g_ref, w_ref, kv0_ref, kv1_ref, prev_ref, shard_ref, *refs, stages):
+    ring_sum.behind(pl.program_id(0), pl.num_programs(0) - 1)
+
+
+def norm_grad_kernel(x_ref, go_ref, g_ref, w_ref, kv0_ref, kv1_ref, prev_ref, *refs, stages):
     core = lax.axis_index('core')
     q_refs = refs[:PAIR * stages]
-    gh_ref, gn_ref, total_ref, all_ref, lhs_ref, tot_ref = refs[PAIR * stages:PAIR * stages + 6]
-    ring_sum = RingSum(prev_ref, total_ref, *refs[PAIR * stages + 6:PAIR * stages + 13])
-    gather = RingGather(shard_ref, all_ref, *refs[PAIR * stages + 13:])
-    plan = (1, 0, 2)
-    host_rings(ring_sum, gather, pl.program_id(0), plan, prev_ref.shape[0])
+    gh_ref, gn_ref, total_ref, lhs_ref, tot_ref = refs[PAIR * stages:PAIR * stages + 5]
+    ring_sum = RingSum(prev_ref, [total_ref], (1, 1), 0, *refs[PAIR * stages + 5:])
+    ring_sum.ahead(pl.program_id(0))
     nb, tok, d = x_ref.shape
     rows = q_refs[0].shape[2]
     half = stages * rows
@@ -548,7 +490,7 @@
         gh_ref[b] = (go_ref[b].astype(F32) + inv * (gu - unit * mean_dot)).astype(BF16)
         gn_ref[:] += jnp.sum((total * unit).reshape(tok // 8, 8, d), axis=0)
 
-    finish_rings(ring_sum, gather, pl.program_id(0), plan, pl.num_programs(0) - 1)
+    ring_sum.behind(pl.program_id(0), pl.num_programs(0) - 1)
 
 
 def transpose_to(out_ref, blk):
@@ -563,9 +505,9 @@
     for s in range(stages):
         @pl.when(pl.program_id(1) == s)
         def _(ref=ins[s]):
-            _, chips, n, d = ref.shape
-            transpose_to(wq_ref, ref[0, :, 0:n_q].reshape(chips * n_q, d))
-            wo_ref[:] = ref[0, :, n_q:n].astype(F32)
+            chips, _, n, d = ref.shape
+            transpose_to(wq_ref, ref[:, 0, 0:n_q].reshape(chips * n_q, d))
+            wo_ref[:] = ref[:, 0, n_q:n].astype(F32)
 
 
 def assemble_tail_kernel(in_ref, _, out_ref):
@@ -676,59 +618,58 @@
         hbm = pl.BlockSpec(memory_space=pl.ANY)
         shard_spec = lambda n: whole(n, d)
 
-        def gathered_shape(n):
-            return jax.ShapeDtypeStruct((CORES, chips, n, d), BF16)
-
-        def attention(s, prev, shard):
+        def gather_shard(shard):
+            return lax.all_gather(shard, ('x', 'core')).reshape(chips, CORES, *shard.shape)
+
+        def attention(s, prev):
             blk = PAIR * tok
-            has_sum, has_gather = prev is not None, shard is not None
+            has_sum = prev is not None
             q_spec = pl.BlockSpec((1, rows, tok), lambda b: (b, s, 0))
             t_spec = pl.BlockSpec((2, tok, d), lambda b: (b // 2, 0, 0))
             r_spec = whole(2, half_rot, tok)
             o_spec = along(1, 2, 1, rows, tok)
             return pl.pallas_call(
-                functools.partial(attn_kernel, has_sum=has_sum, has_gather=has_gather),
+                functools.partial(attn_kernel, has_sum=has_sum),
                 out_shape=[jax.ShapeDtypeStruct((2, n_batch, rows, tok), BF16)] * 2
                 + [jax.ShapeDtypeStruct((chips, n_s, d), BF16)]
-                + [jax.ShapeDtypeStruct((n_s, d), BF16)] * has_sum + [gathered_shape(n_g)] * has_gather,
+                + [jax.ShapeDtypeStruct((n, d), BF16) for n in (e2, n_g)] * has_sum,
                 grid=(n_batch,),
                 in_specs=[q_spec, q_spec, q_spec, q_spec, along(2, chips, 2, 1, e2, tok),
                           t_spec, t_spec, t_spec, t_spec, r_spec, r_spec]
-                + [hbm] * has_sum + [shard_spec(n_g)] * has_gather,
+                + [hbm] * has_sum,
                 out_specs=[o_spec, o_spec, whole(chips, n_s, d)]
-                + [shard_spec(n_s)] * has_sum + [hbm] * has_gather,
+                + [shard_spec(e2), shard_spec(n_g)] * has_sum,
                 scratch_shapes=[pltpu.VMEM((chips, blk, reps * blk), F32), pltpu.VMEM((chips, blk, reps * blk), BF16),
                                 pltpu.VMEM((chips, blk, reps * blk), BF16), pltpu.VMEM((e, reps * blk), F32),
                                 pltpu.VMEM((8, reps * blk), F32),
                                 pltpu.VMEM((chips, blk, e2), BF16), pltpu.VMEM((2, PAIR * rows, blk), BF16),
                                 pltpu.VMEM((PAIR * rows, d), F32)]
-                + (RingSum.scratch(chips, n_s, d) if has_sum else []) + (RingGather.scratch() if has_gather else []),
+                + RingSum.scratch(n_s, d) * has_sum,
                 compiler_params=comm_params(s) if has_sum else params(),
                 cost_estimate=cost(4e10, 3e7, 3e7),
             )(q_own, q_par, do_own, do_par, gathered[s], h_own, h_par, grad_out, go_par, cos_t, sin_t,
-              *([prev] if has_sum else []), *([shard] if has_gather else []))
+              *([prev] * has_sum))
 
         own, par, totals, main = [], [], [], []
         prev = None
         for s in range(stages):
-            shard = totals[s - 2][e2:] if s >= 2 else None
-            outs = attention(s, prev, shard)
-            own.append(outs[0])
-            par.append(lax.ppermute(outs[1], 'core', swap))
-            prev = outs[2]
-            totals += outs[3:4]
-            main += outs[4:5]
+            own_s, par_s, send, *sums = attention(s, prev)
+            own.append(own_s)
+            par.append(lax.ppermute(par_s, 'core', swap))
+            prev = send
+            totals += sums[:1]
+            main += [gather_shard(g) for g in sums[1:]]
 
         nb2 = 2
         t2_spec = along(0, nb2, tok, d)
         block_out, total = pl.pallas_call(
             functools.partial(out_kernel, stages=stages),
-            out_shape=[jax.ShapeDtypeStruct((n_batch, tok, d), BF16), jax.ShapeDtypeStruct((n_s, d), BF16)],
+            out_shape=[jax.ShapeDtypeStruct((n_batch, tok, d), BF16), jax.ShapeDtypeStruct((e2, d), BF16)],
             grid=(n_batch // nb2,),
             in_specs=[t2_spec, whole(n_heads * e, d), hbm]
             + [along(1, 1, nb2, rows, tok)] * (PAIR * stages),
-            out_specs=[t2_spec, shard_spec(n_s)],
-            scratch_shapes=[pltpu.VMEM((nb2 * tok, n_heads * e), BF16)] + RingSum.scratch(chips, n_s, d),
+            out_specs=[t2_spec, shard_spec(e2)],
+            scratch_shapes=[pltpu.VMEM((nb2 * tok, n_heads * e), BF16)] + RingSum.scratch(e2, d),
             compiler_params=comm_params(stages), name='out_proj',
             cost_estimate=cost(PAIR * n_batch * tok * d * n_heads * e, 3e7),
         )(hidden, w_o, prev, *own, *par)
@@ -737,46 +678,45 @@
         gb = 2
         gf_spec = along(0, gb, stages * e2, tok)
         n_kv = stages * e2 // chips
-        kv_own_g, kv_par_g, send_kv, main_2 = pl.pallas_call(
+        kv_own_g, kv_par_g, send_kv, shard = pl.pallas_call(
             functools.partial(kv_grad_kernel, stages=stages),
             out_shape=[jax.ShapeDtypeStruct((n_batch, stages * e2, tok), BF16)] * 2
-            + [jax.ShapeDtypeStruct((chips, n_kv, d), BF16), gathered_shape(n_g)],
+            + [jax.ShapeDtypeStruct((chips, n_kv, d), BF16), jax.ShapeDtypeStruct((n_g, d), BF16)],
             grid=(n_batch // gb,),
             in_specs=[along(1, e2, PAIR * tok * gb)] * stages
             + [along(0, gb, tok, d)] * 2 + [whole(2, half_rot, tok)] * 2
-            + [shard_spec(n_g)],
-            out_specs=[gf_spec, gf_spec, whole(chips, n_kv, d), hbm],
-            scratch_shapes=[pltpu.VMEM((stages * e2, d), F32)] + RingGather.scratch(),
+            + [hbm],
+            out_specs=[gf_spec, gf_spec, whole(chips, n_kv, d), shard_spec(n_g)],
+            scratch_shapes=[pltpu.VMEM((stages * e2, d), F32)] + RingSum.scratch(n_g, d),
             compiler_params=comm_params(stages + 1), name='kv_grad',
             cost_estimate=cost(PAIR * PAIR * n_batch * tok * d * stages * e2, 3e7),
-        )(*totals, h_own, h_par, cos_t, sin_t, totals[-2][e2:])
-        main.append(main_2)
+        )(*totals, h_own, h_par, cos_t, sin_t, prev)
+        main.append(gather_shard(shard))
         kv_other_g = lax.ppermute(kv_par_g, 'core', swap)
 
         nb3 = 2
         t3_spec = along(0, nb3, tok, d)
-        grad_hidden, gn, shard_kv, main_3 = pl.pallas_call(
+        grad_hidden, gn, shard_kv = pl.pallas_call(
             functools.partial(norm_grad_kernel, stages=stages),
             out_shape=[jax.ShapeDtypeStruct((n_batch, tok, d), BF16), jax.ShapeDtypeStruct((8, d), F32),
-                       jax.ShapeDtypeStruct((n_kv, d), BF16), gathered_shape(n_g)],
+                       jax.ShapeDtypeStruct((n_kv, d), BF16)],
             grid=(n_batch // nb3,),
             in_specs=[t3_spec, t3_spec, whole(1, d), whole(*w_qkv.shape)]
-            + [along(0, nb3, stages * e2, tok)] * 2 + [hbm, shard_spec(n_g)]
+            + [along(0, nb3, stages * e2, tok)] * 2 + [hbm]
             + [pl.BlockSpec((1, nb3, rows, tok), lambda b: (1, b, 0, 0))] * (PAIR * stages),
-            out_specs=[t3_spec, whole(8, d), shard_spec(n_kv), hbm],
+            out_specs=[t3_spec, whole(8, d), shard_spec(n_kv)],
             scratch_shapes=[pltpu.VMEM((nb3 * tok, w_qkv.shape[1]), BF16), pltpu.VMEM((nb3 * tok, d), F32)]
-            + RingSum.scratch(chips, n_kv, d) + RingGather.scratch(),
+            + RingSum.scratch(n_kv, d),
             compiler_params=comm_params(stages + 2), name='norm_grad',
             cost_estimate=cost(PAIR * n_batch * tok * d * w_qkv.shape[1], 4e7),
-        )(hidden, grad_out, norm2, w_qkv, kv_own_g, kv_other_g, send_kv, totals[-1][e2:], *own, *par)
-        main.append(main_3)
+        )(hidden, grad_out, norm2, w_qkv, kv_own_g, kv_other_g, send_kv, *own, *par)
 
         gn_row = jnp.sum(gn, axis=0, keepdims=True)
         gn_hi = gn_row.astype(BF16)
         gn_lo = (gn_row - gn_hi.astype(F32)).astype(BF16)
         n_t = n_kv + 16
         tail_block = cat_rows([shard_kv, gn_hi, gn_lo, jnp.zeros((n_t - n_kv - 2, d), BF16)])
-        tail = lax.all_gather(tail_block, ('x', 'core')).reshape(chips, CORES, n_t, d)
+        tail = gather_shard(tail_block)
         n_q = rows // chips
         b_spec = pl.BlockSpec((n_batch // (CORES * stages), tok, d), lambda p, s: (p * stages + s, 0, 0))
         w_cols, grad_w_out, block_out, grad_hidden = pl.pallas_call(
@@ -784,7 +724,7 @@
             out_shape=[jax.ShapeDtypeStruct(w_qkv.shape, F32), jax.ShapeDtypeStruct((n_heads, e, d), F32)]
             + [jax.ShapeDtypeStruct((n_batch, tok, d), BF16)] * PAIR,
             grid=(CORES, stages),
-            in_specs=[along(0, 1, chips, n_g, d)] * stages + [b_spec] * PAIR,
+            in_specs=[along(1, chips, 1, n_g, d)] * stages + [b_spec] * PAIR,
             out_specs=[pl.BlockSpec((d, rows), lambda p, s: (0, p * stages + s)),
                        pl.BlockSpec((reps, e, d), lambda p, s: (p * stages + s, 0, 0)), b_spec, b_spec],
             compiler_params=params(2), name='assemble_main', cost_estimate=cost(2e9, 6e7),

time: 493 us -> 499 us (1.012)
  waiting for transfers between devices: 16 us -> 45.1 us
  Pallas kernels: 435 us -> 419 us
  local copies, waits for them, and re-layouts: 10.5 us -> 3.97 us
    pallas_call x4, Pallas kernels: 237 us -> 211 us  [attention(): pl.pallas_call(functools.partial(attn_kernel, has_sum=has_sum), out_shape...]
    all_gather x1 -> x5, waiting for transfers between devices: 6.53 us -> 31.2 us  [gather_shard(): lax.all_gather(shard, ('x', 'core')).reshape(chips, CORES, *shard.shape)]
    pallas_call x1, Pallas kernels: 28.2 us -> 40.3 us  [device_step(): pl.pallas_call(functools.partial(kv_grad_kernel, stages=stages), out_shap...]
    slice x4 -> x0, local copies, waits for them, and re-layouts: 6.49 us -> none  [the longest x2 3.76 us: device_step(): shard = totals[s - 2][e2:] if s >= 2 else None]
  transfers between devices with their start and end apart: 12 -> 16, of which waited for: 6 -> 8; matrix products, arithmetic and copies ran while one was open for 2% -> 1% of each run, Pallas kernels for 49% -> 71%
where the time goes in v5:
time: 499 us; the launch traced here: 491 us
  Pallas kernels  419 us (84%)
  waiting for transfers between devices  45.1 us (9%)
  between operations  14.3 us (3%)
  other arithmetic  6.21 us (1%)
    pallas_call x4, Pallas kernels, attention(): pl.pallas_call(functools.partial(attn_kernel, has_sum=has_sum), out_shape...  211 us
    pallas_call x1, Pallas kernels, device_step(): pl.pallas_call(functools.partial(out_kernel, stages=stages), out_shape=[j...  46 us
    pallas_call x1, Pallas kernels, device_step(): pl.pallas_call(functools.partial(norm_grad_kernel, stages=stages), out_sh...  44.2 us
    pallas_call x1, Pallas kernels, device_step(): pl.pallas_call(functools.partial(kv_grad_kernel, stages=stages), out_shap...  40.3 us
    all_gather x5, waiting for transfers between devices, gather_shard(): lax.all_gather(shard, ('x', 'core')).reshape(chips, CORES, *shard.shape)  31.2 us
    pallas_call x1, Pallas kernels, device_step(): pl.pallas_call(functools.partial(assemble_main_kernel, stages=stages, n_q...  24 us
    pallas_call x1, Pallas kernels, q_proj(): pl.pallas_call(drop_scalar(q_proj_kernel), out_shape=q_shapes, grid_spec=...  15.9 us
    pallas_call x2, Pallas kernels, kv_proj(): pl.pallas_call(drop_scalar(kv_proj_kernel), out_shape=[jax.ShapeDtypeStru...  15.7 us
  transfers between devices with their start and end apart: 16, of which 8 were waited for; matrix products, arithmetic and copies ran while one was open for 1% of the time, Pallas kernels for 71%

profile of v5, /device:TPU:112, one launch (start us, length us, event | category | flops | bytes accessed | tf_op | source)
XLA Modules:
  0.0 490.7 jit_solution(9046186219515069142)
XLA Ops:
  7.4 1.3 reshape.93.refs_1_.g_ref
  11.0 7.8 %kv_proj.2 = (bf16[8,128,2048]{2,1,0:T(8,128)(2,1)}, bf16[2,8,128,128]{3,2,1,0:T(8,128)(2,1)}, bf16[2,8,128,128]{3,2,1,0:T(8,128)(2,1)}, bf16[2,8,128,128]{3,2,1,0:T(8,128)(2,1)}, bf16[2,8,128,128]{3,2,1,0:T(8,128)(2,1)}) custom-call(s32[2]{0:T(128)} %pad_add_fusion._, bf16[8,128,2048]{2,1,0:T(8,128)(2,1)} %x_ref.3, bf16[1,2048]{1,0:T(2,128)(2,1)} %reshape.93.refs_1_.g_ref, ...), custom_call_target="tpu_custom_call" | custom-call | flops 2147483648 | bytes 12582912 | tf_op jit(solution)/shard_map/kv_proj/pallas_call | solution.py:561
  18.8 7.9 %kv_proj.3 = (bf16[8,128,2048]{2,1,0:T(8,128)(2,1)}, bf16[2,8,128,128]{3,2,1,0:T(8,128)(2,1)}, bf16[2,8,128,128]{3,2,1,0:T(8,128)(2,1)}, bf16[2,8,128,128]{3,2,1,0:T(8,128)(2,1)}, bf16[2,8,128,128]{3,2,1,0:T(8,128)(2,1)}) custom-call(s32[2]{0:T(128)} %pad_add_fusion._, ...), custom_call_target="tpu_custom_call", output_to_operand_aliasing={{1}: (7, {}), {2}: (8, {}), {3}: (9, {}), {4}: (10, {})} | custom-call | flops 2147483648 | bytes 12582912 | tf_op jit(solution)/shard_map/kv_proj/pallas_call | solution.py:561
  29.1 15.9 %q_proj.1 = (bf16[8,1024,128]{2,1,0:T(8,128)(2,1)}, bf16[8,1024,128]{2,1,0:T(8,128)(2,1)}) custom-call(s32[2]{0:T(128)} %pad_add_fusion._, bf16[8,128,2048]{2,1,0:T(8,128)(2,1)} %get-tuple-element.50.refs_0_.h0_ref.refs_4_, bf16[8,128,2048]{2,1,0:T(8,128)(2,1)} %get-tuple-element.55.refs_1_.h1_ref.refs_5_, bf16[2048,3072]{1,0:T(8,128)(2,1)} %w_ref.1, ...), custom_call_target="tpu_custom_call" | custom-call | flops 8589934592 | bytes 25165824 | tf_op jit(solution)/shard_map/q_proj/pallas_call | solution.py:587
  44.9 15.2 %do_proj.1 = (bf16[8,1024,128]{2,1,0:T(8,128)(2,1)}, bf16[8,1024,128]{2,1,0:T(8,128)(2,1)}) custom-call(s32[2]{0:T(128)} %pad_add_fusion._, bf16[8,128,2048]{2,1,0:T(8,128)(2,1)} %go_ref.1, bf16[8,128,2048]{2,1,0:T(8,128)(2,1)} %collective-permute-done.1.refs_1_.g1_ref, bf16[2048,2048]{1,0:T(8,128)(2,1)} %bitcast.30), custom_call_target="tpu_custom_call" | custom-call | flops 8589934592 | bytes 25165824 | tf_op jit(solution)/shard_map/do_proj/pallas_call | solution.py:598
  60.1 23.0 %shard_map.101 = (bf16[2,8,256,128]{3,2,1,0:T(8,128)(2,1)}, bf16[2,8,256,128]{3,2,1,0:T(8,128)(2,1)}, bf16[4,256,2048]{2,1,0:T(8,128)(2,1)}) custom-call(bf16[8,1024,128]{2,1,0:T(8,128)(2,1)} %get-tuple-element.56.q0_ref, bf16[8,1024,128]{2,1,0:T(8,128)(2,1)} %get-tuple-element.57.q1_ref, bf16[8,1024,128]{2,1,0:T(8,128)(2,1)} %get-tuple-element.58.do0_ref, ...), custom_call_target="tpu_custom_call" | custom-call | flops 40000000000 | bytes 30000000 | tf_op jit(solution)/shard_map/pallas_call | solution.py:631
  83.1 1.8 all-gather.19.cloned.1.call-done
  84.9 89.3 %shard_map.102 = (bf16[2,8,256,128]{3,2,1,0:T(8,128)(2,1)}, bf16[2,8,256,128]{3,2,1,0:T(8,128)(2,1)}, bf16[4,256,2048]{2,1,0:T(8,128)(2,1)}, bf16[128,2048]{1,0:T(8,128)(2,1)}, bf16[128,2048]{1,0:T(8,128)(2,1)}) custom-call(bf16[8,1024,128]{2,1,0:T(8,128)(2,1)} %get-tuple-element.56.q0_ref, bf16[8,1024,128]{2,1,0:T(8,128)(2,1)} %get-tuple-element.57.q1_ref, ...), custom_call_target="tpu_custom_call" | custom-call | flops 40000000000 | bytes 30000000 | tf_op jit(solution)/shard_map/pallas_call | solution.py:631
  174.2 44.9 %shard_map.103 = (bf16[2,8,256,128]{3,2,1,0:T(8,128)(2,1)}, bf16[2,8,256,128]{3,2,1,0:T(8,128)(2,1)}, bf16[4,256,2048]{2,1,0:T(8,128)(2,1)}, bf16[128,2048]{1,0:T(8,128)(2,1)}, bf16[128,2048]{1,0:T(8,128)(2,1)}) custom-call(bf16[8,1024,128]{2,1,0:T(8,128)(2,1)} %get-tuple-element.56.q0_ref, bf16[8,1024,128]{2,1,0:T(8,128)(2,1)} %get-tuple-element.57.q1_ref, ...), custom_call_target="tpu_custom_call" | custom-call | flops 40000000000 | bytes 30000000 | tf_op jit(solution)/shard_map/pallas_call | solution.py:631
  219.2 54.1 %shard_map.104 = (bf16[2,8,256,128]{3,2,1,0:T(8,128)(2,1)}, bf16[2,8,256,128]{3,2,1,0:T(8,128)(2,1)}, bf16[4,256,2048]{2,1,0:T(8,128)(2,1)}, bf16[128,2048]{1,0:T(8,128)(2,1)}, bf16[128,2048]{1,0:T(8,128)(2,1)}) custom-call(bf16[8,1024,128]{2,1,0:T(8,128)(2,1)} %get-tuple-element.56.q0_ref, bf16[8,1024,128]{2,1,0:T(8,128)(2,1)} %get-tuple-element.57.q1_ref, ...), custom_call_target="tpu_custom_call" | custom-call | flops 40000000000 | bytes 30000000 | tf_op jit(solution)/shard_map/pallas_call | solution.py:631
  275.9 1.8 collective-permute-done.5.refs_7_
  277.8 1.5 collective-permute-done.4.refs_6_
  279.3 1.5 collective-permute-done.3.refs_5_
  280.8 1.5 collective-permute-done.2.refs_4_
  283.3 46.0 %out_proj.1 = (bf16[8,128,2048]{2,1,0:T(8,128)(2,1)}, bf16[128,2048]{1,0:T(8,128)(2,1)}) custom-call(bf16[8,128,2048]{2,1,0:T(8,128)(2,1)} %x_ref.3, bf16[2048,2048]{1,0:T(8,128)(2,1)} %bitcast.31, bf16[4,256,2048]{2,1,0:T(8,128)(2,1)} %get-tuple-element.73.prev_ref.refs_8_, bf16[2,8,256,128]{3,2,1,0:T(8,128)(2,1)} %get-tuple-element.74.refs_0_, ...), custom_call_target="tpu_custom_call" | custom-call | flops 8589934592 | bytes 30000000 | tf_op jit(solution)/shard_map/out_proj/pallas_call | solution.py:665
  329.3 40.3 %kv_grad.1 = (bf16[8,512,128]{2,1,0:T(8,128)(2,1)}, bf16[8,512,128]{2,1,0:T(8,128)(2,1)}, bf16[4,128,2048]{2,1,0:T(8,128)(2,1)}, bf16[128,2048]{1,0:T(8,128)(2,1)}) custom-call(bf16[128,2048]{1,0:T(8,128)(2,1)} %get-tuple-element.70.refs_0_, bf16[128,2048]{1,0:T(8,128)(2,1)} %get-tuple-element.71.refs_1_, bf16[128,2048]{1,0:T(8,128)(2,1)} %get-tuple-element.72.refs_2_, ...), custom_call_target="tpu_custom_call" | custom-call | flops 4294967296 | bytes 30000000 | tf_op jit(solution)/shard_map/kv_grad/pallas_call | solution.py:681
  369.8 2.8 collective-permute-done.6.kv1_ref
  373.6 44.2 %norm_grad.1 = (bf16[8,128,2048]{2,1,0:T(8,128)(2,1)}, f32[8,2048]{1,0:T(8,128)}, bf16[128,2048]{1,0:T(8,128)(2,1)}) custom-call(bf16[8,128,2048]{2,1,0:T(8,128)(2,1)} %x_ref.3, bf16[8,128,2048]{2,1,0:T(8,128)(2,1)} %go_ref.1, bf16[1,2048]{1,0:T(2,128)(2,1)} %reshape.93.refs_1_.g_ref, bf16[2048,3072]{1,0:T(8,128)(2,1)} %w_ref.1, ...), custom_call_target="tpu_custom_call" | custom-call | flops 12884901888 | bytes 40000000 | tf_op jit(solution)/shard_map/norm_grad/pallas_call | solution.py:699
  418.7 2.0 maximum_maximum_fusion
  420.9 23.4 %all-gather.33.cloned.1.call-done = bf16[1024,2048]{1,0:T(8,128)(2,1)} async-done(((bf16[128,2048]{1,0:T(8,128)(2,1)}), bf16[1024,2048]{1,0:T(8,128)(2,1)}) %all-gather.33.cloned.1.call-update) | async-done | bytes 4194320 | tf_op jit(solution)/shard_map/all_gather | solution.py:622
  444.3 24.0 %assemble_main.1 = (f32[2048,3072]{1,0:T(8,128)}, f32[32,64,2048]{2,1,0:T(8,128)}, bf16[8,128,2048]{2,1,0:T(8,128)(2,1)}, bf16[8,128,2048]{2,1,0:T(8,128)(2,1)}) custom-call(bf16[4,2,128,2048]{3,2,1,0:T(8,128)(2,1)} %bitcast.26, bf16[4,2,128,2048]{3,2,1,0:T(8,128)(2,1)} %bitcast.25, bf16[4,2,128,2048]{3,2,1,0:T(8,128)(2,1)} %bitcast.24, ...), custom_call_target="tpu_custom_call" | custom-call | flops 2000000000 | bytes 60000000 | tf_op jit(solution)/shard_map/assemble_main/pallas_call | solution.py:722
  468.3 7.7 %all-gather.35.cloned.1.call-done = bf16[1152,2048]{1,0:T(8,128)(2,1)} async-done(((bf16[144,2048]{1,0:T(8,128)(2,1)}), bf16[1152,2048]{1,0:T(8,128)(2,1)}) %all-gather.35.cloned.1.call-update) | async-done | bytes 4718608 | tf_op jit(solution)/shard_map/all_gather | solution.py:622
  476.0 1.6 convert_reduce_fusion
  477.6 6.4 %assemble_tail.1 = f32[2048,3072]{1,0:T(8,128)} custom-call(bf16[4,2,144,2048]{3,2,1,0:T(8,128)(2,1)} %bitcast.23, f32[2048,3072]{1,0:T(8,128)} %get-tuple-element.93._), custom_call_target="tpu_custom_call", output_to_operand_aliasing={{}: (1, {})} | custom-call | flops 1000000000 | bytes 20000000 | tf_op jit(solution)/shard_map/assemble_tail/pallas_call | solution.py:733
  (62 shorter events, 10.7 us)
Async XLA Ops:
  7.2 52.9 %all-gather.21.cloned.1.call-start = ((), (), s32[]{:S(2)}) async-start(), calls=%async_computation.1 | async-start | bytes 2621440 | tf_op jit(solution)/shard_map/all_gather | solution.py:612
  7.2 11.6 %collective-permute-start = (bf16[8,128,2048]{2,1,0:T(8,128)(2,1)}, bf16[8,128,2048]{2,1,0:T(8,128)(2,1)}, u32[]{:S(2)}, u32[]{:S(2)}) collective-permute-start(bf16[8,128,2048]{2,1,0:T(8,128)(2,1)} %x_ref.3), channel_id=1, source_target_pairs={{0,1},{1,0},{2,3},{3,2},{4,5},{5,4},{6,7},{7,6},{8,9},{9,8},{10,11... | collective-permute-start | bytes 12582920 | tf_op jit(solution)/shard_map/ppermute | solution.py:540
  10.3 8.5 %copy-start = (f32[2,32,128]{2,1,0:T(8,128)}, f32[2,32,128]{2,1,0:T(8,128)S(1)}, u32[]{:S(2)}) copy-start(f32[2,32,128]{2,1,0:T(8,128)S(1)} %get-tuple-element.99.refs_4_.sin_ref.refs_7_) | copy-start | bytes 98308
  10.3 8.5 %copy-start.1 = (f32[2,32,128]{2,1,0:T(8,128)}, f32[2,32,128]{2,1,0:T(8,128)S(1)}, u32[]{:S(2)}) copy-start(f32[2,32,128]{2,1,0:T(8,128)S(1)} %get-tuple-element.100.refs_3_.cos_ref.refs_6_) | copy-start | bytes 98308
  26.8 58.1 %all-gather.19.cloned.1.call-start = ((), (), s32[]{:S(2)}) async-start(), calls=%async_computation | async-start | bytes 2621440 | tf_op jit(solution)/shard_map/all_gather | solution.py:612
  27.6 146.7 %all-gather.25.cloned.1.call-start = ((), (), s32[]{:S(2)}) async-start(), calls=%async_computation.3 | async-start | bytes 2621440 | tf_op jit(solution)/shard_map/all_gather | solution.py:612
  27.6 17.3 %collective-permute-start.1 = (bf16[8,128,2048]{2,1,0:T(8,128)(2,1)}, bf16[8,128,2048]{2,1,0:T(8,128)(2,1)}, u32[]{:S(2)}, u32[]{:S(2)}) collective-permute-start(bf16[8,128,2048]{2,1,0:T(8,128)(2,1)} %go_ref.1), channel_id=1, source_target_pairs={{0,1},{1,0},{2,3},{3,2},{4,5},{5,4},{6,7},{7,6},{8,9},{9,8},{10,11... | collective-permute-start | bytes 12582920 | tf_op jit(solution)/shard_map/ppermute | solution.py:541
  28.4 190.8 %all-gather.29.cloned.1.call-start = ((), (), s32[]{:S(2)}) async-start(), calls=%async_computation.5 | async-start | bytes 2621440 | tf_op jit(solution)/shard_map/all_gather | solution.py:612
  29.0 391.8 %all-gather.31.cloned.1.call-start = ((), (), s32[]{:S(2)}) async-start(), calls=%async_computation.6 | async-start | bytes 4718592 | tf_op jit(solution)/shard_map/all_gather | solution.py:622
  219.1 56.3 %copy-start.3 = (bf16[2,8,256,128]{3,2,1,0:T(8,128)(2,1)S(1)}, bf16[2,8,256,128]{3,2,1,0:T(8,128)(2,1)}, u32[]{:S(2)}) copy-start(bf16[2,8,256,128]{3,2,1,0:T(8,128)(2,1)} %get-tuple-element.79) | copy-start | bytes 3145732
  219.2 56.4 %copy-start.2 = (bf16[2,8,256,128]{3,2,1,0:T(8,128)(2,1)S(1)}, bf16[2,8,256,128]{3,2,1,0:T(8,128)(2,1)}, u32[]{:S(2)}) copy-start(bf16[2,8,256,128]{3,2,1,0:T(8,128)(2,1)} %get-tuple-element.78) | copy-start | bytes 3145732
  273.3 147.5 %all-gather.27.cloned.1.call-start = ((), (), s32[]{:S(2)}) async-start(), calls=%async_computation.4 | async-start | bytes 4718592 | tf_op jit(solution)/shard_map/all_gather | solution.py:622
  274.0 146.9 %all-gather.23.cloned.1.call-start = ((), (), s32[]{:S(2)}) async-start(), calls=%async_computation.2 | async-start | bytes 4718592 | tf_op jit(solution)/shard_map/all_gather | solution.py:622
  274.8 169.5 %all-gather.33.cloned.1.call-start = ((), (), s32[]{:S(2)}) async-start(), calls=%async_computation.7 | async-start | bytes 4718592 | tf_op jit(solution)/shard_map/all_gather | solution.py:622
  274.8 2.9 collective-permute-start.5
  274.9 4.3 collective-permute-start.4
  275.4 5.4 %collective-permute-start.3 = (bf16[2,8,256,128]{3,2,1,0:T(8,128)(2,1)S(1)}, bf16[2,8,256,128]{3,2,1,0:T(8,128)(2,1)S(1)}, u32[]{:S(2)}, u32[]{:S(2)}) collective-permute-start(bf16[2,8,256,128]{3,2,1,0:T(8,128)(2,1)S(1)} %copy-done.3), channel_id=1, source_target_pairs={{0,1},{1,0},{2,3},{3,2},{4,5},{5,4},{6,7},{7,6},{8,9},{9,8},{10,11... | collective-permute-start | bytes 3145736 | tf_op jit(solution)/shard_map/ppermute | solution.py:658
  275.5 6.8 %collective-permute-start.2 = (bf16[2,8,256,128]{3,2,1,0:T(8,128)(2,1)S(1)}, bf16[2,8,256,128]{3,2,1,0:T(8,128)(2,1)S(1)}, u32[]{:S(2)}, u32[]{:S(2)}) collective-permute-start(bf16[2,8,256,128]{3,2,1,0:T(8,128)(2,1)S(1)} %copy-done.2), channel_id=1, source_target_pairs={{0,1},{1,0},{2,3},{3,2},{4,5},{5,4},{6,7},{7,6},{8,9},{9,8},{10,11... | collective-permute-start | bytes 3145736 | tf_op jit(solution)/shard_map/ppermute | solution.py:658
  277.8 5.5 %copy-start.4 = (bf16[2,8,256,128]{3,2,1,0:T(8,128)(2,1)}, bf16[2,8,256,128]{3,2,1,0:T(8,128)(2,1)S(1)}, u32[]{:S(2)}) copy-start(bf16[2,8,256,128]{3,2,1,0:T(8,128)(2,1)S(1)} %collective-permute-done.5.refs_7_) | copy-start | bytes 3145732
  279.3 3.0 copy-start.5
  280.8 1.5 copy-start.6
  282.3 1.0 copy-start.7
  369.6 106.4 %all-gather.35.cloned.1.call-start = ((), (), s32[]{:S(2)}) async-start(), calls=%async_computation.8 | async-start | bytes 5308416 | tf_op jit(solution)/shard_map/all_gather | solution.py:622
  369.7 2.9 collective-permute-start.6
  (1 other events, 1.0 us)
Sparse Core Ops, SparseCore 0:
  26.9 29.6 all-gather.20
  58.2 26.6 all-gather.18
  86.4 27.0 all-gather.24
  114.9 43.2 all-gather.28
  273.4 54.2 all-gather.30
  329.2 41.1 all-gather.26
  372.0 42.6 all-gather.22
  416.3 27.9 all-gather.32
  445.9 30.0 all-gather.34

commit v6 on v5

--- a/solution.py
+++ b/solution.py
@@ -61,8 +61,9 @@
 def kv_proj_kernel(x_ref, g_ref, wk_ref, wv_ref, cos_ref, sin_ref, *refs):
     nb, tok, d = x_ref.shape
     stages = (wk_ref.shape[1] // (PAIR * cos_ref.shape[0]))
-    h_ref, kv_refs = refs[-stages - 1], refs[-stages:]
-    e2 = kv_refs[0].shape[2]
+    h_ref, first_ref, rest_ref = refs[-3:]
+    kv_refs = [first_ref] + [rest_ref.at[i] for i in range(stages - 1)]
+    e2 = first_ref.shape[2]
     e = e2 // 2
     x = x_ref[:].reshape(nb * tok, d).astype(F32)
     inv = lax.rsqrt(row_mean(x * x) + NORM_EPS)
@@ -448,8 +449,9 @@
 def norm_grad_kernel(x_ref, go_ref, g_ref, w_ref, kv0_ref, kv1_ref, prev_ref, *refs, stages):
     core = lax.axis_index('core')
     q_refs = refs[:PAIR * stages]
-    gh_ref, gn_ref, total_ref, lhs_ref, tot_ref = refs[PAIR * stages:PAIR * stages + 5]
-    ring_sum = RingSum(prev_ref, [total_ref], (1, 1), 0, *refs[PAIR * stages + 5:])
+    gh_ref, tail_ref, lhs_ref, tot_ref, gn_ref = refs[PAIR * stages:PAIR * stages + 5]
+    n_kv = prev_ref.shape[1]
+    ring_sum = RingSum(prev_ref, [tail_ref.at[pl.ds(0, n_kv)]], (1, 1), 0, *refs[PAIR * stages + 5:])
     ring_sum.ahead(pl.program_id(0))
     nb, tok, d = x_ref.shape
     rows = q_refs[0].shape[2]
@@ -490,6 +492,14 @@
         gh_ref[b] = (go_ref[b].astype(F32) + inv * (gu - unit * mean_dot)).astype(BF16)
         gn_ref[:] += jnp.sum((total * unit).reshape(tok // 8, 8, d), axis=0)
 
+    @pl.when(pl.program_id(0) == pl.num_programs(0) - 1)
+    def _():
+        extra = tail_ref.shape[0] - n_kv
+        total = column_sum(gn_ref[:])
+        high = total.astype(BF16).astype(F32)
+        row = lax.broadcasted_iota(jnp.int32, (extra, d), 0)
+        tail_ref[n_kv:] = jnp.where(row == 0, high, jnp.where(row == 1, total - high, 0.0)).astype(BF16)
+
     ring_sum.behind(pl.program_id(0), pl.num_programs(0) - 1)
 
 
@@ -510,7 +520,8 @@
             wo_ref[:] = ref[:, 0, n_q:n].astype(F32)
 
 
-def assemble_tail_kernel(in_ref, _, out_ref):
+def assemble_tail_kernel(in_ref, gn_ref, _, out_ref, norm_ref):
+    norm_ref[:] = jnp.sum(gn_ref[:].astype(F32), axis=(0, 1, 2)).reshape(norm_ref.shape)
     chips, _, n, d = in_ref.shape
     transpose_to(out_ref, in_ref[:, 0].reshape(chips * n, d))
 
@@ -561,14 +572,15 @@
             return pl.pallas_call(
                 drop_scalar(kv_proj_kernel),
                 out_shape=[jax.ShapeDtypeStruct((n_batch, tok, d), BF16)]
-                + [jax.ShapeDtypeStruct((2, n_batch, e2, tok), BF16)] * stages,
+                + [jax.ShapeDtypeStruct((2, n_batch, e2, tok), BF16), jax.ShapeDtypeStruct((stages - 1, 2, n_batch, e2, tok), BF16)],
                 grid_spec=pltpu.PrefetchScalarGridSpec(
                     num_scalar_prefetch=1, grid=(kt,),
                     in_specs=[x_spec, whole(1, d),
                               pl.BlockSpec((d, kv_half), lambda i, c: (0, kb + c[1])),
                               pl.BlockSpec((d, kv_half), lambda i, c: (0, kb + CORES + c[1])), rot_spec, rot_spec]
                     + [any_spec] * len(filled),
-                    out_specs=[x_spec] + [pl.BlockSpec((1, kn, e2, tok), lambda i, _: (side, i, 0, 0))] * stages),
+                    out_specs=[x_spec, pl.BlockSpec((1, kn, e2, tok), lambda i, _: (side, i, 0, 0)),
+                               pl.BlockSpec((stages - 1, 1, kn, e2, tok), lambda i, _: (0, side, i, 0, 0))]),
                 input_output_aliases={7 + i: 1 + i for i in range(len(filled))},
                 compiler_params=params(), name='kv_proj',
                 cost_estimate=cost(PAIR * n_batch * tok * d * PAIR * kv_half, 3 * n_batch * tok * d * 2),
@@ -607,9 +619,7 @@
 
         h_own, *kv_sides = kv_proj(hidden, 0, [])
         h_par, *kv_sides = kv_proj(x_par, 1, kv_sides)
-        gathered = []
-        for s in range(stages):
-            gathered.append(lax.all_gather(kv_sides[s], 'x'))
+        gathered = [lax.all_gather(kv, 'x') for kv in kv_sides]
         q_own, q_par = q_proj(h_own, h_par)
         do_own, do_par = do_proj(grad_out, go_par)
 
@@ -624,6 +634,10 @@
         def attention(s, prev):
             blk = PAIR * tok
             has_sum = prev is not None
+            if s == 0:
+                kv_spec = along(2, chips, 2, 1, e2, tok)
+            else:
+                kv_spec = pl.BlockSpec((chips, None, 2, 1, e2, tok), lambda b: (0, s - 1, 0, b, 0, 0))
             q_spec = pl.BlockSpec((1, rows, tok), lambda b: (b, s, 0))
             t_spec = pl.BlockSpec((2, tok, d), lambda b: (b // 2, 0, 0))
             r_spec = whole(2, half_rot, tok)
@@ -634,7 +648,7 @@
                 + [jax.ShapeDtypeStruct((chips, n_s, d), BF16)]
                 + [jax.ShapeDtypeStruct((n, d), BF16) for n in (e2, n_g)] * has_sum,
                 grid=(n_batch,),
-                in_specs=[q_spec, q_spec, q_spec, q_spec, along(2, chips, 2, 1, e2, tok),
+                in_specs=[q_spec, q_spec, q_spec, q_spec, kv_spec,
                           t_spec, t_spec, t_spec, t_spec, r_spec, r_spec]
                 + [hbm] * has_sum,
                 out_specs=[o_spec, o_spec, whole(chips, n_s, d)]
@@ -647,7 +661,7 @@
                 + RingSum.scratch(n_s, d) * has_sum,
                 compiler_params=comm_params(s) if has_sum else params(),
                 cost_estimate=cost(4e10, 3e7, 3e7),
-            )(q_own, q_par, do_own, do_par, gathered[s], h_own, h_par, grad_out, go_par, cos_t, sin_t,
+            )(q_own, q_par, do_own, do_par, gathered[min(s, 1)], h_own, h_par, grad_out, go_par, cos_t, sin_t,
               *([prev] * has_sum))
 
         own, par, totals, main = [], [], [], []
@@ -696,26 +710,21 @@
 
         nb3 = 2
         t3_spec = along(0, nb3, tok, d)
-        grad_hidden, gn, shard_kv = pl.pallas_call(
+        n_t = n_kv + 16
+        grad_hidden, tail_block = pl.pallas_call(
             functools.partial(norm_grad_kernel, stages=stages),
-            out_shape=[jax.ShapeDtypeStruct((n_batch, tok, d), BF16), jax.ShapeDtypeStruct((8, d), F32),
-                       jax.ShapeDtypeStruct((n_kv, d), BF16)],
+            out_shape=[jax.ShapeDtypeStruct((n_batch, tok, d), BF16), jax.ShapeDtypeStruct((n_t, d), BF16)],
             grid=(n_batch // nb3,),
             in_specs=[t3_spec, t3_spec, whole(1, d), whole(*w_qkv.shape)]
             + [along(0, nb3, stages * e2, tok)] * 2 + [hbm]
             + [pl.BlockSpec((1, nb3, rows, tok), lambda b: (1, b, 0, 0))] * (PAIR * stages),
-            out_specs=[t3_spec, whole(8, d), shard_spec(n_kv)],
-            scratch_shapes=[pltpu.VMEM((nb3 * tok, w_qkv.shape[1]), BF16), pltpu.VMEM((nb3 * tok, d), F32)]
+            out_specs=[t3_spec, shard_spec(n_t)],
+            scratch_shapes=[pltpu.VMEM((nb3 * tok, w_qkv.shape[1]), BF16), pltpu.VMEM((nb3 * tok, d), F32), pltpu.VMEM((8, d), F32)]
             + RingSum.scratch(n_kv, d),
             compiler_params=comm_params(stages + 2), name='norm_grad',
             cost_estimate=cost(PAIR * n_batch * tok * d * w_qkv.shape[1], 4e7),
         )(hidden, grad_out, norm2, w_qkv, kv_own_g, kv_other_g, send_kv, *own, *par)
 
-        gn_row = jnp.sum(gn, axis=0, keepdims=True)
-        gn_hi = gn_row.astype(BF16)
-        gn_lo = (gn_row - gn_hi.astype(F32)).astype(BF16)
-        n_t = n_kv + 16
-        tail_block = cat_rows([shard_kv, gn_hi, gn_lo, jnp.zeros((n_t - n_kv - 2, d), BF16)])
         tail = gather_shard(tail_block)
         n_q = rows // chips
         b_spec = pl.BlockSpec((n_batch // (CORES * stages), tok, d), lambda p, s: (p * stages + s, 0, 0))
@@ -730,17 +739,19 @@
             compiler_params=params(2), name='assemble_main', cost_estimate=cost(2e9, 6e7),
         )(*main, block_out, grad_hidden)
         kcol = PAIR * q_half // kv_half
-        grad_w_qkv = pl.pallas_call(
+        extra = n_t - n_kv
+        grad_w_qkv, grad_norm_w = pl.pallas_call(
             assemble_tail_kernel,
-            out_shape=jax.ShapeDtypeStruct(w_qkv.shape, F32),
-            grid=(CORES, 2),
-            in_specs=[pl.BlockSpec((chips, 1, e, d), lambda p, k: (0, p, k, 0)), pl.BlockSpec(memory_space=pl.ANY)],
-            out_specs=pl.BlockSpec((d, kv_half), lambda p, k: (0, kcol + k * CORES + p)),
-            input_output_aliases={1: 0},
+            out_shape=[jax.ShapeDtypeStruct(w_qkv.shape, F32), jax.ShapeDtypeStruct((1, d), F32)],
+            grid=(CORES, PAIR),
+            in_specs=[pl.BlockSpec((chips, 1, e, d), lambda p, k: (0, p, k, 0)),
+                      pl.BlockSpec((chips, CORES, extra, d), lambda p, k: (0, 0, n_kv // extra, 0)),
+                      pl.BlockSpec(memory_space=pl.ANY)],
+            out_specs=[pl.BlockSpec((d, kv_half), lambda p, k: (0, kcol + k * CORES + p)), whole(1, d)],
+            input_output_aliases={2: 0},
             compiler_params=params(2), name='assemble_tail', cost_estimate=cost(1e9, 2e7),
-        )(tail, w_cols)
-        gn_all = tail[:, :, n_kv:n_kv + 2].astype(F32)
-        grad_norm_w = jnp.sum(gn_all, axis=(0, 1, 2))
+        )(tail, tail, w_cols)
+        grad_norm_w = grad_norm_w.reshape(d)
         return block_out, grad_hidden, grad_w_qkv, grad_w_out, grad_norm_w
 
     tok_spec = P('dp', ('x', 'core'), None)

time: 499 us -> 474 us (0.950)
  Pallas kernels: 419 us -> 388 us
  waiting for transfers between devices: 45.1 us -> 52.5 us
    all_gather x4 -> x2, waiting for transfers between devices: 1.83 us -> 37.6 us  [device_step(): gathered = [lax.all_gather(kv, 'x') for kv in kv_sides]]
    pallas_call x4, Pallas kernels: 211 us -> 181 us  [attention(): pl.pallas_call(functools.partial(attn_kernel, has_sum=has_sum), out_shape...]
    all_gather x5, waiting for transfers between devices: 31.2 us -> 6.24 us  [gather_shard(): lax.all_gather(shard, ('x', 'core')).reshape(chips, CORES, *shard.shape)]
  transfers between devices with their start and end apart: 16 -> 14, of which waited for: 8 -> 7; matrix products, arithmetic and copies ran while one was open for 1% -> 1% of each run, Pallas kernels for 71% -> 71%
where the time goes in v6:
time: 474 us; the launch traced here: 465 us
  Pallas kernels  388 us (82%)
  waiting for transfers between devices  52.5 us (11%)
  between operations  14.5 us (3%)
  local copies, waits for them, and re-layouts  5.93 us (1%)
    pallas_call x4, Pallas kernels, attention(): pl.pallas_call(functools.partial(attn_kernel, has_sum=has_sum), out_shape...  181 us
    pallas_call x1, Pallas kernels, device_step(): pl.pallas_call(functools.partial(out_kernel, stages=stages), out_shape=[j...  47.5 us
    pallas_call x1, Pallas kernels, device_step(): pl.pallas_call(functools.partial(norm_grad_kernel, stages=stages), out_sh...  44.2 us
    pallas_call x1, Pallas kernels, device_step(): pl.pallas_call(functools.partial(kv_grad_kernel, stages=stages), out_shap...  38.9 us
    all_gather x2, waiting for transfers between devices, device_step(): gathered = [lax.all_gather(kv, 'x') for kv in kv_sides]  37.6 us
    pallas_call x1, Pallas kernels, device_step(): pl.pallas_call(functools.partial(assemble_main_kernel, stages=stages, n_q...  24.1 us
    pallas_call x1, Pallas kernels, q_proj(): pl.pallas_call(drop_scalar(q_proj_kernel), out_shape=q_shapes, grid_spec=...  15.9 us
    pallas_call x2, Pallas kernels, kv_proj(): pl.pallas_call(drop_scalar(kv_proj_kernel), out_shape=[jax.ShapeDtypeStru...  15.7 us
  transfers between devices with their start and end apart: 14, of which 7 were waited for; matrix products, arithmetic and copies ran while one was open for 1% of the time, Pallas kernels for 71%

profile of v6, /device:TPU:112, one launch (start us, length us, event | category | flops | bytes accessed | tf_op | source)
XLA Modules:
  0.0 465.4 jit_solution(6865506884035840050)
XLA Ops:
  7.4 1.3 reshape.72.refs_1_.g_ref
  11.0 7.9 %kv_proj.2 = (bf16[8,128,2048]{2,1,0:T(8,128)(2,1)}, bf16[2,8,128,128]{3,2,1,0:T(8,128)(2,1)}, bf16[3,2,8,128,128]{4,3,2,1,0:T(8,128)(2,1)}) custom-call(s32[2]{0:T(128)} %pad_add_fusion._, bf16[8,128,2048]{2,1,0:T(8,128)(2,1)} %x_ref.3, bf16[1,2048]{1,0:T(2,128)(2,1)} %reshape.72.refs_1_.g_ref, bf16[2048,3072]{1,0:T(8,128)(2,1)} %w_ref.1, ...), custom_call_target="tpu_custom_call" | custom-call | flops 2147483648 | bytes 12582912 | tf_op jit(solution)/shard_map/kv_proj/pallas_call | solution.py:572
  18.9 7.9 %kv_proj.3 = (bf16[8,128,2048]{2,1,0:T(8,128)(2,1)}, bf16[2,8,128,128]{3,2,1,0:T(8,128)(2,1)}, bf16[3,2,8,128,128]{4,3,2,1,0:T(8,128)(2,1)}) custom-call(s32[2]{0:T(128)} %pad_add_fusion._, bf16[8,128,2048]{2,1,0:T(8,128)(2,1)} %collective-permute-done.refs_0_, bf16[1,2048]{1,0:T(2,128)(2,1)} %reshape.72.refs_1_.g_ref, ...), custom_call_target="tpu_custom_call", output_to_operand_aliasing={{1}: (7, {}), {2}: (8, {})} | custom-call | flops 2147483648 | bytes 12582912 | tf_op jit(solution)/shard_map/kv_proj/pallas_call | solution.py:572
  26.9 0.7 all-gather.15.cloned.1.call-update
  28.2 15.9 %q_proj.1 = (bf16[8,1024,128]{2,1,0:T(8,128)(2,1)}, bf16[8,1024,128]{2,1,0:T(8,128)(2,1)}) custom-call(s32[2]{0:T(128)} %pad_add_fusion._, bf16[8,128,2048]{2,1,0:T(8,128)(2,1)} %get-tuple-element.47.refs_0_.h0_ref.refs_4_, bf16[8,128,2048]{2,1,0:T(8,128)(2,1)} %get-tuple-element.50.refs_1_.h1_ref.refs_5_, bf16[2048,3072]{1,0:T(8,128)(2,1)} %w_ref.1, ...), custom_call_target="tpu_custom_call" | custom-call | flops 8589934592 | bytes 25165824 | tf_op jit(solution)/shard_map/q_proj/pallas_call | solution.py:599
  44.1 15.2 %do_proj.1 = (bf16[8,1024,128]{2,1,0:T(8,128)(2,1)}, bf16[8,1024,128]{2,1,0:T(8,128)(2,1)}) custom-call(s32[2]{0:T(128)} %pad_add_fusion._, bf16[8,128,2048]{2,1,0:T(8,128)(2,1)} %go_ref.1, bf16[8,128,2048]{2,1,0:T(8,128)(2,1)} %collective-permute-done.1.refs_1_.g1_ref, bf16[2048,2048]{1,0:T(8,128)(2,1)} %bitcast.26), custom_call_target="tpu_custom_call" | custom-call | flops 8589934592 | bytes 25165824 | tf_op jit(solution)/shard_map/do_proj/pallas_call | solution.py:610
  59.2 23.0 %shard_map.101 = (bf16[2,8,256,128]{3,2,1,0:T(8,128)(2,1)}, bf16[2,8,256,128]{3,2,1,0:T(8,128)(2,1)}, bf16[4,256,2048]{2,1,0:T(8,128)(2,1)}) custom-call(bf16[8,1024,128]{2,1,0:T(8,128)(2,1)} %get-tuple-element.51.q0_ref, bf16[8,1024,128]{2,1,0:T(8,128)(2,1)} %get-tuple-element.52.q1_ref, bf16[8,1024,128]{2,1,0:T(8,128)(2,1)} %get-tuple-element.53.do0_ref, ...), custom_call_target="tpu_custom_call" | custom-call | flops 40000000000 | bytes 30000000 | tf_op jit(solution)/shard_map/pallas_call | solution.py:645
  82.2 37.6 %all-gather.15.cloned.1.call-done = bf16[12,2,8,128,128]{4,3,2,1,0:T(8,128)(2,1)} async-done(((bf16[3,2,8,128,128]{4,3,2,1,0:T(8,128)(2,1)}), bf16[12,2,8,128,128]{4,3,2,1,0:T(8,128)(2,1)}) %all-gather.15.cloned.1.call-update) | async-done | bytes 6291472 | tf_op jit(solution)/shard_map/all_gather | solution.py:622
  119.8 44.5 %shard_map.102 = (bf16[2,8,256,128]{3,2,1,0:T(8,128)(2,1)}, bf16[2,8,256,128]{3,2,1,0:T(8,128)(2,1)}, bf16[4,256,2048]{2,1,0:T(8,128)(2,1)}, bf16[128,2048]{1,0:T(8,128)(2,1)}, bf16[128,2048]{1,0:T(8,128)(2,1)}) custom-call(bf16[8,1024,128]{2,1,0:T(8,128)(2,1)} %get-tuple-element.51.q0_ref, bf16[8,1024,128]{2,1,0:T(8,128)(2,1)} %get-tuple-element.52.q1_ref, ...), custom_call_target="tpu_custom_call" | custom-call | flops 40000000000 | bytes 30000000 | tf_op jit(solution)/shard_map/pallas_call | solution.py:645
  164.5 69.2 %shard_map.103 = (bf16[2,8,256,128]{3,2,1,0:T(8,128)(2,1)}, bf16[2,8,256,128]{3,2,1,0:T(8,128)(2,1)}, bf16[4,256,2048]{2,1,0:T(8,128)(2,1)}, bf16[128,2048]{1,0:T(8,128)(2,1)}, bf16[128,2048]{1,0:T(8,128)(2,1)}) custom-call(bf16[8,1024,128]{2,1,0:T(8,128)(2,1)} %get-tuple-element.51.q0_ref, bf16[8,1024,128]{2,1,0:T(8,128)(2,1)} %get-tuple-element.52.q1_ref, ...), custom_call_target="tpu_custom_call" | custom-call | flops 40000000000 | bytes 30000000 | tf_op jit(solution)/shard_map/pallas_call | solution.py:645
  233.7 44.0 %shard_map.104 = (bf16[2,8,256,128]{3,2,1,0:T(8,128)(2,1)}, bf16[2,8,256,128]{3,2,1,0:T(8,128)(2,1)}, bf16[4,256,2048]{2,1,0:T(8,128)(2,1)}, bf16[128,2048]{1,0:T(8,128)(2,1)}, bf16[128,2048]{1,0:T(8,128)(2,1)}) custom-call(bf16[8,1024,128]{2,1,0:T(8,128)(2,1)} %get-tuple-element.51.q0_ref, bf16[8,1024,128]{2,1,0:T(8,128)(2,1)} %get-tuple-element.52.q1_ref, ...), custom_call_target="tpu_custom_call" | custom-call | flops 40000000000 | bytes 30000000 | tf_op jit(solution)/shard_map/pallas_call | solution.py:645
  279.5 1.6 collective-permute-done.2.refs_4_
  281.2 1.5 collective-permute-done.3.refs_5_
  282.7 1.0 copy-done.5
  284.2 1.0 copy-done.6
  285.7 1.0 copy-done.7
  286.7 47.5 %out_proj.1 = (bf16[8,128,2048]{2,1,0:T(8,128)(2,1)}, bf16[128,2048]{1,0:T(8,128)(2,1)}) custom-call(bf16[8,128,2048]{2,1,0:T(8,128)(2,1)} %x_ref.3, bf16[2048,2048]{1,0:T(8,128)(2,1)} %bitcast.27, bf16[4,256,2048]{2,1,0:T(8,128)(2,1)} %get-tuple-element.66.prev_ref.refs_8_, bf16[2,8,256,128]{3,2,1,0:T(8,128)(2,1)} %get-tuple-element.67.refs_0_, ...), custom_call_target="tpu_custom_call" | custom-call | flops 8589934592 | bytes 30000000 | tf_op jit(solution)/shard_map/out_proj/pallas_call | solution.py:679
  334.1 38.9 %kv_grad.1 = (bf16[8,512,128]{2,1,0:T(8,128)(2,1)}, bf16[8,512,128]{2,1,0:T(8,128)(2,1)}, bf16[4,128,2048]{2,1,0:T(8,128)(2,1)}, bf16[128,2048]{1,0:T(8,128)(2,1)}) custom-call(bf16[128,2048]{1,0:T(8,128)(2,1)} %get-tuple-element.63.refs_0_, bf16[128,2048]{1,0:T(8,128)(2,1)} %get-tuple-element.64.refs_1_, bf16[128,2048]{1,0:T(8,128)(2,1)} %get-tuple-element.65.refs_2_, ...), custom_call_target="tpu_custom_call" | custom-call | flops 4294967296 | bytes 30000000 | tf_op jit(solution)/shard_map/kv_grad/pallas_call | solution.py:695
  373.2 3.0 collective-permute-done.6.kv1_ref
  376.3 1.0 copy-done.8
  377.2 44.2 %norm_grad.1 = (bf16[8,128,2048]{2,1,0:T(8,128)(2,1)}, bf16[144,2048]{1,0:T(8,128)(2,1)}) custom-call(bf16[8,128,2048]{2,1,0:T(8,128)(2,1)} %x_ref.3, bf16[8,128,2048]{2,1,0:T(8,128)(2,1)} %go_ref.1, bf16[1,2048]{1,0:T(2,128)(2,1)} %reshape.72.refs_1_.g_ref, bf16[2048,3072]{1,0:T(8,128)(2,1)} %w_ref.1, bf16[8,512,128]{2,1,0:T(8,128)(2,1)} %get-tuple-element.78.kv0_ref, ...), custom_call_target="tpu_custom_call" | custom-call | flops 12884901888 | bytes 40000000 | tf_op jit(solution)/shard_map/norm_grad/pallas_call | solution.py:714
  421.6 24.1 %assemble_main.1 = (f32[2048,3072]{1,0:T(8,128)}, f32[32,64,2048]{2,1,0:T(8,128)}, bf16[8,128,2048]{2,1,0:T(8,128)(2,1)}, bf16[8,128,2048]{2,1,0:T(8,128)(2,1)}) custom-call(bf16[4,2,128,2048]{3,2,1,0:T(8,128)(2,1)} %bitcast.22, bf16[4,2,128,2048]{3,2,1,0:T(8,128)(2,1)} %bitcast.24, bf16[4,2,128,2048]{3,2,1,0:T(8,128)(2,1)} %bitcast.23, ...), custom_call_target="tpu_custom_call" | custom-call | flops 2000000000 | bytes 60000000 | tf_op jit(solution)/shard_map/assemble_main/pallas_call | solution.py:731
  445.7 6.2 %all-gather.27.cloned.1.call-done = bf16[1152,2048]{1,0:T(8,128)(2,1)} async-done(((bf16[144,2048]{1,0:T(8,128)(2,1)}), bf16[1152,2048]{1,0:T(8,128)(2,1)}) %all-gather.27.cloned.1.call-update) | async-done | bytes 4718608 | tf_op jit(solution)/shard_map/all_gather | solution.py:632
  451.8 6.5 %assemble_tail.1 = (f32[2048,3072]{1,0:T(8,128)}, f32[1,2048]{1,0:T(1,128)}) custom-call(bf16[4,2,144,2048]{3,2,1,0:T(8,128)(2,1)} %bitcast.20, bf16[4,2,144,2048]{3,2,1,0:T(8,128)(2,1)} %bitcast.21, f32[2048,3072]{1,0:T(8,128)} %get-tuple-element.85._), custom_call_target="tpu_custom_call", output_to_operand_aliasing={{0}: (2, {})} | custom-call | flops 1000000000 | bytes 20000000 | tf_op jit(solution)/shard_map/assemble_tail/pallas_call | solution.py:743
  (49 shorter events, 6.5 us)
Async XLA Ops:
  7.2 52.1 %all-gather.17.cloned.1.call-start = ((), (), s32[]{:S(2)}) async-start(), calls=%async_computation.1 | async-start | bytes 2621440 | tf_op jit(solution)/shard_map/all_gather | solution.py:622
  7.2 11.6 %collective-permute-start = (bf16[8,128,2048]{2,1,0:T(8,128)(2,1)}, bf16[8,128,2048]{2,1,0:T(8,128)(2,1)}, u32[]{:S(2)}, u32[]{:S(2)}) collective-permute-start(bf16[8,128,2048]{2,1,0:T(8,128)(2,1)} %x_ref.3), channel_id=1, source_target_pairs={{0,1},{1,0},{2,3},{3,2},{4,5},{5,4},{6,7},{7,6},{8,9},{9,8},{10,11... | collective-permute-start | bytes 12582920 | tf_op jit(solution)/shard_map/ppermute | solution.py:551
  10.3 8.5 %copy-start = (f32[2,32,128]{2,1,0:T(8,128)}, f32[2,32,128]{2,1,0:T(8,128)S(1)}, u32[]{:S(2)}) copy-start(f32[2,32,128]{2,1,0:T(8,128)S(1)} %get-tuple-element.93.refs_4_.sin_ref.refs_7_) | copy-start | bytes 98308
  10.3 8.5 %copy-start.1 = (f32[2,32,128]{2,1,0:T(8,128)}, f32[2,32,128]{2,1,0:T(8,128)S(1)}, u32[]{:S(2)}) copy-start(f32[2,32,128]{2,1,0:T(8,128)S(1)} %get-tuple-element.94.refs_3_.cos_ref.refs_6_) | copy-start | bytes 98308
  26.8 93.0 %all-gather.15.cloned.1.call-start = ((), (), s32[]{:S(2)}) async-start(), calls=%async_computation | async-start | bytes 7864320 | tf_op jit(solution)/shard_map/all_gather | solution.py:622
  27.6 393.9 %all-gather.19.cloned.1.call-start = ((), (), s32[]{:S(2)}) async-start(), calls=%async_computation.2 | async-start | bytes 4718592 | tf_op jit(solution)/shard_map/all_gather | solution.py:632
  27.7 16.4 %collective-permute-start.1 = (bf16[8,128,2048]{2,1,0:T(8,128)(2,1)}, bf16[8,128,2048]{2,1,0:T(8,128)(2,1)}, u32[]{:S(2)}, u32[]{:S(2)}) collective-permute-start(bf16[8,128,2048]{2,1,0:T(8,128)(2,1)} %go_ref.1), channel_id=1, source_target_pairs={{0,1},{1,0},{2,3},{3,2},{4,5},{5,4},{6,7},{7,6},{8,9},{9,8},{10,11... | collective-permute-start | bytes 12582920 | tf_op jit(solution)/shard_map/ppermute | solution.py:552
  164.4 257.1 %all-gather.23.cloned.1.call-start = ((), (), s32[]{:S(2)}) async-start(), calls=%async_computation.4 | async-start | bytes 4718592 | tf_op jit(solution)/shard_map/all_gather | solution.py:632
  233.7 44.8 %copy-start.2 = (bf16[2,8,256,128]{3,2,1,0:T(8,128)(2,1)S(1)}, bf16[2,8,256,128]{3,2,1,0:T(8,128)(2,1)}, u32[]{:S(2)}) copy-start(bf16[2,8,256,128]{3,2,1,0:T(8,128)(2,1)} %get-tuple-element.71) | copy-start | bytes 3145732
  233.7 44.9 %copy-start.4 = (bf16[2,8,256,128]{3,2,1,0:T(8,128)(2,1)S(1)}, bf16[2,8,256,128]{3,2,1,0:T(8,128)(2,1)}, u32[]{:S(2)}) copy-start(bf16[2,8,256,128]{3,2,1,0:T(8,128)(2,1)} %get-tuple-element.72) | copy-start | bytes 3145732
  277.7 143.8 %all-gather.21.cloned.1.call-start = ((), (), s32[]{:S(2)}) async-start(), calls=%async_computation.3 | async-start | bytes 4718592 | tf_op jit(solution)/shard_map/all_gather | solution.py:632
  278.4 143.2 %all-gather.25.cloned.1.call-start = ((), (), s32[]{:S(2)}) async-start(), calls=%async_computation.5 | async-start | bytes 4718592 | tf_op jit(solution)/shard_map/all_gather | solution.py:632
  278.5 2.7 collective-permute-start.2
  278.6 4.1 collective-permute-start.3
  279.0 5.1 %collective-permute-start.5 = (bf16[2,8,256,128]{3,2,1,0:T(8,128)(2,1)}, bf16[2,8,256,128]{3,2,1,0:T(8,128)(2,1)S(1)}, u32[]{:S(2)}, u32[]{:S(2)}) collective-permute-start(bf16[2,8,256,128]{3,2,1,0:T(8,128)(2,1)} %get-tuple-element.74), channel_id=1, source_target_pairs={{0,1},{1,0},{2,3},{3,2},{4,5},{5,4},{6,7},{7,6},{8,9},{9,8},{10,11... | collective-permute-start | bytes 3145736 | tf_op jit(solution)/shard_map/ppermute | solution.py:672
  279.1 6.5 %collective-permute-start.4 = (bf16[2,8,256,128]{3,2,1,0:T(8,128)(2,1)}, bf16[2,8,256,128]{3,2,1,0:T(8,128)(2,1)S(1)}, u32[]{:S(2)}, u32[]{:S(2)}) collective-permute-start(bf16[2,8,256,128]{3,2,1,0:T(8,128)(2,1)} %get-tuple-element.73), channel_id=1, source_target_pairs={{0,1},{1,0},{2,3},{3,2},{4,5},{5,4},{6,7},{7,6},{8,9},{9,8},{10,11... | collective-permute-start | bytes 3145736 | tf_op jit(solution)/shard_map/ppermute | solution.py:672
  281.2 5.5 %copy-start.3 = (bf16[2,8,256,128]{3,2,1,0:T(8,128)(2,1)}, bf16[2,8,256,128]{3,2,1,0:T(8,128)(2,1)S(1)}, u32[]{:S(2)}) copy-start(bf16[2,8,256,128]{3,2,1,0:T(8,128)(2,1)S(1)} %collective-permute-done.2.refs_4_) | copy-start | bytes 3145732
  282.7 1.0 copy-start.5
  284.2 1.0 copy-start.6
  285.7 1.0 copy-start.7
  373.1 78.7 %all-gather.27.cloned.1.call-start = ((), (), s32[]{:S(2)}) async-start(), calls=%async_computation.6 | async-start | bytes 5308416 | tf_op jit(solution)/shard_map/all_gather | solution.py:632
  373.1 3.1 collective-permute-start.6
  376.3 1.0 copy-start.8
Sparse Core Ops, SparseCore 0:
  26.9 29.6 all-gather.16
  58.2 61.5 all-gather.14
  164.5 55.6 all-gather.18
  277.8 54.4 all-gather.22
  333.8 41.6 all-gather.20
  377.0 41.9 all-gather.24
  421.6 30.1 all-gather.26

commit v7 on v6

--- a/solution.py
+++ b/solution.py
@@ -61,8 +61,8 @@
 def kv_proj_kernel(x_ref, g_ref, wk_ref, wv_ref, cos_ref, sin_ref, *refs):
     nb, tok, d = x_ref.shape
     stages = (wk_ref.shape[1] // (PAIR * cos_ref.shape[0]))
-    h_ref, first_ref, rest_ref = refs[-3:]
-    kv_refs = [first_ref] + [rest_ref.at[i] for i in range(stages - 1)]
+    h_ref, first_ref, second_ref, rest_ref = refs[-4:]
+    kv_refs = [first_ref, second_ref] + [rest_ref.at[i] for i in range(stages - 2)]
     e2 = first_ref.shape[2]
     e = e2 // 2
     x = x_ref[:].reshape(nb * tok, d).astype(F32)
@@ -78,43 +78,31 @@
             kv_refs[i][0, b, e:PAIR * e] = v[i * e:(i + 1) * e, b * tok:(b + 1) * tok].astype(BF16)
 
 
-def q_proj_kernel(h0_ref, h1_ref, w_ref, cos_ref, sin_ref, q0_ref, q1_ref):
+def q_do_proj_kernel(h0_ref, h1_ref, g0_ref, g1_ref, wq_ref, wo_ref, cos_ref, sin_ref, q0_ref, q1_ref, do0_ref, do1_ref):
     nb, tok, d = h0_ref.shape
     e = PAIR * cos_ref.shape[1]
-    rows = w_ref.shape[1]
+    rows = wo_ref.shape[0]
     scale = e ** -0.5
     step = 4 * e
 
-    def run(h_ref, q_ref, side):
+    def run(h_ref, g_ref, q_ref, do_ref, side):
         h = h_ref[:].reshape(nb * tok, d)
+        g = g_ref[:].reshape(nb * tok, d)
         cos, sin = cos_ref[side], sin_ref[side]
         for r in range(0, rows, step):
-            blk = dot(h, w_ref[:, r:r + step]).T
+            blk = dot(h, wq_ref[:, r:r + step]).T
             for i in range(0, step, e):
                 for b in range(nb):
                     q_ref[b, r + i:r + i + e] = (rope_rows(blk[i:i + e, b * tok:(b + 1) * tok], cos, sin, 1.0).astype(BF16)
                                                  * scale).astype(BF16)
+        for r in range(0, rows, 512):
+            blk = dot(wo_ref[r:r + 512], g, NT)
+            for b in range(nb):
+                do_ref[b, r:r + 512] = blk[:, b * tok:(b + 1) * tok].astype(BF16)
 
     half = pl.num_programs(0) // 2
-    pl.when(pl.program_id(0) < half)(lambda: run(h0_ref, q0_ref, 0))
-    pl.when(pl.program_id(0) >= half)(lambda: run(h1_ref, q1_ref, 1))
-
-
-def do_proj_kernel(g0_ref, g1_ref, w_ref, o0_ref, o1_ref):
-    nb, tok, d = g0_ref.shape
-    rows = w_ref.shape[0]
-    step = 512
-
-    def run(g_ref, o_ref):
-        g = g_ref[:].reshape(nb * tok, d)
-        for r in range(0, rows, step):
-            blk = dot(w_ref[r:r + step], g, NT)
-            for b in range(nb):
-                o_ref[b, r:r + step] = blk[:, b * tok:(b + 1) * tok].astype(BF16)
-
-    half = pl.num_programs(0) // 2
-    pl.when(pl.program_id(0) < half)(lambda: run(g0_ref, o0_ref))
-    pl.when(pl.program_id(0) >= half)(lambda: run(g1_ref, o1_ref))
+    pl.when(pl.program_id(0) < half)(lambda: run(h0_ref, g0_ref, q0_ref, do0_ref, 0))
+    pl.when(pl.program_id(0) >= half)(lambda: run(h1_ref, g1_ref, q1_ref, do1_ref, 1))
 
 
 def drop_scalar(kernel):
@@ -545,7 +533,7 @@
         chip = lax.axis_index('x')
         core = lax.axis_index('core')
         ids = jnp.stack([chip, core]).astype(jnp.int32)
-        tiles = 2
+        tiles = 4
         nb = n_batch // tiles
 
         x_par = lax.ppermute(hidden, 'core', swap)
@@ -572,15 +560,16 @@
             return pl.pallas_call(
                 drop_scalar(kv_proj_kernel),
                 out_shape=[jax.ShapeDtypeStruct((n_batch, tok, d), BF16)]
-                + [jax.ShapeDtypeStruct((2, n_batch, e2, tok), BF16), jax.ShapeDtypeStruct((stages - 1, 2, n_batch, e2, tok), BF16)],
+                + [jax.ShapeDtypeStruct((2, n_batch, e2, tok), BF16)] * PAIR
+                + [jax.ShapeDtypeStruct((stages - 2, 2, n_batch, e2, tok), BF16)],
                 grid_spec=pltpu.PrefetchScalarGridSpec(
                     num_scalar_prefetch=1, grid=(kt,),
                     in_specs=[x_spec, whole(1, d),
                               pl.BlockSpec((d, kv_half), lambda i, c: (0, kb + c[1])),
                               pl.BlockSpec((d, kv_half), lambda i, c: (0, kb + CORES + c[1])), rot_spec, rot_spec]
                     + [any_spec] * len(filled),
-                    out_specs=[x_spec, pl.BlockSpec((1, kn, e2, tok), lambda i, _: (side, i, 0, 0)),
-                               pl.BlockSpec((stages - 1, 1, kn, e2, tok), lambda i, _: (0, side, i, 0, 0))]),
+                    out_specs=[x_spec] + [pl.BlockSpec((1, kn, e2, tok), lambda i, _: (side, i, 0, 0))] * PAIR
+                    + [pl.BlockSpec((stages - 2, 1, kn, e2, tok), lambda i, _: (0, side, i, 0, 0))]),
                 input_output_aliases={7 + i: 1 + i for i in range(len(filled))},
                 compiler_params=params(), name='kv_proj',
                 cost_estimate=cost(PAIR * n_batch * tok * d * PAIR * kv_half, 3 * n_batch * tok * d * 2),
@@ -593,35 +582,24 @@
         own_out = pl.BlockSpec((nb, q_half, tok), lambda i, _: (first(i), 0, 0))
         par_out = pl.BlockSpec((nb, q_half, tok), lambda i, _: (second(i), 0, 0))
         both_rot = whole(2, half_rot, tok)
-        q_shapes = (jax.ShapeDtypeStruct((n_batch, q_half, tok), BF16), jax.ShapeDtypeStruct((n_batch, q_half, tok), BF16))
-
-        def q_proj(h0, h1):
+        q_shapes = [jax.ShapeDtypeStruct((n_batch, q_half, tok), BF16)] * PAIR
+
+        def q_do_proj(h0, h1, g0, g1):
             return pl.pallas_call(
-                drop_scalar(q_proj_kernel), out_shape=q_shapes,
+                drop_scalar(q_do_proj_kernel), out_shape=q_shapes * PAIR,
                 grid_spec=pltpu.PrefetchScalarGridSpec(
                     num_scalar_prefetch=1, grid=(PAIR * tiles,),
-                    in_specs=[own_spec, par_spec, pl.BlockSpec((d, q_half), lambda i, c: (0, c[1])), both_rot, both_rot],
-                    out_specs=(own_out, par_out)),
-                compiler_params=params(), name='q_proj',
-                cost_estimate=cost(4 * n_batch * tok * d * q_half, 6 * n_batch * tok * d * 2),
-            )(ids, h0, h1, w_qkv, cos_t, sin_t)
-
-        def do_proj(g0, g1):
-            return pl.pallas_call(
-                drop_scalar(do_proj_kernel), out_shape=q_shapes,
-                grid_spec=pltpu.PrefetchScalarGridSpec(
-                    num_scalar_prefetch=1, grid=(PAIR * tiles,),
-                    in_specs=[own_spec, par_spec, pl.BlockSpec((q_half, d), lambda i, c: (c[1], 0))],
-                    out_specs=(own_out, par_out)),
-                compiler_params=params(), name='do_proj',
-                cost_estimate=cost(4 * n_batch * tok * d * q_half, 6 * n_batch * tok * d * 2),
-            )(ids, g0, g1, w_o)
+                    in_specs=[own_spec, par_spec, own_spec, par_spec, pl.BlockSpec((d, q_half), lambda i, c: (0, c[1])),
+                              pl.BlockSpec((q_half, d), lambda i, c: (c[1], 0)), both_rot, both_rot],
+                    out_specs=[own_out, par_out] * PAIR),
+                compiler_params=params(), name='q_do_proj',
+                cost_estimate=cost(8 * n_batch * tok * d * q_half, 8 * n_batch * tok * d * 2),
+            )(ids, h0, h1, g0, g1, w_qkv, w_o, cos_t, sin_t)
 
         h_own, *kv_sides = kv_proj(hidden, 0, [])
         h_par, *kv_sides = kv_proj(x_par, 1, kv_sides)
         gathered = [lax.all_gather(kv, 'x') for kv in kv_sides]
-        q_own, q_par = q_proj(h_own, h_par)
-        do_own, do_par = do_proj(grad_out, go_par)
+        q_own, q_par, do_own, do_par = q_do_proj(h_own, h_par, grad_out, go_par)
 
         n_g = PAIR * rows // chips
         n_s = e2 + n_g
@@ -634,10 +612,10 @@
         def attention(s, prev):
             blk = PAIR * tok
             has_sum = prev is not None
-            if s == 0:
+            if s < 2:
                 kv_spec = along(2, chips, 2, 1, e2, tok)
             else:
-                kv_spec = pl.BlockSpec((chips, None, 2, 1, e2, tok), lambda b: (0, s - 1, 0, b, 0, 0))
+                kv_spec = pl.BlockSpec((chips, None, 2, 1, e2, tok), lambda b: (0, s - 2, 0, b, 0, 0))
             q_spec = pl.BlockSpec((1, rows, tok), lambda b: (b, s, 0))
             t_spec = pl.BlockSpec((2, tok, d), lambda b: (b // 2, 0, 0))
             r_spec = whole(2, half_rot, tok)
@@ -661,7 +639,7 @@
                 + RingSum.scratch(n_s, d) * has_sum,
                 compiler_params=comm_params(s) if has_sum else params(),
                 cost_estimate=cost(4e10, 3e7, 3e7),
-            )(q_own, q_par, do_own, do_par, gathered[min(s, 1)], h_own, h_par, grad_out, go_par, cos_t, sin_t,
+            )(q_own, q_par, do_own, do_par, gathered[min(s, 2)], h_own, h_par, grad_out, go_par, cos_t, sin_t,
               *([prev] * has_sum))
 
         own, par, totals, main = [], [], [], []
@@ -672,7 +650,8 @@
             par.append(lax.ppermute(par_s, 'core', swap))
             prev = send
             totals += sums[:1]
-            main += [gather_shard(g) for g in sums[1:]]
+            if s < stages - 1:
+                main += [gather_shard(g) for g in sums[1:]]
 
         nb2 = 2
         t2_spec = along(0, nb2, tok, d)
@@ -687,6 +666,8 @@
             compiler_params=comm_params(stages), name='out_proj',
             cost_estimate=cost(PAIR * n_batch * tok * d * n_heads * e, 3e7),
         )(hidden, w_o, prev, *own, *par)
+        late, total = lax.optimization_barrier((sums[-1], total))
+        main.append(gather_shard(late))
         totals.append(total)
 
         gb = 2

time: 474 us -> 466 us (0.983); the launches traced: 465 us -> 462 us
  Pallas kernels: 388 us -> 393 us
    pallas_call x4, Pallas kernels: 181 us -> 227 us  [attention(): pl.pallas_call(functools.partial(attn_kernel, has_sum=has_sum), out_shape...]
    all_gather x2 -> x3, waiting for transfers between devices: 37.6 us -> 1.25 us  [device_step(): gathered = [lax.all_gather(kv, 'x') for kv in kv_sides]]
    all_gather x5, waiting for transfers between devices: 6.24 us -> 32.4 us  [gather_shard(): lax.all_gather(shard, ('x', 'core')).reshape(chips, CORES, *shard.shape)]
    pallas_call x1, Pallas kernels: 47.5 us -> 27.1 us  [device_step(): pl.pallas_call(functools.partial(out_kernel, stages=stages), out_shape=[j...]
    pallas_call x1, Pallas kernels: 38.9 us -> 24.2 us  [device_step(): pl.pallas_call(functools.partial(kv_grad_kernel, stages=stages), out_shap...]
    ppermute x1, waiting for transfers between devices: 0.01 us -> 5.54 us  [device_step(): go_par = lax.ppermute(grad_out, 'core', swap)]
    pallas_call x2 -> x1, Pallas kernels: 31 us -> 26.2 us  [q_do_proj(): pl.pallas_call(drop_scalar(q_do_proj_kernel), out_shape=q_shapes * PAIR,...]
  transfers between devices with their start and end apart: 14 -> 15, of which waited for: 7 -> 7; matrix products, arithmetic and copies ran while one was open for 1% -> 1% of each run, Pallas kernels for 71% -> 82%
where the time goes in v7:
time: 466 us; the launch traced here: 462 us
  Pallas kernels  393 us (84%)
  waiting for transfers between devices  47.9 us (10%)
  between operations  14.5 us (3%)
    pallas_call x4, Pallas kernels, attention(): pl.pallas_call(functools.partial(attn_kernel, has_sum=has_sum), out_shape...  227 us
    pallas_call x1, Pallas kernels, device_step(): pl.pallas_call(functools.partial(norm_grad_kernel, stages=stages), out_sh...  41.8 us
    all_gather x5, waiting for transfers between devices, gather_shard(): lax.all_gather(shard, ('x', 'core')).reshape(chips, CORES, *shard.shape)  32.4 us
    pallas_call x1, Pallas kernels, device_step(): pl.pallas_call(functools.partial(out_kernel, stages=stages), out_shape=[j...  27.1 us
    pallas_call x1, Pallas kernels, q_do_proj(): pl.pallas_call(drop_scalar(q_do_proj_kernel), out_shape=q_shapes * PAIR,...  26.2 us
    pallas_call x1, Pallas kernels, device_step(): pl.pallas_call(functools.partial(kv_grad_kernel, stages=stages), out_shap...  24.2 us
    pallas_call x1, Pallas kernels, device_step(): pl.pallas_call(functools.partial(assemble_main_kernel, stages=stages, n_q...  24 us
    pallas_call x2, Pallas kernels, kv_proj(): pl.pallas_call(drop_scalar(kv_proj_kernel), out_shape=[jax.ShapeDtypeStru...  15.7 us
  transfers between devices with their start and end apart: 15, of which 7 were waited for; matrix products, arithmetic and copies ran while one was open for 1% of the time, Pallas kernels for 82%

profile of v7, /device:TPU:112, one launch (start us, length us, event | category | flops | bytes accessed | tf_op | source)
XLA Modules:
  0.0 462.4 jit_solution(3846105934778564670)
XLA Ops:
  7.4 1.3 reshape.72.refs_1_.g_ref
  9.4 0.7 multiply_divide_fusion
  11.0 7.9 %kv_proj.2 = (bf16[8,128,2048]{2,1,0:T(8,128)(2,1)}, bf16[2,8,128,128]{3,2,1,0:T(8,128)(2,1)}, bf16[2,8,128,128]{3,2,1,0:T(8,128)(2,1)}, bf16[2,2,8,128,128]{4,3,2,1,0:T(8,128)(2,1)}) custom-call(s32[2]{0:T(128)} %pad_add_fusion._, bf16[8,128,2048]{2,1,0:T(8,128)(2,1)} %x_ref.3, bf16[1,2048]{1,0:T(2,128)(2,1)} %reshape.72.refs_1_.g_ref, ...), custom_call_target="tpu_custom_call" | custom-call | flops 2147483648 | bytes 12582912 | tf_op jit(solution)/shard_map/kv_proj/pallas_call | solution.py:560
  18.8 7.9 %kv_proj.3 = (bf16[8,128,2048]{2,1,0:T(8,128)(2,1)}, bf16[2,8,128,128]{3,2,1,0:T(8,128)(2,1)}, bf16[2,8,128,128]{3,2,1,0:T(8,128)(2,1)}, bf16[2,2,8,128,128]{4,3,2,1,0:T(8,128)(2,1)}) custom-call(s32[2]{0:T(128)} %pad_add_fusion._, bf16[8,128,2048]{2,1,0:T(8,128)(2,1)} %collective-permute-done.refs_0_, ...), custom_call_target="tpu_custom_call", output_to_operand_aliasing={{1}: (7, {}), {2}: (8, {}), {3}: (9, {})} | custom-call | flops 2147483648 | bytes 12582912 | tf_op jit(solution)/shard_map/kv_proj/pallas_call | solution.py:560
  27.7 0.7 all-gather.23.cloned.1.call-update
  29.0 5.5 %collective-permute-done.1.refs_3_.g1_ref = bf16[8,128,2048]{2,1,0:T(8,128)(2,1)} collective-permute-done((bf16[8,128,2048]{2,1,0:T(8,128)(2,1)}, bf16[8,128,2048]{2,1,0:T(8,128)(2,1)}, u32[]{:S(2)}, u32[]{:S(2)}) %collective-permute-start.1) | collective-permute-done | bytes 4194336 | tf_op jit(solution)/shard_map/ppermute | solution.py:540
  34.5 26.2 %q_do_proj.1 = (bf16[8,1024,128]{2,1,0:T(8,128)(2,1)}, bf16[8,1024,128]{2,1,0:T(8,128)(2,1)}, bf16[8,1024,128]{2,1,0:T(8,128)(2,1)}, bf16[8,1024,128]{2,1,0:T(8,128)(2,1)}) custom-call(s32[2]{0:T(128)} %pad_add_fusion._, bf16[8,128,2048]{2,1,0:T(8,128)(2,1)} %get-tuple-element.51.refs_0_.h0_ref.refs_4_, ...), custom_call_target="tpu_custom_call" | custom-call | flops 17179869184 | bytes 33554432 | tf_op jit(solution)/shard_map/q_do_proj/pallas_call | solution.py:588
  60.8 22.9 %shard_map.101 = (bf16[2,8,256,128]{3,2,1,0:T(8,128)(2,1)}, bf16[2,8,256,128]{3,2,1,0:T(8,128)(2,1)}, bf16[4,256,2048]{2,1,0:T(8,128)(2,1)}) custom-call(bf16[8,1024,128]{2,1,0:T(8,128)(2,1)} %get-tuple-element.56.q0_ref, bf16[8,1024,128]{2,1,0:T(8,128)(2,1)} %get-tuple-element.57.q1_ref, bf16[8,1024,128]{2,1,0:T(8,128)(2,1)} %get-tuple-element.58.do0_ref, ...), custom_call_target="tpu_custom_call" | custom-call | flops 40000000000 | bytes 30000000 | tf_op jit(solution)/shard_map/pallas_call | solution.py:623
  83.7 1.2 all-gather.17.cloned.1.call-done
  84.9 82.2 %shard_map.102 = (bf16[2,8,256,128]{3,2,1,0:T(8,128)(2,1)}, bf16[2,8,256,128]{3,2,1,0:T(8,128)(2,1)}, bf16[4,256,2048]{2,1,0:T(8,128)(2,1)}, bf16[128,2048]{1,0:T(8,128)(2,1)}, bf16[128,2048]{1,0:T(8,128)(2,1)}) custom-call(bf16[8,1024,128]{2,1,0:T(8,128)(2,1)} %get-tuple-element.56.q0_ref, bf16[8,1024,128]{2,1,0:T(8,128)(2,1)} %get-tuple-element.57.q1_ref, ...), custom_call_target="tpu_custom_call" | custom-call | flops 40000000000 | bytes 30000000 | tf_op jit(solution)/shard_map/pallas_call | solution.py:623
  167.3 61.3 %shard_map.103 = (bf16[2,8,256,128]{3,2,1,0:T(8,128)(2,1)}, bf16[2,8,256,128]{3,2,1,0:T(8,128)(2,1)}, bf16[4,256,2048]{2,1,0:T(8,128)(2,1)}, bf16[128,2048]{1,0:T(8,128)(2,1)}, bf16[128,2048]{1,0:T(8,128)(2,1)}) custom-call(bf16[8,1024,128]{2,1,0:T(8,128)(2,1)} %get-tuple-element.56.q0_ref, bf16[8,1024,128]{2,1,0:T(8,128)(2,1)} %get-tuple-element.57.q1_ref, ...), custom_call_target="tpu_custom_call" | custom-call | flops 40000000000 | bytes 30000000 | tf_op jit(solution)/shard_map/pallas_call | solution.py:623
  229.3 60.5 %shard_map.104 = (bf16[2,8,256,128]{3,2,1,0:T(8,128)(2,1)}, bf16[2,8,256,128]{3,2,1,0:T(8,128)(2,1)}, bf16[4,256,2048]{2,1,0:T(8,128)(2,1)}, bf16[128,2048]{1,0:T(8,128)(2,1)}, bf16[128,2048]{1,0:T(8,128)(2,1)}) custom-call(bf16[8,1024,128]{2,1,0:T(8,128)(2,1)} %get-tuple-element.56.q0_ref, bf16[8,1024,128]{2,1,0:T(8,128)(2,1)} %get-tuple-element.57.q1_ref, ...), custom_call_target="tpu_custom_call" | custom-call | flops 40000000000 | bytes 30000000 | tf_op jit(solution)/shard_map/pallas_call | solution.py:623
  290.4 2.3 collective-permute-done.5.refs_7_
  292.7 1.6 collective-permute-done.4.refs_6_
  294.4 27.1 %out_proj.1 = (bf16[8,128,2048]{2,1,0:T(8,128)(2,1)}, bf16[128,2048]{1,0:T(8,128)(2,1)}) custom-call(bf16[8,128,2048]{2,1,0:T(8,128)(2,1)} %x_ref.3, bf16[2048,2048]{1,0:T(8,128)(2,1)} %bitcast.28, bf16[4,256,2048]{2,1,0:T(8,128)(2,1)} %get-tuple-element.69.prev_ref.refs_8_, bf16[2,8,256,128]{3,2,1,0:T(8,128)(2,1)} %get-tuple-element.70.refs_0_, ...), custom_call_target="tpu_custom_call" | custom-call | flops 8589934592 | bytes 30000000 | tf_op jit(solution)/shard_map/out_proj/pallas_call | solution.py:658
  321.5 24.2 %kv_grad.1 = (bf16[8,512,128]{2,1,0:T(8,128)(2,1)}, bf16[8,512,128]{2,1,0:T(8,128)(2,1)}, bf16[4,128,2048]{2,1,0:T(8,128)(2,1)}, bf16[128,2048]{1,0:T(8,128)(2,1)}) custom-call(bf16[128,2048]{1,0:T(8,128)(2,1)} %get-tuple-element.80.refs_0_, bf16[128,2048]{1,0:T(8,128)(2,1)} %get-tuple-element.81.refs_1_, bf16[128,2048]{1,0:T(8,128)(2,1)} %get-tuple-element.82.refs_2_, ...), custom_call_target="tpu_custom_call" | custom-call | flops 4294967296 | bytes 30000000 | tf_op jit(solution)/shard_map/kv_grad/pallas_call | solution.py:676
  345.8 0.7 all-gather.27.cloned.1.call-update
  346.7 2.8 collective-permute-done.6.kv1_ref
  349.6 1.0 copy-done.5
  350.5 41.8 %norm_grad.1 = (bf16[8,128,2048]{2,1,0:T(8,128)(2,1)}, bf16[144,2048]{1,0:T(8,128)(2,1)}) custom-call(bf16[8,128,2048]{2,1,0:T(8,128)(2,1)} %x_ref.3, bf16[8,128,2048]{2,1,0:T(8,128)(2,1)} %go_ref.1, bf16[1,2048]{1,0:T(2,128)(2,1)} %reshape.72.refs_1_.g_ref, bf16[2048,3072]{1,0:T(8,128)(2,1)} %w_ref.1, bf16[8,512,128]{2,1,0:T(8,128)(2,1)} %get-tuple-element.86.kv0_ref, ...), custom_call_target="tpu_custom_call" | custom-call | flops 12884901888 | bytes 40000000 | tf_op jit(solution)/shard_map/norm_grad/pallas_call | solution.py:695
  392.5 24.7 %all-gather.27.cloned.1.call-done = bf16[1024,2048]{1,0:T(8,128)(2,1)} async-done(((bf16[128,2048]{1,0:T(8,128)(2,1)}), bf16[1024,2048]{1,0:T(8,128)(2,1)}) %all-gather.27.cloned.1.call-update) | async-done | bytes 4194320 | tf_op jit(solution)/shard_map/all_gather | solution.py:610
  417.2 24.0 %assemble_main.1 = (f32[2048,3072]{1,0:T(8,128)}, f32[32,64,2048]{2,1,0:T(8,128)}, bf16[8,128,2048]{2,1,0:T(8,128)(2,1)}, bf16[8,128,2048]{2,1,0:T(8,128)(2,1)}) custom-call(bf16[4,2,128,2048]{3,2,1,0:T(8,128)(2,1)} %bitcast.23, bf16[4,2,128,2048]{3,2,1,0:T(8,128)(2,1)} %bitcast.24, bf16[4,2,128,2048]{3,2,1,0:T(8,128)(2,1)} %bitcast.26, ...), custom_call_target="tpu_custom_call" | custom-call | flops 2000000000 | bytes 60000000 | tf_op jit(solution)/shard_map/assemble_main/pallas_call | solution.py:712
  441.2 7.7 %all-gather.31.cloned.1.call-done = bf16[1152,2048]{1,0:T(8,128)(2,1)} async-done(((bf16[144,2048]{1,0:T(8,128)(2,1)}), bf16[1152,2048]{1,0:T(8,128)(2,1)}) %all-gather.31.cloned.1.call-update) | async-done | bytes 4718608 | tf_op jit(solution)/shard_map/all_gather | solution.py:610
  448.9 6.5 %assemble_tail.1 = (f32[2048,3072]{1,0:T(8,128)}, f32[1,2048]{1,0:T(1,128)}) custom-call(bf16[4,2,144,2048]{3,2,1,0:T(8,128)(2,1)} %bitcast.21, bf16[4,2,144,2048]{3,2,1,0:T(8,128)(2,1)} %bitcast.22, f32[2048,3072]{1,0:T(8,128)} %get-tuple-element.93._), custom_call_target="tpu_custom_call", output_to_operand_aliasing={{0}: (2, {})} | custom-call | flops 1000000000 | bytes 20000000 | tf_op jit(solution)/shard_map/assemble_tail/pallas_call | solution.py:724
  (45 shorter events, 5.1 us)
Async XLA Ops:
  7.2 53.6 %all-gather.19.cloned.1.call-start = ((), (), s32[]{:S(2)}) async-start(), calls=%async_computation.1 | async-start | bytes 2621440 | tf_op jit(solution)/shard_map/all_gather | solution.py:601
  7.2 11.6 %collective-permute-start = (bf16[8,128,2048]{2,1,0:T(8,128)(2,1)}, bf16[8,128,2048]{2,1,0:T(8,128)(2,1)}, u32[]{:S(2)}, u32[]{:S(2)}) collective-permute-start(bf16[8,128,2048]{2,1,0:T(8,128)(2,1)} %x_ref.3), channel_id=1, source_target_pairs={{0,1},{1,0},{2,3},{3,2},{4,5},{5,4},{6,7},{7,6},{8,9},{9,8},{10,11... | collective-permute-start | bytes 12582920 | tf_op jit(solution)/shard_map/ppermute | solution.py:539
  10.3 8.5 %copy-start = (f32[2,32,128]{2,1,0:T(8,128)}, f32[2,32,128]{2,1,0:T(8,128)S(1)}, u32[]{:S(2)}) copy-start(f32[2,32,128]{2,1,0:T(8,128)S(1)} %get-tuple-element.101.refs_7_.sin_ref) | copy-start | bytes 98308
  10.3 8.5 %copy-start.1 = (f32[2,32,128]{2,1,0:T(8,128)}, f32[2,32,128]{2,1,0:T(8,128)S(1)}, u32[]{:S(2)}) copy-start(f32[2,32,128]{2,1,0:T(8,128)S(1)} %get-tuple-element.102.refs_6_.cos_ref) | copy-start | bytes 98308
  26.8 58.1 %all-gather.17.cloned.1.call-start = ((), (), s32[]{:S(2)}) async-start(), calls=%async_computation | async-start | bytes 2621440 | tf_op jit(solution)/shard_map/all_gather | solution.py:601
  26.9 7.7 %collective-permute-start.1 = (bf16[8,128,2048]{2,1,0:T(8,128)(2,1)}, bf16[8,128,2048]{2,1,0:T(8,128)(2,1)}, u32[]{:S(2)}, u32[]{:S(2)}) collective-permute-start(bf16[8,128,2048]{2,1,0:T(8,128)(2,1)} %go_ref.1), channel_id=1, source_target_pairs={{0,1},{1,0},{2,3},{3,2},{4,5},{5,4},{6,7},{7,6},{8,9},{9,8},{10,11... | collective-permute-start | bytes 12582920 | tf_op jit(solution)/shard_map/ppermute | solution.py:540
  27.6 139.7 %all-gather.23.cloned.1.call-start = ((), (), s32[]{:S(2)}) async-start(), calls=%async_computation.3 | async-start | bytes 5242880 | tf_op jit(solution)/shard_map/all_gather | solution.py:601
  28.4 364.0 %all-gather.21.cloned.1.call-start = ((), (), s32[]{:S(2)}) async-start(), calls=%async_computation.2 | async-start | bytes 4718592 | tf_op jit(solution)/shard_map/all_gather | solution.py:610
  167.2 225.3 %all-gather.25.cloned.1.call-start = ((), (), s32[]{:S(2)}) async-start(), calls=%async_computation.4 | async-start | bytes 4718592 | tf_op jit(solution)/shard_map/all_gather | solution.py:610
  228.6 163.9 %all-gather.29.cloned.1.call-start = ((), (), s32[]{:S(2)}) async-start(), calls=%async_computation.6 | async-start | bytes 4718592 | tf_op jit(solution)/shard_map/all_gather | solution.py:610
  228.7 61.7 %collective-permute-start.3 = (bf16[2,8,256,128]{3,2,1,0:T(8,128)(2,1)}, bf16[2,8,256,128]{3,2,1,0:T(8,128)(2,1)S(1)}, u32[]{:S(2)}, u32[]{:S(2)}) collective-permute-start(bf16[2,8,256,128]{3,2,1,0:T(8,128)(2,1)} %get-tuple-element.75), channel_id=1, source_target_pairs={{0,1},{1,0},{2,3},{3,2},{4,5},{5,4},{6,7},{7,6},{8,9},{9,8},{10,11... | collective-permute-start | bytes 3145736 | tf_op jit(solution)/shard_map/ppermute | solution.py:650
  228.8 61.6 %collective-permute-start.2 = (bf16[2,8,256,128]{3,2,1,0:T(8,128)(2,1)}, bf16[2,8,256,128]{3,2,1,0:T(8,128)(2,1)S(1)}, u32[]{:S(2)}, u32[]{:S(2)}) collective-permute-start(bf16[2,8,256,128]{3,2,1,0:T(8,128)(2,1)} %get-tuple-element.74), channel_id=1, source_target_pairs={{0,1},{1,0},{2,3},{3,2},{4,5},{5,4},{6,7},{7,6},{8,9},{9,8},{10,11... | collective-permute-start | bytes 3145736 | tf_op jit(solution)/shard_map/ppermute | solution.py:650
  289.8 2.9 collective-permute-start.5
  289.9 4.5 collective-permute-start.4
  290.4 4.0 copy-start.2
  290.4 4.0 copy-start.3
  292.7 1.6 copy-start.4
  345.7 71.4 %all-gather.27.cloned.1.call-start = ((), (), s32[]{:S(2)}) async-start(), calls=%async_computation.5 | async-start | bytes 4718592 | tf_op jit(solution)/shard_map/all_gather | solution.py:610
  346.6 102.3 %all-gather.31.cloned.1.call-start = ((), (), s32[]{:S(2)}) async-start(), calls=%async_computation.7 | async-start | bytes 5308416 | tf_op jit(solution)/shard_map/all_gather | solution.py:610
  346.6 2.9 collective-permute-start.6
  349.6 1.0 copy-start.5
Sparse Core Ops, SparseCore 0:
  26.9 29.6 all-gather.18
  58.2 26.6 all-gather.16
  86.5 62.1 all-gather.22
  167.3 47.4 all-gather.20
  228.8 46.6 all-gather.24
  345.9 41.9 all-gather.28
  389.5 27.6 all-gather.26
  418.7 30.0 all-gather.30
